TPU v7x, 128 devices: a whole 4x4x4 slice. The times are simulated.
128 devices in a mesh: book: 8 (over y, core), path: 16 (over z, x).
Axes of the slice: x: 4, y: 4, z: 4, core: 2. Of those that a mesh axis runs over, the one named last changes fastest.
Arguments:
- states: float32 [10, 20, 262144], P(None, None, ('book', 'path')), parts along dimension 2, may hold values from -7.5 to 7.5
- itm_flags: int32 [10, 262144], P(None, ('book', 'path')), parts along dimension 1, may hold values 0 or 1
- terminal: float32 [262144], P(('book', 'path')), parts along dimension 0, may hold values from -3.5 to 5.5
- strike: float32 [8], P('book'), parts along dimension 0, may hold values from 0.025 to 0.035
- date_index: int32 [262144], P(('book', 'path')), parts along dimension 0, may hold values from 0 to 9
Outputs:
- cash_flow: float32 [262144], P(('book', 'path')), parts along dimension 0
- book_price: float32 [8], P('book'), parts along dimension 0
- coefficients: float32 [80, 231], P('book'), parts along dimension 0
There are 8 independent parts, one for each index of `book`. A program takes and returns all parts, laid end to end along the dimension named above; each array names one. Nothing has to cross between parts.
All inputs are finite; a program needn't handle non-finite values. No bound on the sum of `itm_flags` on one device may be relied on, other than what follows from the above.
Results may differ from a plain program's by a relative error of at most 0.0003.
Values sent between devices are 32-bit elements; how exact they have to be, the bound alone decides.
No kernel may reach another device: no remote copies, remote signals or barrier semaphores. Data moves between devices by JAX's collectives and lax.ppermute only.
A program may use at most 192 MiB of HBM per device.

v0:
```python
import jax
import jax.numpy as jnp
import numpy as np
from jax import lax
from jax.sharding import Mesh
from jax.sharding import PartitionSpec as P

PATH = ("path_0", "path_1")
BOOK_PATH = ("book", "path_0", "path_1")


ridge_weight = 0.05
temper_scale = 0.5
highest = lax.Precision.HIGHEST


def one_axis_at_a_time(shard, axes):
    for axis in axes:
        shard = lax.psum(shard, axis)
    return shard


def sent_to_all(shard, axis):
    length = lax.axis_size(axis)
    return lax.all_to_all(
        jnp.broadcast_to(shard[None], (length, *shard.shape)), axis, 0, 0, tiled=True
    )


def over_copies(shard, axis):
    return sent_to_all(shard, axis).sum(axis=0)


def swap_terms(factors, strike_level):
    forwards = 0.03 * jnp.exp(0.25 * factors)
    discount = jnp.cumprod(1.0 / (1.0 + 0.25 * forwards), axis=0)
    annuity = 0.25 * jnp.sum(discount, axis=0)
    swap_rate = (1.0 - discount[-1]) / annuity
    return (100.0 * annuity * (swap_rate - strike_level), discount[0])


def basis_of(scaled, pair_left, pair_right):
    ones_row = jnp.ones((1, scaled.shape[1]), jnp.float32)
    return jnp.concatenate([ones_row, scaled, scaled[pair_left] * scaled[pair_right]], axis=0)


def gram_only(basis_rows, money_flags):
    weighted = basis_rows * money_flags
    return lax.dot_general(
        weighted,
        basis_rows,
        (((1,), (1,)), ((), ())),
        precision=highest,
        preferred_element_type=jnp.float32,
    )


def system_of(gram_sums, path_count):
    return gram_sums / path_count + ridge_weight * jnp.eye(gram_sums.shape[0], dtype=jnp.float32)


def shards(states, itm_flags, terminal, strike, date_index):
    date_count, factor_count, local_paths = states.shape
    pair_left, pair_right = np.triu_indices(factor_count)
    total_paths = local_paths * lax.axis_size(PATH)
    value_now = terminal
    coef_list = []
    money_all = itm_flags.astype(jnp.float32)
    count_all, first_all, second_all = (
        one_axis_at_a_time(jnp.sum(money_all, axis=1), PATH),
        one_axis_at_a_time(jnp.sum(money_all[:, None, :] * states, axis=2), PATH),
        one_axis_at_a_time(jnp.sum(money_all[:, None, :] * states * states, axis=2), PATH),
    )
    mean_all = first_all / count_all[:, None]
    scale_all = jnp.sqrt(second_all / count_all[:, None] - mean_all * mean_all + 1e-05)
    local_list = []
    for date_step in range(date_count):
        scaled = (states[date_step] - mean_all[date_step][:, None]) / scale_all[date_step][:, None]
        local_list.append(gram_only(basis_of(scaled, pair_left, pair_right), money_all[date_step]))
    gram_stack = lax.psum(jnp.stack(local_list, axis=0), PATH)
    chol_list = [
        jnp.linalg.cholesky(system_of(gram_stack[date_step], count_all[date_step]))
        for date_step in range(date_count)
    ]
    for date_step in range(date_count - 1, -1, -1):
        factors = states[date_step]
        exercise, discount = swap_terms(factors, strike[0])
        value_now = value_now * discount
        money_flags = money_all[date_step]
        scaled = (factors - mean_all[date_step][:, None]) / scale_all[date_step][:, None]
        basis_rows = basis_of(scaled, pair_left, pair_right)
        rhs_local = jnp.dot(
            basis_rows * money_flags,
            value_now,
            precision=highest,
            preferred_element_type=jnp.float32,
        )
        rhs_total = over_copies(rhs_local, PATH)
        coef_vector = jax.scipy.linalg.cho_solve(
            (chol_list[date_step], True), rhs_total / count_all[date_step]
        )
        continuation = jnp.dot(
            coef_vector, basis_rows, precision=highest, preferred_element_type=jnp.float32
        )
        open_date = (date_index <= date_step).astype(jnp.float32)
        weights = jax.nn.sigmoid((exercise - continuation) / temper_scale) * money_flags * open_date
        value_now = value_now + weights * (exercise - value_now)
        coef_list.append(coef_vector)
    book_sum = one_axis_at_a_time(jnp.sum(value_now), PATH)
    book_price = jnp.reshape(book_sum / total_paths, (1,))
    return (value_now, book_price, jnp.stack(coef_list[::-1], axis=0))


def solution(mesh):
    split = Mesh(mesh.devices.reshape(mesh.shape["book"], 4, 4), ("book", "path_0", "path_1"))
    return jax.shard_map(
        shards,
        mesh=split,
        in_specs=(
            P(None, None, BOOK_PATH),
            P(None, BOOK_PATH),
            P(BOOK_PATH),
            P("book"),
            P(BOOK_PATH),
        ),
        out_specs=(P(BOOK_PATH), P("book"), P("book", None)),
        check_vma=False,
    )
```

profile of v0, /device:TPU:0, one launch (start us, length us, event | category | flops | bytes accessed | tf_op | source)
XLA Modules:
  0.0 1114.3 jit_solution(1723377565558352581)
XLA Ops:
  11.3 18.4 %all-reduce.4 = (f32[10,20]{1,0:T(8,128)S(1)}, f32[10]{0:T(128)S(1)}, f32[10,20]{1,0:T(8,128)S(1)}) all-reduce(f32[10,20]{1,0:T(8,128)S(1)} %get-tuple-element.80, f32[10]{0:T(128)S(1)} %convert_reduce_fusion, f32[10,20]{1,0:T(8,128)S(1)} %get-tuple-element.79), channel_id=1, replica_groups=mesh['book'=8,'path_0'=4,'path_1'=4] {'path_0'}, use_global_device_ids=true, to_apply=%region_9.0 | all-reduce | flops 410 | bytes 3280 | tf_op jit(solution)/shard_map/psum | solution.py:19
  29.7 17.0 %all-reduce.3 = (f32[10,20]{1,0:T(8,128)S(1)}, f32[10]{0:T(128)S(1)}, f32[10,20]{1,0:T(8,128)S(1)}) all-reduce(f32[10,20]{1,0:T(8,128)S(1)} %get-tuple-element.84, f32[10]{0:T(128)S(1)} %get-tuple-element.85, f32[10,20]{1,0:T(8,128)S(1)} %get-tuple-element.86), channel_id=1, replica_groups=mesh['book'=8,'path_0'=4,'path_1'=4] {'path_1'}, use_global_device_ids=true, to_apply=%region_10.11 | all-reduce | flops 410 | bytes 3280 | tf_op jit(solution)/shard_map/psum | solution.py:19
  184.8 69.2 %all-reduce.7.cloned.1.call-done = f32[10,231,231]{1,2,0:T(8,128)} async-done(((f32[10,231,231]{1,2,0:T(8,128)}), f32[10,231,231]{1,2,0:T(8,128)}) %all-reduce.7.cloned.1.call-update) | async-done | bytes 2134456 | tf_op jit(solution)/shard_map/psum | solution.py:80
  257.5 11.7 %cholesky.504 = f32[128,128]{1,0:T(8,128)S(1)} custom-call(f32[128,128]{1,0:T(8,128)S(1)} %cholesky.880), custom_call_target="Cholesky" | custom-call | tf_op jit(solution)/shard_map/jit(cholesky)/cholesky | solution.py:82
  269.9 9.8 custom-call.31
  304.6 12.1 %cholesky.846 = f32[128,128]{1,0:T(8,128)S(1)} custom-call(f32[128,128]{1,0:T(8,128)S(1)} %cholesky.907), custom_call_target="Cholesky" | custom-call | tf_op jit(solution)/shard_map/jit(cholesky)/cholesky | solution.py:82
  318.1 9.8 custom-call.49
  348.6 12.7 %cholesky.808 = f32[128,128]{1,0:T(8,128)S(1)} custom-call(f32[128,128]{1,0:T(8,128)} %cholesky.904), custom_call_target="Cholesky" | custom-call | tf_op jit(solution)/shard_map/jit(cholesky)/cholesky | solution.py:82
  363.2 10.6 custom-call.47
  377.2 10.2 cholesky.828
  396.5 12.5 %cholesky.770 = f32[128,128]{1,0:T(8,128)S(1)} custom-call(f32[128,128]{1,0:T(8,128)} %cholesky.901), custom_call_target="Cholesky" | custom-call | tf_op jit(solution)/shard_map/jit(cholesky)/cholesky | solution.py:82
  411.1 10.6 custom-call.45
  425.3 10.2 cholesky.790
  442.9 11.7 %cholesky.732 = f32[128,128]{1,0:T(8,128)S(1)} custom-call(f32[128,128]{1,0:T(8,128)S(1)} %cholesky.898), custom_call_target="Cholesky" | custom-call | tf_op jit(solution)/shard_map/jit(cholesky)/cholesky | solution.py:82
  484.1 11.7 %cholesky.694 = f32[128,128]{1,0:T(8,128)S(1)} custom-call(f32[128,128]{1,0:T(8,128)S(1)} %cholesky.895), custom_call_target="Cholesky" | custom-call | tf_op jit(solution)/shard_map/jit(cholesky)/cholesky | solution.py:82
  523.6 11.9 %cholesky.656 = f32[128,128]{1,0:T(8,128)S(1)} custom-call(f32[128,128]{1,0:T(8,128)S(1)} %cholesky.892), custom_call_target="Cholesky" | custom-call | tf_op jit(solution)/shard_map/jit(cholesky)/cholesky | solution.py:82
  536.9 9.8 custom-call.39
  561.8 11.7 %cholesky.618 = f32[128,128]{1,0:T(8,128)S(1)} custom-call(f32[128,128]{1,0:T(8,128)S(1)} %cholesky.889), custom_call_target="Cholesky" | custom-call | tf_op jit(solution)/shard_map/jit(cholesky)/cholesky | solution.py:82
  574.8 10.2 custom-call.37
  600.0 11.7 %cholesky.580 = f32[128,128]{1,0:T(8,128)S(1)} custom-call(f32[128,128]{1,0:T(8,128)S(1)} %cholesky.886), custom_call_target="Cholesky" | custom-call | tf_op jit(solution)/shard_map/jit(cholesky)/cholesky | solution.py:82
  613.1 9.8 custom-call.35
  638.1 11.7 %cholesky.542 = f32[128,128]{1,0:T(8,128)S(1)} custom-call(f32[128,128]{1,0:T(8,128)S(1)} %cholesky.883), custom_call_target="Cholesky" | custom-call | tf_op jit(solution)/shard_map/jit(cholesky)/cholesky | solution.py:82
  676.6 19.7 %custom-call.32 = f32[2,128,128]{1,2,0:T(8,128)S(1)} custom-call(f32[2,128,128]{2,1,0:T(8,128)S(1)} %pad_maximum_fusion.10), custom_call_target="InvertDiagBlocksLowerTriangular" | custom-call | tf_op jit(solution)/shard_map/jit(_cho_solve)/triangular_solve | solution.py:99
  719.7 21.1 %custom-call.50 = f32[2,128,128]{1,2,0:T(8,128)} custom-call(f32[2,128,128]{2,1,0:T(8,128)} %pad_maximum_fusion.19), custom_call_target="InvertDiagBlocksLowerTriangular" | custom-call | tf_op jit(solution)/shard_map/jit(_cho_solve)/triangular_solve | solution.py:99
  740.8 21.1 %custom-call.36 = f32[2,128,128]{1,2,0:T(8,128)} custom-call(f32[2,128,128]{2,1,0:T(8,128)} %pad_maximum_fusion.12), custom_call_target="InvertDiagBlocksLowerTriangular" | custom-call | tf_op jit(solution)/shard_map/jit(_cho_solve)/triangular_solve | solution.py:99
  761.9 21.1 %custom-call.38 = f32[2,128,128]{1,2,0:T(8,128)} custom-call(f32[2,128,128]{2,1,0:T(8,128)} %pad_maximum_fusion.13), custom_call_target="InvertDiagBlocksLowerTriangular" | custom-call | tf_op jit(solution)/shard_map/jit(_cho_solve)/triangular_solve | solution.py:99
  783.0 21.1 %custom-call.40 = f32[2,128,128]{1,2,0:T(8,128)} custom-call(f32[2,128,128]{2,1,0:T(8,128)} %pad_maximum_fusion.14), custom_call_target="InvertDiagBlocksLowerTriangular" | custom-call | tf_op jit(solution)/shard_map/jit(_cho_solve)/triangular_solve | solution.py:99
  804.1 21.1 %custom-call.42 = f32[2,128,128]{1,2,0:T(8,128)} custom-call(f32[2,128,128]{2,1,0:T(8,128)} %pad_maximum_fusion.15), custom_call_target="InvertDiagBlocksLowerTriangular" | custom-call | tf_op jit(solution)/shard_map/jit(_cho_solve)/triangular_solve | solution.py:99
  825.2 21.3 %custom-call.44 = f32[2,128,128]{1,2,0:T(8,128)} custom-call(f32[2,128,128]{2,1,0:T(8,128)} %pad_maximum_fusion.16), custom_call_target="InvertDiagBlocksLowerTriangular" | custom-call | tf_op jit(solution)/shard_map/jit(_cho_solve)/triangular_solve | solution.py:99
  846.5 21.1 %custom-call.46 = f32[2,128,128]{1,2,0:T(8,128)} custom-call(f32[2,128,128]{2,1,0:T(8,128)} %pad_maximum_fusion.17), custom_call_target="InvertDiagBlocksLowerTriangular" | custom-call | tf_op jit(solution)/shard_map/jit(_cho_solve)/triangular_solve | solution.py:99
  867.6 21.1 %custom-call.48 = f32[2,128,128]{1,2,0:T(8,128)} custom-call(f32[2,128,128]{2,1,0:T(8,128)} %pad_maximum_fusion.18), custom_call_target="InvertDiagBlocksLowerTriangular" | custom-call | tf_op jit(solution)/shard_map/jit(_cho_solve)/triangular_solve | solution.py:99
  888.7 21.1 %custom-call.34 = f32[2,128,128]{1,2,0:T(8,128)} custom-call(f32[2,128,128]{2,1,0:T(8,128)} %pad_maximum_fusion.11), custom_call_target="InvertDiagBlocksLowerTriangular" | custom-call | tf_op jit(solution)/shard_map/jit(_cho_solve)/triangular_solve | solution.py:99
  (684 shorter events, 557.4 us)
Async XLA Ops:
  7.2 39.6 %copy-start.142 = (s32[210]{0:T(256)S(1)}, s32[210]{0:T(256)}, u32[]{:S(2)}) copy-start(s32[210]{0:T(256)} %constant.243) | copy-start | bytes 2524
  7.2 39.6 %copy-start.143 = (s32[210]{0:T(256)S(1)}, s32[210]{0:T(256)}, u32[]{:S(2)}) copy-start(s32[210]{0:T(256)} %constant.242) | copy-start | bytes 2524
  9.2 117.4 %copy-start.71 = (f32[1,2048]{1,0:T(1,128)}, f32[1,2048]{1,0:T(1,128)S(1)}, u32[]{:S(2)}) copy-start(f32[1,2048]{1,0:T(1,128)S(1)} %get-tuple-element.145) | copy-start | bytes 24580
  9.2 126.6 %copy-start.75 = (f32[1,2048]{1,0:T(1,128)}, f32[1,2048]{1,0:T(1,128)S(1)}, u32[]{:S(2)}) copy-start(f32[1,2048]{1,0:T(1,128)S(1)} %get-tuple-element.144) | copy-start | bytes 24580
  9.2 129.3 %copy-start.77 = (f32[1,2048]{1,0:T(1,128)}, f32[1,2048]{1,0:T(1,128)S(1)}, u32[]{:S(2)}) copy-start(f32[1,2048]{1,0:T(1,128)S(1)} %get-tuple-element.143) | copy-start | bytes 24580
  9.2 132.0 %copy-start.79 = (f32[1,2048]{1,0:T(1,128)}, f32[1,2048]{1,0:T(1,128)S(1)}, u32[]{:S(2)}) copy-start(f32[1,2048]{1,0:T(1,128)S(1)} %get-tuple-element.142) | copy-start | bytes 24580
  9.3 134.7 %copy-start.81 = (f32[1,2048]{1,0:T(1,128)}, f32[1,2048]{1,0:T(1,128)S(1)}, u32[]{:S(2)}) copy-start(f32[1,2048]{1,0:T(1,128)S(1)} %get-tuple-element.141) | copy-start | bytes 24580
  9.3 137.6 %copy-start.83 = (f32[1,2048]{1,0:T(1,128)}, f32[1,2048]{1,0:T(1,128)S(1)}, u32[]{:S(2)}) copy-start(f32[1,2048]{1,0:T(1,128)S(1)} %get-tuple-element.140) | copy-start | bytes 24580
  9.3 140.3 %copy-start.85 = (f32[1,2048]{1,0:T(1,128)}, f32[1,2048]{1,0:T(1,128)S(1)}, u32[]{:S(2)}) copy-start(f32[1,2048]{1,0:T(1,128)S(1)} %get-tuple-element.139) | copy-start | bytes 24580
  9.3 143.0 %copy-start.88 = (f32[1,2048]{1,0:T(1,128)}, f32[1,2048]{1,0:T(1,128)S(1)}, u32[]{:S(2)}) copy-start(f32[1,2048]{1,0:T(1,128)S(1)} %get-tuple-element.138) | copy-start | bytes 24580
  9.3 145.7 %copy-start.90 = (f32[1,2048]{1,0:T(1,128)}, f32[1,2048]{1,0:T(1,128)S(1)}, u32[]{:S(2)}) copy-start(f32[1,2048]{1,0:T(1,128)S(1)} %get-tuple-element.137) | copy-start | bytes 24580
  9.3 148.4 %copy-start.96 = (f32[1,2048]{1,0:T(1,128)}, f32[1,2048]{1,0:T(1,128)S(1)}, u32[]{:S(2)}) copy-start(f32[1,2048]{1,0:T(1,128)S(1)} %get-tuple-element.146) | copy-start | bytes 24580
  60.6 97.1 %copy-start.127 = (f32[1,2048]{1,0:T(1,128)}, f32[1,2048]{1,0:T(1,128)S(1)}, u32[]{:S(2)}) copy-start(f32[1,2048]{1,0:T(1,128)S(1)} %broadcast.242) | copy-start | bytes 24580
  62.9 121.1 %all-to-all-start = ((f32[16,1,231]{2,1,0:T(1,128)}), f32[16,1,231]{2,1,0:T(1,128)S(1)}, u32[]{:S(2)}, u32[]{:S(2)}) async-start(f32[16,1,231]{2,1,0:T(1,128)} %broadcast_in_dim.208), calls=%async_computation | async-start | bytes 32768 | tf_op jit(solution)/shard_map/all_to_all | solution.py:25
  66.7 187.3 %all-reduce.7.cloned.1.call-start = ((), (), s32[]{:S(2)}) async-start(), calls=%async_computation.10 | async-start | bytes 4751360 | tf_op jit(solution)/shard_map/psum | solution.py:80
  634.2 42.3 %copy-start.52 = (f32[128,25]{1,0:T(8,128)S(1)}, f32[128,25]{1,0:T(8,128)}, u32[]{:S(2)}) copy-start(f32[128,25]{1,0:T(8,128)} %pad_convert_fusion) | copy-start | bytes 38404
  634.2 42.3 %copy-start.61 = (f32[103,103]{1,0:T(8,128)S(1)}, f32[103,103]{1,0:T(8,128)}, u32[]{:S(2)}) copy-start(f32[103,103]{1,0:T(8,128)} %triangular_solve.700) | copy-start | bytes 127312
  636.2 40.4 %copy-start.60 = (f32[1,128,128]{2,1,0:T(8,128)S(1)}, f32[1,128,128]{2,1,0:T(8,128)}, u32[]{:S(2)}) copy-start(f32[1,128,128]{2,1,0:T(8,128)} %slice_bitcast_fusion.19) | copy-start | bytes 196612
  637.9 61.2 %copy-start.128 = (f32[1,2048]{1,0:T(1,128)S(1)}, f32[1,2048]{1,0:T(1,128)}, u32[]{:S(2)}) copy-start(f32[1,2048]{1,0:T(1,128)} %copy-done.127) | copy-start | bytes 24580
  704.3 205.5 %all-to-all-start.1 = ((f32[16,1,231]{2,1,0:T(1,128)}), f32[16,1,231]{2,1,0:T(1,128)}, u32[]{:S(2)}, u32[]{:S(2)}) async-start(f32[16,1,231]{2,1,0:T(1,128)} %broadcast_in_dim.211), calls=%async_computation.1 | async-start | bytes 32768 | tf_op jit(solution)/shard_map/all_to_all | solution.py:25
  713.0 208.9 %copy-start.31 = (f32[210,2048]{1,0:T(8,128)S(1)}, f32[210,2048]{1,0:T(8,128)}, u32[]{:S(2)}) copy-start(f32[210,2048]{1,0:T(8,128)} %copy-done.30) | copy-start | bytes 5160964
  713.0 208.9 %copy-start.89 = (f32[1,2048]{1,0:T(1,128)S(1)}, f32[1,2048]{1,0:T(1,128)}, u32[]{:S(2)}) copy-start(f32[1,2048]{1,0:T(1,128)} %copy-done.88) | copy-start | bytes 24580
  924.3 14.9 %all-to-all-start.2 = ((f32[16,1,231]{2,1,0:T(1,128)}), f32[16,1,231]{2,1,0:T(1,128)S(1)}, u32[]{:S(2)}, u32[]{:S(2)}) async-start(f32[16,1,231]{2,1,0:T(1,128)} %broadcast_in_dim.214), calls=%async_computation.2 | async-start | bytes 32768 | tf_op jit(solution)/shard_map/all_to_all | solution.py:25
  951.0 11.0 all-to-all-start.3
  970.4 11.0 all-to-all-start.4
  990.0 11.4 %all-to-all-start.5 = ((f32[16,1,231]{2,1,0:T(1,128)}), f32[16,1,231]{2,1,0:T(1,128)S(1)}, u32[]{:S(2)}, u32[]{:S(2)}) async-start(f32[16,1,231]{2,1,0:T(1,128)} %broadcast_in_dim.223), calls=%async_computation.5 | async-start | bytes 32768 | tf_op jit(solution)/shard_map/all_to_all | solution.py:25
  1009.8 11.0 all-to-all-start.6
  1029.3 11.0 all-to-all-start.7
  1048.7 11.2 %all-to-all-start.8 = ((f32[16,1,231]{2,1,0:T(1,128)}), f32[16,1,231]{2,1,0:T(1,128)S(1)}, u32[]{:S(2)}, u32[]{:S(2)}) async-start(f32[16,1,231]{2,1,0:T(1,128)} %broadcast_in_dim.232), calls=%async_computation.8 | async-start | bytes 32768 | tf_op jit(solution)/shard_map/all_to_all | solution.py:25
  1067.7 37.1 %copy-start.136 = (f32[1,231]{1,0:T(1,128)S(1)}, f32[1,231]{1,0:T(1,128)}, u32[]{:S(2)}) copy-start(f32[1,231]{1,0:T(1,128)} %fusion.420) | copy-start | bytes 2776
  1067.8 37.1 %copy-start.137 = (f32[1,231]{1,0:T(1,128)S(1)}, f32[1,231]{1,0:T(1,128)}, u32[]{:S(2)}) copy-start(f32[1,231]{1,0:T(1,128)} %fusion.419) | copy-start | bytes 2776
  1068.4 11.0 all-to-all-start.9
  (123 other events, 1440.3 us)
Sparse Core Ops, SparseCore 0:
  160.6 93.2 all-reduce.6
where the time goes:
time: 1120 us; the launch traced here: 1110 us
  other arithmetic  630 us (56%)
  waiting for transfers between devices  127 us (11%)
  matrix products  123 us (11%)
  local copies, waits for them, and re-layouts  106 us (9%)
  blocking collectives  54.3 us (5%)
  starting transfers between devices  41.8 us (4%)
  between operations  31.9 us (3%)
    another operation x70, other arithmetic, shards(): jnp.linalg.cholesky(system_of(gram_stack[date_step], count_all[date_step]))  336 us
    another operation x34, other arithmetic, shards(): jax.scipy.linalg.cho_solve((chol_list[date_step], True), rhs_total / coun...  229 us
    psum x1, waiting for transfers between devices, shards(): gram_stack = lax.psum(jnp.stack(local_list, axis=0), PATH)  69.2 us
    all_to_all x10, waiting for transfers between devices, sent_to_all(): lax.all_to_all(jnp.broadcast_to(shard[None], (length, *shard.shape)), axi...  58 us
    psum x4, blocking collectives, one_axis_at_a_time(): shard = lax.psum(shard, axis)  54.3 us
    all_to_all x10, starting transfers between devices, sent_to_all(): lax.all_to_all(jnp.broadcast_to(shard[None], (length, *shard.shape)), axi...  41.5 us
    another operation x60, matrix products, shards(): jax.scipy.linalg.cho_solve((chol_list[date_step], True), rhs_total / coun...  33.7 us
    dot_general x10, matrix products, gram_only(): lax.dot_general(weighted, basis_rows, (((1,), (1,)), ((), ())), precision...  27.3 us
  transfers between devices with their start and end apart: 11, of which 9 were waited for; matrix products, arithmetic and copies ran while one was open for 27% of the time, Pallas kernels for 0%

commit v1 on v0

v1 whole, which is shorter than its diff:
```python
import jax
import jax.numpy as jnp
from jax import lax
from jax.experimental import pallas as pl
from jax.experimental.pallas import tpu as pltpu
from jax.sharding import Mesh
from jax.sharding import PartitionSpec as P

PATH = ("path_0", "path_1")
BOOK_PATH = ("book", "path_0", "path_1")
ridge_weight = 0.05
temper_scale = 0.5
highest = lax.Precision.HIGHEST
f32 = jnp.float32
bf16 = jnp.bfloat16
NT = (((1,), (1,)), ((), ()))
TN = (((0,), (0,)), ((), ()))
ROWS = 240
HALF = 128
BLOCK = 16
CHUNK = 1024


def spec(shape, index=None):
    if index is None:
        index = (0,) * len(shape)
    return pl.BlockSpec(shape, lambda *_: index)


def lanes_of(shape):
    return lax.broadcasted_iota(jnp.int32, shape, 1)


def rows_of(shape):
    return lax.broadcasted_iota(jnp.int32, shape, 0)


def stats_kernel(z_ref, m_ref, out_ref):
    dates, factors, _ = z_ref.shape
    lane = lanes_of((factors, 128))
    packed = jnp.zeros((factors, 128), f32)
    for d in range(dates):
        z = z_ref[d]
        m = m_ref[d : d + 1, :].astype(f32)
        mz = z * m
        packed = jnp.where(lane == 3 * d, jnp.sum(mz, axis=1, keepdims=True), packed)
        packed = jnp.where(lane == 3 * d + 1, jnp.sum(mz * z, axis=1, keepdims=True), packed)
        packed = jnp.where(lane == 3 * d + 2, jnp.sum(m, axis=1, keepdims=True), packed)
    for i in range(out_ref.shape[0]):
        out_ref[i] = packed


def swap_kernel(strike_ref, z_ref, ex_ref, disc_ref, fac_ref):
    dates, factors, _ = z_ref.shape
    for d in range(dates):
        fac_ref[...] = 1.0 / (1.0 + 0.25 * (0.03 * jnp.exp(0.25 * z_ref[d])))
        first = fac_ref[0:1, :]
        disc = first
        total = first
        for j in range(1, factors):
            disc = disc * fac_ref[j : j + 1, :]
            total = total + disc
        disc_ref[d : d + 1, :] = first
        ex_ref[d : d + 1, :] = 100.0 * ((1.0 - disc) - strike_ref[0] * (0.25 * total))


def rhs_row(phi_ref, weights):
    acc = jnp.zeros((ROWS, 128), f32)
    for c in range(0, weights.shape[1], 128):
        acc = acc + phi_ref[:, c : c + 128] * weights[:, c : c + 128]
    row = lax.dot_general(
        jnp.ones((8, 128), f32), acc, NT, precision=highest, preferred_element_type=f32
    )
    return jnp.concatenate([row, jnp.zeros((8, 256 - ROWS), f32)], axis=1)


def gram_kernel(stats_ref, z_ref, m_ref, disc_ref, term_ref, phi_ref, slot_ref, v_ref, x_ref, gram_ref, rhs_ref):
    step = pl.program_id(0)
    dates = m_ref.shape[0]
    factors = z_ref.shape[0]
    paths = z_ref.shape[1]

    @pl.when(step < dates)
    def _():
        d = dates - 1 - step
        stats = stats_ref[0]
        for i in range(1, stats_ref.shape[0]):
            stats = stats + stats_ref[i]
        lane = lanes_of((factors, 128))

        def column(i):
            return jnp.sum(jnp.where(lane == i, stats, 0.0), axis=1, keepdims=True)

        count = column(3 * d + 2)
        mean = column(3 * d) / count
        inverse = 1.0 / jnp.sqrt(column(3 * d + 1) / count - mean * mean + 1e-05)
        gram_ref[...] = jnp.zeros_like(gram_ref)

        def chunk(c, carry):
            at = pl.ds(pl.multiple_of(c * CHUNK, CHUNK), CHUNK)
            x_ref[...] = (z_ref[:, at] - mean) * inverse
            phi_ref[0:1, at] = jnp.ones((1, CHUNK), f32)
            phi_ref[1 : 1 + factors, at] = x_ref[...]
            offset = 1 + factors
            for j in range(factors):
                phi_ref[offset : offset + factors - j, at] = x_ref[j : j + 1, :] * x_ref[j:factors, :]
                offset += factors - j
            phi_ref[offset:ROWS, at] = jnp.zeros((ROWS - offset, CHUNK), f32)
            phi = phi_ref[:, at]
            m = m_ref[pl.ds(d, 1), at].astype(f32)
            pad = jnp.zeros((256 - ROWS, CHUNK), bf16)
            hi = phi.astype(bf16)
            rest = phi - hi.astype(f32)
            lo = rest.astype(bf16)
            him = jnp.concatenate([(phi * m).astype(bf16), pad], axis=0)
            lom = jnp.concatenate([(rest * m).astype(bf16), pad], axis=0)
            hi = jnp.concatenate([hi, pad], axis=0)
            lo = jnp.concatenate([lo, pad], axis=0)
            gram_ref[...] += (
                lax.dot_general(him, hi, NT, preferred_element_type=f32)
                + lax.dot_general(him, lo, NT, preferred_element_type=f32)
                + lax.dot_general(lom, hi, NT, preferred_element_type=f32)
            )
            return carry

        lax.fori_loop(0, paths // CHUNK, chunk, 0)

        @pl.when(step == 0)
        def _():
            value = term_ref[...] * disc_ref[dates - 1 : dates, :]
            v_ref[...] = value
            rhs_ref[...] = rhs_row(phi_ref, value * m_ref[dates - 1 : dates, :].astype(f32))

        gram = gram_ref[...]
        slot_ref[0:HALF, :] = folded(gram[0:HALF, 0:HALF], gram[0:HALF, HALF:], gram[HALF:, HALF:])
        slot_ref[HALF:, :] = rhs_ref[...]

    @pl.when(step >= dates)
    def _():
        slot_ref[0:HALF, :] = jnp.zeros((HALF, 256), f32)
        slot_ref[HALF:, :] = rhs_ref[...]


def folded(first, beside, last):
    row, lane = rows_of((HALF, HALF)), lanes_of((HALF, HALF))
    diagonal = jnp.sum(jnp.where(row == lane, last, 0.0), axis=0, keepdims=True)
    left = jnp.where(row <= lane, first, last)
    left = jnp.where((row == HALF - 1) & (lane < HALF - 1), diagonal, left)
    return jnp.concatenate([left, beside], axis=1)


def unfolded(packed):
    row, lane = rows_of((HALF, HALF)), lanes_of((HALF, HALF))
    left, beside = packed[:, 0:HALF], packed[:, HALF:]
    turned = left.T
    first = jnp.where(row <= lane, left, turned)
    diagonal = left[HALF - 1 : HALF, :]
    last = jnp.where(row > lane, left, turned)
    last = jnp.where(row == lane, diagonal, last)
    last = jnp.where((row < HALF - 1) & (lane < HALF - 1), last, 0.0)
    return first, beside, last


def inverse_kernel(parts_ref, out_ref, a_ref):
    basis = 231
    packed = parts_ref[0, 0:HALF, :]
    for i in range(1, parts_ref.shape[0]):
        packed = packed + parts_ref[i, 0:HALF, :]
    first, beside, last = unfolded(packed)
    a_ref[0:HALF, 0:HALF] = first
    a_ref[0:HALF, HALF:] = beside
    a_ref[HALF:, 0:HALF] = beside.T
    a_ref[HALF:, HALF:] = last
    count = packed[0:1, 0:1]
    row, lane = rows_of((256, 256)), lanes_of((256, 256))
    added = jnp.where(row < basis, ridge_weight * count, 1.0)
    a_ref[...] = a_ref[...] + jnp.where(row == lane, added, 0.0)
    lane_a = lanes_of((BLOCK, 128))
    lane_b = lane_a + 128
    row_a = rows_of((BLOCK, 128))
    lane_r = lanes_of((BLOCK, 256))

    def split(x):
        one = x.astype(bf16)
        rest = x - one.astype(f32)
        two = rest.astype(bf16)
        return one, two, (rest - two.astype(f32)).astype(bf16)

    def sweep(i, carry):
        start = pl.multiple_of(i * BLOCK, BLOCK)
        panel = a_ref[pl.ds(start, BLOCK), :]
        ra, rb = panel[:, 0:128], panel[:, 128:]
        cols = []
        for c in range(BLOCK):
            both = jnp.where(lane_a == start + c, ra, 0.0) + jnp.where(lane_b == start + c, rb, 0.0)
            cols.append(jnp.broadcast_to(jnp.sum(both, axis=1, keepdims=True), (BLOCK, 128)))
        for k in range(BLOCK):
            pivot = 1.0 / cols[k][k : k + 1, :]
            here = row_a == k
            unit = jnp.where(here, 1.0, 0.0)
            ra = jnp.where(lane_a == start + k, unit, ra)
            rb = jnp.where(lane_b == start + k, unit, rb)
            row_k = ra[k : k + 1, :] * pivot
            ra = jnp.where(here, row_k, ra - cols[k] * row_k)
            row_k = rb[k : k + 1, :] * pivot
            rb = jnp.where(here, row_k, rb - cols[k] * row_k)
            for c in range(k + 1, BLOCK):
                f = cols[c][k : k + 1, :] * pivot
                cols[c] = jnp.where(here, f, cols[c] - cols[k] * f)
        inside = (lane_r >= start) & (lane_r < start + BLOCK)
        w = jnp.concatenate([ra, rb], axis=1)
        w = jnp.where(inside, -w, w)
        r1, r2, r3 = split(panel)
        w1, w2, w3 = split(w)
        left = jnp.concatenate([r1, r1, r2, r2, r1, r3], axis=0)
        right = jnp.concatenate([w1, w2, w1, w2, w3, w1], axis=0)
        change = lax.dot_general(left, right, TN, preferred_element_type=f32)
        within = (lane >= start) & (lane < start + BLOCK)
        a_ref[...] = jnp.where(within, 0.0, a_ref[...]) - change
        a_ref[pl.ds(start, BLOCK), :] = w
        return carry

    lax.fori_loop(0, ROWS // BLOCK, sweep, 0)
    result = -a_ref[...]
    packed = folded(result[0:HALF, 0:HALF], result[0:HALF, HALF:], result[HALF:, HALF:])
    for i in range(out_ref.shape[0]):
        out_ref[i] = packed


def unfold_kernel(packed_ref, out_ref):
    first, beside, last = unfolded(packed_ref[...])
    out_ref[0:HALF, 0:HALF] = first
    out_ref[0:HALF, HALF:] = beside
    out_ref[HALF:, 0:HALF] = beside.T[0 : ROWS - HALF, :]
    out_ref[HALF:, HALF:] = last[0 : ROWS - HALF, :]


def chain_kernel(date, *refs):
    parts_ref, inv_ref, phi_ref, ex_ref, m_ref, index_ref, v_ref, disc_ref = refs[:8]
    rhs = parts_ref[0, 0:1, :]
    for i in range(1, parts_ref.shape[0]):
        rhs = rhs + parts_ref[i, 0:1, :]
    product = inv_ref[...] * rhs
    coef = jnp.sum(product[:, 0:128] + product[:, 128:], axis=1, keepdims=True)
    coef = jnp.broadcast_to(coef, (ROWS, 128))
    continuation = []
    for c in range(0, v_ref.shape[1], 128):
        continuation.append(jnp.sum(coef * phi_ref[:, c : c + 128], axis=0, keepdims=True))
    continuation = jnp.concatenate(continuation, axis=1)
    exercise = ex_ref[date : date + 1, :]
    opened = jnp.where(index_ref[...] <= date, m_ref[date : date + 1, :].astype(f32), 0.0)
    weights = jax.nn.sigmoid((exercise - continuation) / temper_scale) * opened
    value = v_ref[...]
    value = value + weights * (exercise - value)
    if date:
        next_ref, out_ref, coef_ref, send_ref = refs[8:]
        value = value * disc_ref[date - 1 : date, :]
        row = rhs_row(next_ref, value * m_ref[date - 1 : date, :].astype(f32))
        for i in range(send_ref.shape[0]):
            send_ref[i] = row[0:1, :]
    else:
        out_ref, coef_ref, send_ref = refs[8:]
        total = jnp.broadcast_to(jnp.sum(value, axis=1, keepdims=True), (1, 128))
        for i in range(send_ref.shape[0]):
            send_ref[i] = total
    out_ref[...] = value
    coef_ref[...] = coef


def exchange(slots):
    return lax.all_to_all(slots, PATH, 0, 0, tiled=True)


def shards(states, itm_flags, terminal, strike, date_index):
    dates, factors, paths = states.shape
    size = lax.axis_size(PATH)
    sds = jax.ShapeDtypeStruct
    terminal = terminal.reshape(1, paths)
    date_index = date_index.reshape(1, paths)
    stats = pl.pallas_call(
        stats_kernel, out_shape=sds((size, factors, 128), f32), name="stats"
    )(states, itm_flags)
    stats = exchange(stats)
    exercise, discount = pl.pallas_call(
        swap_kernel,
        in_specs=[
            pl.BlockSpec(memory_space=pltpu.SMEM),
            pl.BlockSpec(memory_space=pltpu.VMEM),
        ],
        out_shape=[sds((dates, paths), f32), sds((dates, paths), f32)],
        scratch_shapes=[pltpu.VMEM((factors, paths), f32)],
        name="swap",
    )(strike, states)

    def date_of(i):
        return jnp.maximum(dates - 1 - i, 0)

    phi, slots, value = pl.pallas_call(
        gram_kernel,
        grid=(size,),
        in_specs=[
            spec((size, factors, 128)),
            pl.BlockSpec((None, factors, paths), lambda i: (date_of(i), 0, 0)),
            spec((dates, paths)),
            spec((dates, paths)),
            spec((1, paths)),
        ],
        out_specs=[
            pl.BlockSpec((None, ROWS, paths), lambda i: (date_of(i), 0, 0)),
            pl.BlockSpec((None, HALF + 8, 256), lambda i: (jnp.where(i < dates, date_of(i), i), 0, 0)),
            spec((1, paths)),
        ],
        out_shape=[
            sds((dates, ROWS, paths), f32),
            sds((size, HALF + 8, 256), f32),
            sds((1, paths), f32),
        ],
        scratch_shapes=[
            pltpu.VMEM((factors, CHUNK), f32),
            pltpu.VMEM((256, 256), f32),
            pltpu.VMEM((8, 256), f32),
        ],
        name="gram",
    )(stats, states, itm_flags, discount, terminal)
    slots = exchange(slots)
    inverse = pl.pallas_call(
        inverse_kernel,
        in_specs=[spec((size, HALF + 8, 256))],
        out_specs=spec((size, HALF, 256)),
        grid=(1,),
        out_shape=sds((size, HALF, 256), f32),
        scratch_shapes=[pltpu.VMEM((256, 256), f32)],
        name="inverse",
    )(slots)
    inverse = exchange(inverse)

    def unfold(first, number):
        return pl.pallas_call(
            unfold_kernel,
            grid=(number,),
            in_specs=[pl.BlockSpec((None, HALF, 256), lambda i: (first + i, 0, 0))],
            out_specs=pl.BlockSpec((None, ROWS, 256), lambda i: (i, 0, 0)),
            out_shape=sds((number, ROWS, 256), f32),
            name="unfold",
        )(inverse)

    last_inverse = unfold(dates - 1, 1)
    other_inverse = unfold(0, dates - 1)
    received = slots
    coefs = [None] * dates
    for date in range(dates - 1, -1, -1):
        is_last = date == dates - 1
        args = [received, last_inverse if is_last else other_inverse, phi, exercise, itm_flags, date_index, value, discount]
        in_specs = [
            spec((size, 8, 256), (0, HALF // 8, 0)) if is_last else spec((size, 1, 256)),
            spec((None, ROWS, 256), (0 if is_last else date, 0, 0)),
            spec((None, ROWS, paths), (date, 0, 0)),
            spec((dates, paths)),
            spec((dates, paths)),
            spec((1, paths)),
            spec((1, paths)),
            spec((dates, paths)),
        ]
        if date:
            args.append(phi)
            in_specs.append(spec((None, ROWS, paths), (date - 1, 0, 0)))
        width = 256 if date else 128

        def kernel(*refs, date=date):
            chain_kernel(date, *refs)

        value, coefs[date], send = pl.pallas_call(
            kernel,
            grid=(1,),
            in_specs=in_specs,
            out_specs=[spec((1, paths)), spec((ROWS, 128)), spec((size, 1, width))],
            out_shape=[sds((1, paths), f32), sds((ROWS, 128), f32), sds((size, 1, width), f32)],
            name="chain",
        )(*args)
        received = exchange(send)
    book_price = jnp.sum(received[:, 0, 0:1], axis=0) / (paths * size)
    basis = 1 + factors + factors * (factors + 1) // 2
    coefficients = jnp.stack([c[0:basis, 0] for c in coefs], axis=0)
    return (value.reshape(paths), book_price, coefficients)


def solution(mesh):
    split = Mesh(mesh.devices.reshape(mesh.shape["book"], 4, 4), ("book", "path_0", "path_1"))
    return jax.shard_map(
        shards,
        mesh=split,
        in_specs=(
            P(None, None, BOOK_PATH),
            P(None, BOOK_PATH),
            P(BOOK_PATH),
            P("book"),
            P(BOOK_PATH),
        ),
        out_specs=(P(BOOK_PATH), P("book"), P("book", None)),
        check_vma=False,
    )
```

time: 1120 us -> 280 us (0.25)
  other arithmetic: 630 us -> 0.62 us
  matrix products: 123 us -> 0 us
  local copies, waits for them, and re-layouts: 106 us -> 17.4 us
  Pallas kernels: 0 us -> 83.9 us
  waiting for transfers between devices: 127 us -> 62.4 us
  between operations: 31.9 us -> 3.22 us
    another operation x124 -> x0, other arithmetic: 573 us -> none  [the longest x70 336 us: shards(): jnp.linalg.cholesky(system_of(gram_stack[date_step], count_all[date_step]))]
    pallas_call x0 -> x16, Pallas kernels: none -> 83.9 us  [the longest x10 36.5 us: shards(): pl.pallas_call(kernel, grid=(1,), in_specs=in_specs, out_specs=[spec((1,...]
    psum x1 -> x0, waiting for transfers between devices: 69.2 us -> none  [shards(): gram_stack = lax.psum(jnp.stack(local_list, axis=0), PATH)]
    dot_general x30 -> x0, matrix products: 69.1 us -> none  [the longest x10 27.3 us: gram_only(): lax.dot_general(weighted, basis_rows, (((1,), (1,)), ((), ())), precision...]
    all_to_all x0 -> x2, blocking collectives: none -> 64.6 us  [exchange(): return lax.all_to_all(slots, PATH, 0, 0, tiled=True)]
    psum x4 -> x0, blocking collectives: 54.3 us -> none  [one_axis_at_a_time(): shard = lax.psum(shard, axis)]
    another operation x80 -> x0, matrix products: 53.7 us -> none  [the longest x60 33.7 us: shards(): jax.scipy.linalg.cho_solve((chol_list[date_step], True), rhs_total / coun...]
    gather x20 -> x0, local copies, waits for them, and re-layouts: 49.5 us -> none  [the longest x10 25.1 us: basis_of(): scaled[pair_right]]
  transfers between devices with their start and end apart: 11 -> 11, of which waited for: 9 -> 11; matrix products, arithmetic and copies ran while one was open for 27% -> 4% of each run, Pallas kernels for 0% -> 3%
where the time goes in v1:
time: 280 us; the launch traced here: 278 us
  Pallas kernels  83.9 us (30%)
  blocking collectives  64.6 us (23%)
  waiting for transfers between devices  62.4 us (22%)
  starting transfers between devices  46.3 us (17%)
  local copies, waits for them, and re-layouts  17.4 us (6%)
  between operations  3.22 us (1%)
    all_to_all x2, blocking collectives, exchange(): return lax.all_to_all(slots, PATH, 0, 0, tiled=True)  64.6 us
    all_to_all x11, waiting for transfers between devices, exchange(): return lax.all_to_all(slots, PATH, 0, 0, tiled=True)  62.4 us
    all_to_all x11, starting transfers between devices, exchange(): return lax.all_to_all(slots, PATH, 0, 0, tiled=True)  46.3 us
    pallas_call x10, Pallas kernels, shards(): pl.pallas_call(kernel, grid=(1,), in_specs=in_specs, out_specs=[spec((1,...  36.5 us
    pallas_call x1, Pallas kernels, shards(): pl.pallas_call(gram_kernel, grid=(size,), in_specs=[spec((size, factors,...  23.6 us
    pallas_call x1, Pallas kernels, shards(): pl.pallas_call(inverse_kernel, in_specs=[spec((size, HALF + 8, 256))], ou...  10.2 us
    slice x10, local copies, waits for them, and re-layouts, shards(): coefficients = jnp.stack([c[0:basis, 0] for c in coefs], axis=0)  10 us
    pallas_call x2, Pallas kernels, unfold(): pl.pallas_call(unfold_kernel, grid=(number,), in_specs=[pl.BlockSpec((Non...  7.98 us
  transfers between devices with their start and end apart: 11, of which 11 were waited for; matrix products, arithmetic and copies ran while one was open for 4% of the time, Pallas kernels for 3%

profile of v1, /device:TPU:0, one launch (start us, length us, event | category | flops | bytes accessed | tf_op | source)
XLA Modules:
  0.0 278.4 jit_solution(14747398796359862414)
XLA Ops:
  3.3 8.0 %all-to-all-start = ((f32[16,20,128]{2,1,0:T(8,128)}), f32[16,20,128]{2,1,0:T(8,128)S(1)}, u32[]{:S(2)}, u32[]{:S(2)}) async-start(f32[16,20,128]{2,1,0:T(8,128)} %stats.1), calls=%async_computation | async-start | bytes 393216 | tf_op jit(solution)/shard_map/all_to_all | solution.py:271
  15.0 4.7 %all-to-all-done.stats_ref = f32[16,20,128]{2,1,0:T(8,128)S(1)} async-done(((f32[16,20,128]{2,1,0:T(8,128)}), f32[16,20,128]{2,1,0:T(8,128)S(1)}, u32[]{:S(2)}, u32[]{:S(2)}) %all-to-all-start) | async-done | bytes 163872 | tf_op jit(solution)/shard_map/all_to_all | solution.py:271
  20.3 23.6 %gram.1 = (f32[10,240,2048]{2,1,0:T(8,128)}, f32[16,136,256]{2,1,0:T(8,128)}, f32[1,2048]{1,0:T(1,128)}) custom-call(f32[16,20,128]{2,1,0:T(8,128)} %copy-done, f32[10,20,2048]{2,1,0:T(8,128)} %z_ref.5, s32[10,2048]{1,0:T(8,128)} %refs_4_.19, f32[10,2048]{1,0:T(8,128)} %get-tuple-element.38.disc_ref.refs_7_, f32[1,2048]{1,0:T(1,128)} %bitcast.24), custom_call_target="tpu_custom_call" | custom-call | tf_op jit(solution)/shard_map/gram/pallas_call | solution.py:298
  43.9 33.6 %all_to_all.65.parts_ref.refs_0_ = f32[16,136,256]{2,1,0:T(8,128)} all-to-all(f32[16,136,256]{2,1,0:T(8,128)} %get-tuple-element.39), channel_id=1, replica_groups=mesh['book'=8,'path_0'=4,'path_1'=4] {'path_0','path_1'}, dimensions={0} | all-to-all | bytes 4456448 | tf_op jit(solution)/shard_map/all_to_all | solution.py:271
  77.5 10.2 %inverse.1 = f32[16,128,256]{2,1,0:T(8,128)} custom-call(f32[16,136,256]{2,1,0:T(8,128)} %all_to_all.65.parts_ref.refs_0_), custom_call_target="tpu_custom_call" | custom-call | tf_op jit(solution)/shard_map/inverse/pallas_call | solution.py:326
  87.7 31.0 %all_to_all.66.packed_ref = f32[16,128,256]{2,1,0:T(8,128)} all-to-all(f32[16,128,256]{2,1,0:T(8,128)} %inverse.1), channel_id=1, replica_groups=mesh['book'=8,'path_0'=4,'path_1'=4] {'path_0','path_1'}, dimensions={0} | all-to-all | bytes 4194304 | tf_op jit(solution)/shard_map/all_to_all | solution.py:271
  120.4 3.8 %chain.10 = (f32[1,2048]{1,0:T(1,128)}, f32[240,128]{1,0:T(8,128)}, f32[16,1,256]{2,1,0:T(1,128)}) custom-call(f32[16,136,256]{2,1,0:T(8,128)} %all_to_all.65.parts_ref.refs_0_, f32[1,240,256]{2,1,0:T(8,128)} %unfold.2.refs_1_, f32[10,240,2048]{2,1,0:T(8,128)} %get-tuple-element.40.refs_2_.refs_8_, f32[10,2048]{1,0:T(8,128)} %get-tuple-element.41.refs_3_, ...), custom_call_target="tpu_custom_call" | custom-call | tf_op jit(solution)/shard_map/chain/pallas_call | solution.py:372
  124.2 3.5 %all-to-all-start.3 = ((f32[16,1,256]{2,1,0:T(1,128)}), f32[16,1,256]{2,1,0:T(1,128)S(1)}, u32[]{:S(2)}, u32[]{:S(2)}) async-start(f32[16,1,256]{2,1,0:T(1,128)} %get-tuple-element.43), calls=%async_computation.3 | async-start | bytes 32768 | tf_op jit(solution)/shard_map/all_to_all | solution.py:271
  128.7 6.3 %unfold.3.refs_1_ = f32[9,240,256]{2,1,0:T(8,128)} custom-call(f32[16,128,256]{2,1,0:T(8,128)} %all_to_all.66.packed_ref), custom_call_target="tpu_custom_call" | custom-call | tf_op jit(solution)/shard_map/unfold/pallas_call | solution.py:338
  135.8 3.7 %chain.11 = (f32[1,2048]{1,0:T(1,128)}, f32[240,128]{1,0:T(8,128)}, f32[16,1,256]{2,1,0:T(1,128)}) custom-call(f32[16,1,256]{2,1,0:T(1,128)} %copy-done.2, f32[9,240,256]{2,1,0:T(8,128)} %unfold.3.refs_1_, f32[10,240,2048]{2,1,0:T(8,128)} %get-tuple-element.40.refs_2_.refs_8_, f32[10,2048]{1,0:T(8,128)} %get-tuple-element.41.refs_3_, s32[10,2048]{1,0:T(8,128)} %refs_4_.19, ...), custom_call_target="tpu_custom_call" | custom-call | tf_op jit(solution)/shard_map/chain/pallas_call | solution.py:372
  139.6 6.9 %all-to-all-start.4 = ((f32[16,1,256]{2,1,0:T(1,128)}), f32[16,1,256]{2,1,0:T(1,128)S(1)}, u32[]{:S(2)}, u32[]{:S(2)}) async-start(f32[16,1,256]{2,1,0:T(1,128)} %get-tuple-element.45), calls=%async_computation.4 | async-start | bytes 32768 | tf_op jit(solution)/shard_map/all_to_all | solution.py:271
  147.5 6.6 %all-to-all-done.4.refs_0_ = f32[16,1,256]{2,1,0:T(1,128)S(1)} async-done(((f32[16,1,256]{2,1,0:T(1,128)}), f32[16,1,256]{2,1,0:T(1,128)S(1)}, u32[]{:S(2)}, u32[]{:S(2)}) %all-to-all-start.4) | async-done | bytes 16416 | tf_op jit(solution)/shard_map/all_to_all | solution.py:271
  154.7 3.7 %chain.12 = (f32[1,2048]{1,0:T(1,128)}, f32[240,128]{1,0:T(8,128)}, f32[16,1,256]{2,1,0:T(1,128)}) custom-call(f32[16,1,256]{2,1,0:T(1,128)} %copy-done.3, f32[9,240,256]{2,1,0:T(8,128)} %unfold.3.refs_1_, f32[10,240,2048]{2,1,0:T(8,128)} %get-tuple-element.40.refs_2_.refs_8_, f32[10,2048]{1,0:T(8,128)} %get-tuple-element.41.refs_3_, s32[10,2048]{1,0:T(8,128)} %refs_4_.19, ...), custom_call_target="tpu_custom_call" | custom-call | tf_op jit(solution)/shard_map/chain/pallas_call | solution.py:372
  158.4 3.5 %all-to-all-start.5 = ((f32[16,1,256]{2,1,0:T(1,128)}), f32[16,1,256]{2,1,0:T(1,128)S(1)}, u32[]{:S(2)}, u32[]{:S(2)}) async-start(f32[16,1,256]{2,1,0:T(1,128)} %get-tuple-element.47), calls=%async_computation.5 | async-start | bytes 32768 | tf_op jit(solution)/shard_map/all_to_all | solution.py:271
  162.9 6.5 %all-to-all-done.5.refs_0_ = f32[16,1,256]{2,1,0:T(1,128)S(1)} async-done(((f32[16,1,256]{2,1,0:T(1,128)}), f32[16,1,256]{2,1,0:T(1,128)S(1)}, u32[]{:S(2)}, u32[]{:S(2)}) %all-to-all-start.5) | async-done | bytes 16416 | tf_op jit(solution)/shard_map/all_to_all | solution.py:271
  170.1 3.7 %chain.13 = (f32[1,2048]{1,0:T(1,128)}, f32[240,128]{1,0:T(8,128)}, f32[16,1,256]{2,1,0:T(1,128)}) custom-call(f32[16,1,256]{2,1,0:T(1,128)} %copy-done.4, f32[9,240,256]{2,1,0:T(8,128)} %unfold.3.refs_1_, f32[10,240,2048]{2,1,0:T(8,128)} %get-tuple-element.40.refs_2_.refs_8_, f32[10,2048]{1,0:T(8,128)} %get-tuple-element.41.refs_3_, s32[10,2048]{1,0:T(8,128)} %refs_4_.19, ...), custom_call_target="tpu_custom_call" | custom-call | tf_op jit(solution)/shard_map/chain/pallas_call | solution.py:372
  173.8 3.5 %all-to-all-start.6 = ((f32[16,1,256]{2,1,0:T(1,128)}), f32[16,1,256]{2,1,0:T(1,128)S(1)}, u32[]{:S(2)}, u32[]{:S(2)}) async-start(f32[16,1,256]{2,1,0:T(1,128)} %get-tuple-element.49), calls=%async_computation.6 | async-start | bytes 32768 | tf_op jit(solution)/shard_map/all_to_all | solution.py:271
  178.3 6.5 %all-to-all-done.6.refs_0_ = f32[16,1,256]{2,1,0:T(1,128)S(1)} async-done(((f32[16,1,256]{2,1,0:T(1,128)}), f32[16,1,256]{2,1,0:T(1,128)S(1)}, u32[]{:S(2)}, u32[]{:S(2)}) %all-to-all-start.6) | async-done | bytes 16416 | tf_op jit(solution)/shard_map/all_to_all | solution.py:271
  185.4 3.7 %chain.14 = (f32[1,2048]{1,0:T(1,128)}, f32[240,128]{1,0:T(8,128)}, f32[16,1,256]{2,1,0:T(1,128)}) custom-call(f32[16,1,256]{2,1,0:T(1,128)} %copy-done.5, f32[9,240,256]{2,1,0:T(8,128)} %unfold.3.refs_1_, f32[10,240,2048]{2,1,0:T(8,128)} %get-tuple-element.40.refs_2_.refs_8_, f32[10,2048]{1,0:T(8,128)} %get-tuple-element.41.refs_3_, s32[10,2048]{1,0:T(8,128)} %refs_4_.19, ...), custom_call_target="tpu_custom_call" | custom-call | tf_op jit(solution)/shard_map/chain/pallas_call | solution.py:372
  189.2 3.5 %all-to-all-start.7 = ((f32[16,1,256]{2,1,0:T(1,128)}), f32[16,1,256]{2,1,0:T(1,128)S(1)}, u32[]{:S(2)}, u32[]{:S(2)}) async-start(f32[16,1,256]{2,1,0:T(1,128)} %get-tuple-element.51), calls=%async_computation.7 | async-start | bytes 32768 | tf_op jit(solution)/shard_map/all_to_all | solution.py:271
  193.7 6.5 %all-to-all-done.7.refs_0_ = f32[16,1,256]{2,1,0:T(1,128)S(1)} async-done(((f32[16,1,256]{2,1,0:T(1,128)}), f32[16,1,256]{2,1,0:T(1,128)S(1)}, u32[]{:S(2)}, u32[]{:S(2)}) %all-to-all-start.7) | async-done | bytes 16416 | tf_op jit(solution)/shard_map/all_to_all | solution.py:271
  200.8 3.7 %chain.15 = (f32[1,2048]{1,0:T(1,128)}, f32[240,128]{1,0:T(8,128)}, f32[16,1,256]{2,1,0:T(1,128)}) custom-call(f32[16,1,256]{2,1,0:T(1,128)} %copy-done.6, f32[9,240,256]{2,1,0:T(8,128)} %unfold.3.refs_1_, f32[10,240,2048]{2,1,0:T(8,128)} %get-tuple-element.40.refs_2_.refs_8_, f32[10,2048]{1,0:T(8,128)} %get-tuple-element.41.refs_3_, s32[10,2048]{1,0:T(8,128)} %refs_4_.19, ...), custom_call_target="tpu_custom_call" | custom-call | tf_op jit(solution)/shard_map/chain/pallas_call | solution.py:372
  204.6 3.5 %all-to-all-start.8 = ((f32[16,1,256]{2,1,0:T(1,128)}), f32[16,1,256]{2,1,0:T(1,128)S(1)}, u32[]{:S(2)}, u32[]{:S(2)}) async-start(f32[16,1,256]{2,1,0:T(1,128)} %get-tuple-element.53), calls=%async_computation.8 | async-start | bytes 32768 | tf_op jit(solution)/shard_map/all_to_all | solution.py:271
  209.1 6.5 %all-to-all-done.8.refs_0_ = f32[16,1,256]{2,1,0:T(1,128)S(1)} async-done(((f32[16,1,256]{2,1,0:T(1,128)}), f32[16,1,256]{2,1,0:T(1,128)S(1)}, u32[]{:S(2)}, u32[]{:S(2)}) %all-to-all-start.8) | async-done | bytes 16416 | tf_op jit(solution)/shard_map/all_to_all | solution.py:271
  216.2 3.7 %chain.16 = (f32[1,2048]{1,0:T(1,128)}, f32[240,128]{1,0:T(8,128)}, f32[16,1,256]{2,1,0:T(1,128)}) custom-call(f32[16,1,256]{2,1,0:T(1,128)} %copy-done.7, f32[9,240,256]{2,1,0:T(8,128)} %unfold.3.refs_1_, f32[10,240,2048]{2,1,0:T(8,128)} %get-tuple-element.40.refs_2_.refs_8_, f32[10,2048]{1,0:T(8,128)} %get-tuple-element.41.refs_3_, s32[10,2048]{1,0:T(8,128)} %refs_4_.19, ...), custom_call_target="tpu_custom_call" | custom-call | tf_op jit(solution)/shard_map/chain/pallas_call | solution.py:372
  219.9 3.5 %all-to-all-start.9 = ((f32[16,1,256]{2,1,0:T(1,128)}), f32[16,1,256]{2,1,0:T(1,128)S(1)}, u32[]{:S(2)}, u32[]{:S(2)}) async-start(f32[16,1,256]{2,1,0:T(1,128)} %get-tuple-element.55), calls=%async_computation.9 | async-start | bytes 32768 | tf_op jit(solution)/shard_map/all_to_all | solution.py:271
  224.5 6.5 %all-to-all-done.9.refs_0_ = f32[16,1,256]{2,1,0:T(1,128)S(1)} async-done(((f32[16,1,256]{2,1,0:T(1,128)}), f32[16,1,256]{2,1,0:T(1,128)S(1)}, u32[]{:S(2)}, u32[]{:S(2)}) %all-to-all-start.9) | async-done | bytes 16416 | tf_op jit(solution)/shard_map/all_to_all | solution.py:271
  231.6 3.7 %chain.17 = (f32[1,2048]{1,0:T(1,128)}, f32[240,128]{1,0:T(8,128)}, f32[16,1,256]{2,1,0:T(1,128)}) custom-call(f32[16,1,256]{2,1,0:T(1,128)} %copy-done.8, f32[9,240,256]{2,1,0:T(8,128)} %unfold.3.refs_1_, f32[10,240,2048]{2,1,0:T(8,128)} %get-tuple-element.40.refs_2_.refs_8_, f32[10,2048]{1,0:T(8,128)} %get-tuple-element.41.refs_3_, s32[10,2048]{1,0:T(8,128)} %refs_4_.19, ...), custom_call_target="tpu_custom_call" | custom-call | tf_op jit(solution)/shard_map/chain/pallas_call | solution.py:372
  239.8 6.5 %all-to-all-done.10.refs_0_ = f32[16,1,256]{2,1,0:T(1,128)S(1)} async-done(((f32[16,1,256]{2,1,0:T(1,128)}), f32[16,1,256]{2,1,0:T(1,128)S(1)}, u32[]{:S(2)}, u32[]{:S(2)}) %all-to-all-start.10) | async-done | bytes 16416 | tf_op jit(solution)/shard_map/all_to_all | solution.py:271
  247.0 3.7 %chain.18 = (f32[1,2048]{1,0:T(1,128)}, f32[240,128]{1,0:T(8,128)}, f32[16,1,256]{2,1,0:T(1,128)}) custom-call(f32[16,1,256]{2,1,0:T(1,128)} %copy-done.9, f32[9,240,256]{2,1,0:T(8,128)} %unfold.3.refs_1_, f32[10,240,2048]{2,1,0:T(8,128)} %get-tuple-element.40.refs_2_.refs_8_, f32[10,2048]{1,0:T(8,128)} %get-tuple-element.41.refs_3_, s32[10,2048]{1,0:T(8,128)} %refs_4_.19, ...), custom_call_target="tpu_custom_call" | custom-call | tf_op jit(solution)/shard_map/chain/pallas_call | solution.py:372
  255.2 6.5 %all-to-all-done.11.refs_0_ = f32[16,1,256]{2,1,0:T(1,128)S(1)} async-done(((f32[16,1,256]{2,1,0:T(1,128)}), f32[16,1,256]{2,1,0:T(1,128)S(1)}, u32[]{:S(2)}, u32[]{:S(2)}) %all-to-all-start.11) | async-done | bytes 16416 | tf_op jit(solution)/shard_map/all_to_all | solution.py:271
  270.8 5.3 %all-to-all-done.12 = f32[16,1,128]{2,1,0:T(1,128)S(1)} async-done(((f32[16,1,128]{2,1,0:T(1,128)}), f32[16,1,128]{2,1,0:T(1,128)S(1)}, u32[]{:S(2)}, u32[]{:S(2)}) %all-to-all-start.12) | async-done | bytes 8224 | tf_op jit(solution)/shard_map/all_to_all | solution.py:271
  (40 shorter events, 38.8 us)
Async XLA Ops:
  3.3 16.3 %all-to-all-start = ((f32[16,20,128]{2,1,0:T(8,128)}), f32[16,20,128]{2,1,0:T(8,128)S(1)}, u32[]{:S(2)}, u32[]{:S(2)}) async-start(f32[16,20,128]{2,1,0:T(8,128)} %stats.1), calls=%async_computation | async-start | bytes 393216 | tf_op jit(solution)/shard_map/all_to_all | solution.py:271
  19.7 0.7 copy-start
  124.2 11.0 %all-to-all-start.3 = ((f32[16,1,256]{2,1,0:T(1,128)}), f32[16,1,256]{2,1,0:T(1,128)S(1)}, u32[]{:S(2)}, u32[]{:S(2)}) async-start(f32[16,1,256]{2,1,0:T(1,128)} %get-tuple-element.43), calls=%async_computation.3 | async-start | bytes 32768 | tf_op jit(solution)/shard_map/all_to_all | solution.py:271
  135.2 0.6 copy-start.2
  139.6 14.5 %all-to-all-start.4 = ((f32[16,1,256]{2,1,0:T(1,128)}), f32[16,1,256]{2,1,0:T(1,128)S(1)}, u32[]{:S(2)}, u32[]{:S(2)}) async-start(f32[16,1,256]{2,1,0:T(1,128)} %get-tuple-element.45), calls=%async_computation.4 | async-start | bytes 32768 | tf_op jit(solution)/shard_map/all_to_all | solution.py:271
  154.1 0.6 copy-start.3
  158.4 11.0 %all-to-all-start.5 = ((f32[16,1,256]{2,1,0:T(1,128)}), f32[16,1,256]{2,1,0:T(1,128)S(1)}, u32[]{:S(2)}, u32[]{:S(2)}) async-start(f32[16,1,256]{2,1,0:T(1,128)} %get-tuple-element.47), calls=%async_computation.5 | async-start | bytes 32768 | tf_op jit(solution)/shard_map/all_to_all | solution.py:271
  169.5 0.6 copy-start.4
  173.8 11.0 %all-to-all-start.6 = ((f32[16,1,256]{2,1,0:T(1,128)}), f32[16,1,256]{2,1,0:T(1,128)S(1)}, u32[]{:S(2)}, u32[]{:S(2)}) async-start(f32[16,1,256]{2,1,0:T(1,128)} %get-tuple-element.49), calls=%async_computation.6 | async-start | bytes 32768 | tf_op jit(solution)/shard_map/all_to_all | solution.py:271
  184.8 0.6 copy-start.5
  189.2 11.0 %all-to-all-start.7 = ((f32[16,1,256]{2,1,0:T(1,128)}), f32[16,1,256]{2,1,0:T(1,128)S(1)}, u32[]{:S(2)}, u32[]{:S(2)}) async-start(f32[16,1,256]{2,1,0:T(1,128)} %get-tuple-element.51), calls=%async_computation.7 | async-start | bytes 32768 | tf_op jit(solution)/shard_map/all_to_all | solution.py:271
  200.2 0.6 copy-start.6
  204.6 11.0 %all-to-all-start.8 = ((f32[16,1,256]{2,1,0:T(1,128)}), f32[16,1,256]{2,1,0:T(1,128)S(1)}, u32[]{:S(2)}, u32[]{:S(2)}) async-start(f32[16,1,256]{2,1,0:T(1,128)} %get-tuple-element.53), calls=%async_computation.8 | async-start | bytes 32768 | tf_op jit(solution)/shard_map/all_to_all | solution.py:271
  215.6 0.6 copy-start.7
  219.9 11.0 %all-to-all-start.9 = ((f32[16,1,256]{2,1,0:T(1,128)}), f32[16,1,256]{2,1,0:T(1,128)S(1)}, u32[]{:S(2)}, u32[]{:S(2)}) async-start(f32[16,1,256]{2,1,0:T(1,128)} %get-tuple-element.55), calls=%async_computation.9 | async-start | bytes 32768 | tf_op jit(solution)/shard_map/all_to_all | solution.py:271
  231.0 0.6 copy-start.8
  235.3 11.0 %all-to-all-start.10 = ((f32[16,1,256]{2,1,0:T(1,128)}), f32[16,1,256]{2,1,0:T(1,128)S(1)}, u32[]{:S(2)}, u32[]{:S(2)}) async-start(f32[16,1,256]{2,1,0:T(1,128)} %get-tuple-element.57), calls=%async_computation.10 | async-start | bytes 32768 | tf_op jit(solution)/shard_map/all_to_all | solution.py:271
  246.4 0.6 copy-start.9
  250.7 11.0 %all-to-all-start.11 = ((f32[16,1,256]{2,1,0:T(1,128)}), f32[16,1,256]{2,1,0:T(1,128)S(1)}, u32[]{:S(2)}, u32[]{:S(2)}) async-start(f32[16,1,256]{2,1,0:T(1,128)} %get-tuple-element.59), calls=%async_computation.11 | async-start | bytes 32768 | tf_op jit(solution)/shard_map/all_to_all | solution.py:271
  261.7 0.6 copy-start.1
  265.1 10.9 %all-to-all-start.12 = ((f32[16,1,128]{2,1,0:T(1,128)}), f32[16,1,128]{2,1,0:T(1,128)S(1)}, u32[]{:S(2)}, u32[]{:S(2)}) async-start(f32[16,1,128]{2,1,0:T(1,128)} %get-tuple-element.62), calls=%async_computation.12 | async-start | bytes 16384 | tf_op jit(solution)/shard_map/all_to_all | solution.py:271

commit v2 on v1

--- a/solution.py
+++ b/solution.py
@@ -27,6 +27,13 @@
     return pl.BlockSpec(shape, lambda *_: index)
 
 
+WHOLE = pl.BlockSpec(memory_space=pltpu.VMEM)
+
+
+def near(x):
+    return pltpu.with_memory_space_constraint(x, pltpu.VMEM)
+
+
 def lanes_of(shape):
     return lax.broadcasted_iota(jnp.int32, shape, 1)
 
@@ -74,11 +81,20 @@
     return jnp.concatenate([row, jnp.zeros((8, 256 - ROWS), f32)], axis=1)
 
 
-def gram_kernel(stats_ref, z_ref, m_ref, disc_ref, term_ref, phi_ref, slot_ref, v_ref, x_ref, gram_ref, rhs_ref):
+def gram_kernel(stats_ref, z_all_ref, m_ref, disc_ref, term_ref, *refs):
+    *phi_refs, slot_ref, v_ref, phi_two_ref, x_ref, gram_ref, rhs_ref, sems = refs
     step = pl.program_id(0)
-    dates = m_ref.shape[0]
-    factors = z_ref.shape[0]
-    paths = z_ref.shape[1]
+    dates, factors, paths = z_all_ref.shape
+    z_ref = z_all_ref.at[jnp.maximum(dates - 1 - step, 0)]
+    side = step % 2
+    phi_ref = phi_two_ref.at[side]
+
+    def copy_of(date):
+        return pltpu.make_async_copy(phi_ref, phi_refs[date], sems.at[side])
+
+    @pl.when((step >= 2) & (step < dates + 2))
+    def _():
+        copy_of(0).wait()
 
     @pl.when(step < dates)
     def _():
@@ -124,6 +140,11 @@
             return carry
 
         lax.fori_loop(0, paths // CHUNK, chunk, 0)
+        for date in range(dates):
+
+            @pl.when(d == date)
+            def _(date=date):
+                copy_of(date).start()
 
         @pl.when(step == 0)
         def _():
@@ -228,21 +249,32 @@
 
 
 def unfold_kernel(packed_ref, out_ref):
-    first, beside, last = unfolded(packed_ref[...])
-    out_ref[0:HALF, 0:HALF] = first
-    out_ref[0:HALF, HALF:] = beside
-    out_ref[HALF:, 0:HALF] = beside.T[0 : ROWS - HALF, :]
-    out_ref[HALF:, HALF:] = last[0 : ROWS - HALF, :]
-
-
-def chain_kernel(date, *refs):
-    parts_ref, inv_ref, phi_ref, ex_ref, m_ref, index_ref, v_ref, disc_ref = refs[:8]
+    for i in range(out_ref.shape[0]):
+        first, beside, last = unfolded(packed_ref[i])
+        out_ref[i, 0:HALF, 0:HALF] = first
+        out_ref[i, 0:HALF, HALF:] = beside
+        out_ref[i, HALF:, 0:HALF] = beside.T[0 : ROWS - HALF, :]
+        out_ref[i, HALF:, HALF:] = last[0 : ROWS - HALF, :]
+
+
+def chain_kernel(date, dates, *refs):
+    inv_ref, parts_ref, phi_ref, ex_ref, m_ref, index_ref, v_ref, disc_ref = refs[:8]
+    refs = refs[8:]
+    if date:
+        next_ref = refs[0]
+        refs = refs[1:]
+    if date == dates - 1:
+        coefs = jnp.zeros((ROWS, 128), f32)
+    else:
+        coefs = refs[0][...]
+        refs = refs[1:]
     rhs = parts_ref[0, 0:1, :]
     for i in range(1, parts_ref.shape[0]):
         rhs = rhs + parts_ref[i, 0:1, :]
-    product = inv_ref[...] * rhs
+    product = inv_ref[date] * rhs
     coef = jnp.sum(product[:, 0:128] + product[:, 128:], axis=1, keepdims=True)
     coef = jnp.broadcast_to(coef, (ROWS, 128))
+    out_ref, coef_ref, send_ref = refs
     continuation = []
     for c in range(0, v_ref.shape[1], 128):
         continuation.append(jnp.sum(coef * phi_ref[:, c : c + 128], axis=0, keepdims=True))
@@ -253,18 +285,23 @@
     value = v_ref[...]
     value = value + weights * (exercise - value)
     if date:
-        next_ref, out_ref, coef_ref, send_ref = refs[8:]
         value = value * disc_ref[date - 1 : date, :]
         row = rhs_row(next_ref, value * m_ref[date - 1 : date, :].astype(f32))
         for i in range(send_ref.shape[0]):
             send_ref[i] = row[0:1, :]
     else:
-        out_ref, coef_ref, send_ref = refs[8:]
         total = jnp.broadcast_to(jnp.sum(value, axis=1, keepdims=True), (1, 128))
         for i in range(send_ref.shape[0]):
             send_ref[i] = total
     out_ref[...] = value
-    coef_ref[...] = coef
+    coefs = jnp.where(lanes_of((ROWS, 128)) == date, coef, coefs)
+    if date:
+        coef_ref[...] = coefs
+    else:
+        for c in range(0, ROWS, 128):
+            coef_ref[:, c : c + 128] = coefs[0:128, :].T if c == 0 else jnp.concatenate(
+                [coefs[c:, :], jnp.zeros((128 - (ROWS - c), 128), f32)], axis=0
+            ).T
 
 
 def exchange(slots):
@@ -277,110 +314,101 @@
     sds = jax.ShapeDtypeStruct
     terminal = terminal.reshape(1, paths)
     date_index = date_index.reshape(1, paths)
+    vmem = pltpu.VMEM
+    limit = pltpu.CompilerParams(vmem_limit_bytes=24 << 20)
     stats = pl.pallas_call(
-        stats_kernel, out_shape=sds((size, factors, 128), f32), name="stats"
+        stats_kernel,
+        out_shape=vmem((size, factors, 128), f32),
+        out_specs=WHOLE,
+        compiler_params=limit,
+        name="stats",
     )(states, itm_flags)
     stats = exchange(stats)
     exercise, discount = pl.pallas_call(
         swap_kernel,
-        in_specs=[
-            pl.BlockSpec(memory_space=pltpu.SMEM),
-            pl.BlockSpec(memory_space=pltpu.VMEM),
-        ],
-        out_shape=[sds((dates, paths), f32), sds((dates, paths), f32)],
+        in_specs=[pl.BlockSpec(memory_space=pltpu.SMEM), WHOLE],
+        out_specs=[WHOLE, WHOLE],
+        out_shape=[vmem((dates, paths), f32), vmem((dates, paths), f32)],
         scratch_shapes=[pltpu.VMEM((factors, paths), f32)],
+        compiler_params=limit,
         name="swap",
     )(strike, states)
 
-    def date_of(i):
-        return jnp.maximum(dates - 1 - i, 0)
-
-    phi, slots, value = pl.pallas_call(
+    *phi, slots, value = pl.pallas_call(
         gram_kernel,
         grid=(size,),
-        in_specs=[
-            spec((size, factors, 128)),
-            pl.BlockSpec((None, factors, paths), lambda i: (date_of(i), 0, 0)),
-            spec((dates, paths)),
-            spec((dates, paths)),
-            spec((1, paths)),
+        in_specs=[WHOLE, WHOLE, WHOLE, WHOLE, WHOLE],
+        out_specs=[pl.BlockSpec(memory_space=pltpu.HBM)] * dates
+        + [
+            pl.BlockSpec((None, HALF + 8, 256), lambda i: (jnp.where(i < dates, jnp.maximum(dates - 1 - i, 0), i), 0, 0)),
+            WHOLE,
         ],
-        out_specs=[
-            pl.BlockSpec((None, ROWS, paths), lambda i: (date_of(i), 0, 0)),
-            pl.BlockSpec((None, HALF + 8, 256), lambda i: (jnp.where(i < dates, date_of(i), i), 0, 0)),
-            spec((1, paths)),
-        ],
-        out_shape=[
-            sds((dates, ROWS, paths), f32),
+        out_shape=[pltpu.HBM((ROWS, paths), f32)] * dates
+        + [
             sds((size, HALF + 8, 256), f32),
-            sds((1, paths), f32),
+            vmem((1, paths), f32),
         ],
         scratch_shapes=[
+            pltpu.VMEM((2, ROWS, paths), f32),
             pltpu.VMEM((factors, CHUNK), f32),
             pltpu.VMEM((256, 256), f32),
             pltpu.VMEM((8, 256), f32),
+            pltpu.SemaphoreType.DMA((2,)),
         ],
+        compiler_params=limit,
         name="gram",
-    )(stats, states, itm_flags, discount, terminal)
+    )(near(stats), states, itm_flags, near(discount), terminal)
     slots = exchange(slots)
     inverse = pl.pallas_call(
         inverse_kernel,
+        grid=(1,),
         in_specs=[spec((size, HALF + 8, 256))],
         out_specs=spec((size, HALF, 256)),
-        grid=(1,),
-        out_shape=sds((size, HALF, 256), f32),
+        out_shape=pltpu.HBM((size, HALF, 256), f32),
         scratch_shapes=[pltpu.VMEM((256, 256), f32)],
+        compiler_params=limit,
         name="inverse",
     )(slots)
     inverse = exchange(inverse)
-
-    def unfold(first, number):
-        return pl.pallas_call(
-            unfold_kernel,
-            grid=(number,),
-            in_specs=[pl.BlockSpec((None, HALF, 256), lambda i: (first + i, 0, 0))],
-            out_specs=pl.BlockSpec((None, ROWS, 256), lambda i: (i, 0, 0)),
-            out_shape=sds((number, ROWS, 256), f32),
-            name="unfold",
-        )(inverse)
-
-    last_inverse = unfold(dates - 1, 1)
-    other_inverse = unfold(0, dates - 1)
-    received = slots
-    coefs = [None] * dates
+    inverse = pl.pallas_call(
+        unfold_kernel,
+        grid=(1,),
+        in_specs=[spec((dates, HALF, 256))],
+        out_specs=WHOLE,
+        out_shape=vmem((dates, ROWS, 256), f32),
+        compiler_params=limit,
+        name="unfold",
+    )(inverse)
+    received = slots[:, HALF : HALF + 1, :]
+    coefs = None
     for date in range(dates - 1, -1, -1):
-        is_last = date == dates - 1
-        args = [received, last_inverse if is_last else other_inverse, phi, exercise, itm_flags, date_index, value, discount]
-        in_specs = [
-            spec((size, 8, 256), (0, HALF // 8, 0)) if is_last else spec((size, 1, 256)),
-            spec((None, ROWS, 256), (0 if is_last else date, 0, 0)),
-            spec((None, ROWS, paths), (date, 0, 0)),
-            spec((dates, paths)),
-            spec((dates, paths)),
-            spec((1, paths)),
-            spec((1, paths)),
-            spec((dates, paths)),
-        ]
+        args = [inverse, received, phi[date], exercise, itm_flags, date_index, value, discount]
         if date:
-            args.append(phi)
-            in_specs.append(spec((None, ROWS, paths), (date - 1, 0, 0)))
-        width = 256 if date else 128
+            args.append(phi[date - 1])
+        if date < dates - 1:
+            args.append(coefs)
 
         def kernel(*refs, date=date):
-            chain_kernel(date, *refs)
-
-        value, coefs[date], send = pl.pallas_call(
+            chain_kernel(date, dates, *refs)
+
+        value, coefs, send = pl.pallas_call(
             kernel,
-            grid=(1,),
-            in_specs=in_specs,
-            out_specs=[spec((1, paths)), spec((ROWS, 128)), spec((size, 1, width))],
-            out_shape=[sds((1, paths), f32), sds((ROWS, 128), f32), sds((size, 1, width), f32)],
+            in_specs=[WHOLE] * len(args),
+            out_specs=[WHOLE] * 3,
+            out_shape=[
+                vmem((1, paths), f32),
+                vmem((ROWS, 128), f32),
+                vmem((size, 1, 256), f32),
+            ]
+            if date
+            else [sds((1, paths), f32), sds((128, 256), f32), sds((size, 1, 128), f32)],
+            compiler_params=limit,
             name="chain",
-        )(*args)
+        )(*(near(x) for x in args))
         received = exchange(send)
     book_price = jnp.sum(received[:, 0, 0:1], axis=0) / (paths * size)
     basis = 1 + factors + factors * (factors + 1) // 2
-    coefficients = jnp.stack([c[0:basis, 0] for c in coefs], axis=0)
+    coefficients = coefs[0:dates, 0:basis]
     return (value.reshape(paths), book_price, coefficients)
 
 

time: 280 us -> 233 us (0.83)
  blocking collectives: 64.6 us -> 127 us
  Pallas kernels: 83.9 us -> 39.6 us
  starting transfers between devices: 46.3 us -> 15.9 us
  waiting for transfers between devices: 62.4 us -> 41.9 us
  local copies, waits for them, and re-layouts: 17.4 us -> 3.75 us
    all_to_all x2 -> x10, blocking collectives: 64.6 us -> 127 us  [exchange(): return lax.all_to_all(slots, PATH, 0, 0, tiled=True)]
    pallas_call x15 -> x14, Pallas kernels: 80.9 us -> 38.9 us  [the longest x1 20.8 us: shards(): pl.pallas_call(gram_kernel, grid=(size,), in_specs=[WHOLE, WHOLE, WHOLE,...]
    all_to_all x11 -> x3, starting transfers between devices: 46.3 us -> 15.9 us  [exchange(): return lax.all_to_all(slots, PATH, 0, 0, tiled=True)]
    all_to_all x11 -> x3, waiting for transfers between devices: 62.4 us -> 41.9 us  [exchange(): return lax.all_to_all(slots, PATH, 0, 0, tiled=True)]
    slice x10 -> x2, local copies, waits for them, and re-layouts: 10 us -> 0.62 us  [the longest x1 0.61 us: shards(): coefficients = coefs[0:dates, 0:basis]]
    unnamed x20 -> x32, local copies, waits for them, and re-layouts: 6.13 us -> 3.14 us
  transfers between devices with their start and end apart: 11 -> 3, of which waited for: 11 -> 3; matrix products, arithmetic and copies ran while one was open for 4% -> 0% of each run, Pallas kernels for 3% -> 0%
where the time goes in v2:
time: 233 us; the launch traced here: 232 us
  blocking collectives  127 us (55%)
  waiting for transfers between devices  41.9 us (18%)
  Pallas kernels  39.6 us (17%)
  starting transfers between devices  15.9 us (7%)
  local copies, waits for them, and re-layouts  3.75 us (2%)
  between operations  3.16 us (1%)
    all_to_all x10, blocking collectives, exchange(): return lax.all_to_all(slots, PATH, 0, 0, tiled=True)  127 us
    all_to_all x3, waiting for transfers between devices, exchange(): return lax.all_to_all(slots, PATH, 0, 0, tiled=True)  41.9 us
    pallas_call x1, Pallas kernels, shards(): pl.pallas_call(gram_kernel, grid=(size,), in_specs=[WHOLE, WHOLE, WHOLE,...  20.8 us
    all_to_all x3, starting transfers between devices, exchange(): return lax.all_to_all(slots, PATH, 0, 0, tiled=True)  15.9 us
    pallas_call x1, Pallas kernels, shards(): pl.pallas_call(inverse_kernel, grid=(1,), in_specs=[spec((size, HALF + 8,...  8.47 us
    pallas_call x10, Pallas kernels, shards(): pl.pallas_call(kernel, in_specs=[WHOLE] * len(args), out_specs=[WHOLE] *...  6.6 us
  transfers between devices with their start and end apart: 3, of which 3 were waited for; matrix products, arithmetic and copies ran while one was open for 0% of the time, Pallas kernels for 0%

profile of v2, /device:TPU:0, one launch (start us, length us, event | category | flops | bytes accessed | tf_op | source)
XLA Modules:
  0.0 232.3 jit_solution(10839495142546883479)
XLA Ops:
  0.6 0.9 copy-done
  1.5 1.5 copy-done.2
  3.1 1.2 stats.1
  4.3 8.0 %all-to-all-start = ((f32[16,20,128]{2,1,0:T(8,128)}), f32[16,20,128]{2,1,0:T(8,128)S(1)}, u32[]{:S(2)}, u32[]{:S(2)}) async-start(f32[16,20,128]{2,1,0:T(8,128)} %stats.1), calls=%async_computation | async-start | bytes 393216 | tf_op jit(solution)/shard_map/all_to_all | solution.py:308
  12.9 0.8 swap.1
  13.7 6.9 %all-to-all-done.stats_ref = f32[16,20,128]{2,1,0:T(8,128)S(1)} async-done(((f32[16,20,128]{2,1,0:T(8,128)}), f32[16,20,128]{2,1,0:T(8,128)S(1)}, u32[]{:S(2)}, u32[]{:S(2)}) %all-to-all-start) | async-done | bytes 163872 | tf_op jit(solution)/shard_map/all_to_all | solution.py:308
  20.6 20.8 %gram.1 = (f32[240,2048]{1,0:T(8,128)}, f32[240,2048]{1,0:T(8,128)}, f32[240,2048]{1,0:T(8,128)}, f32[240,2048]{1,0:T(8,128)}, f32[240,2048]{1,0:T(8,128)}, /*in...) custom-call(f32[16,20,128]{2,1,0:T(8,128)S(1)} %all-to-all-done.stat, ...), custom_call_target="tpu_custom_call" | custom-call | tf_op jit(solution)/shard_map/gram/pallas_call | solution.py:337
  41.4 32.1 %all_to_all.65.parts_ref = f32[16,136,256]{2,1,0:T(8,128)S(1)} all-to-all(f32[16,136,256]{2,1,0:T(8,128)S(1)} %get-tuple-element.48), channel_id=1, replica_groups=mesh['book'=8,'path_0'=4,'path_1'=4] {'path_0','path_1'}, dimensions={0} | all-to-all | bytes 4456448 | tf_op jit(solution)/shard_map/all_to_all | solution.py:308
  73.5 8.5 %inverse.1 = f32[16,128,256]{2,1,0:T(8,128)} custom-call(f32[16,136,256]{2,1,0:T(8,128)S(1)} %all_to_all.65.parts_ref), custom_call_target="tpu_custom_call" | custom-call | tf_op jit(solution)/shard_map/inverse/pallas_call | solution.py:362
  82.0 4.4 %all-to-all-start.2 = ((f32[16,128,256]{2,1,0:T(8,128)}), f32[16,128,256]{2,1,0:T(8,128)}, u32[]{:S(2)}, u32[]{:S(2)}) async-start(f32[16,128,256]{2,1,0:T(8,128)} %inverse.1), calls=%async_computation.2 | async-start | bytes 4194304 | tf_op jit(solution)/shard_map/all_to_all | solution.py:308
  86.4 28.2 %all-to-all-done.2.packed_ref = f32[16,128,256]{2,1,0:T(8,128)} async-done(((f32[16,128,256]{2,1,0:T(8,128)}), f32[16,128,256]{2,1,0:T(8,128)}, u32[]{:S(2)}, u32[]{:S(2)}) %all-to-all-start.2) | async-done | bytes 2097184 | tf_op jit(solution)/shard_map/all_to_all | solution.py:308
  114.7 1.9 unfold.1.refs_0_
  117.8 10.2 %all_to_all.66.refs_1_ = f32[16,1,256]{2,1,0:T(1,128)S(1)} all-to-all(f32[16,1,256]{2,1,0:T(1,128)S(1)} %get-tuple-element.53), channel_id=1, replica_groups=mesh['book'=8,'path_0'=4,'path_1'=4] {'path_0','path_1'}, dimensions={0} | all-to-all | bytes 32768 | tf_op jit(solution)/shard_map/all_to_all | solution.py:308
  128.0 0.6 chain.11
  128.6 10.7 %all_to_all.67.refs_1_ = f32[16,1,256]{2,1,0:T(1,128)S(1)} all-to-all(f32[16,1,256]{2,1,0:T(1,128)S(1)} %get-tuple-element.57), channel_id=1, replica_groups=mesh['book'=8,'path_0'=4,'path_1'=4] {'path_0','path_1'}, dimensions={0} | all-to-all | bytes 32768 | tf_op jit(solution)/shard_map/all_to_all | solution.py:308
  139.3 0.6 chain.12
  139.9 10.6 %all_to_all.68.refs_1_ = f32[16,1,256]{2,1,0:T(1,128)S(1)} all-to-all(f32[16,1,256]{2,1,0:T(1,128)S(1)} %get-tuple-element.61), channel_id=1, replica_groups=mesh['book'=8,'path_0'=4,'path_1'=4] {'path_0','path_1'}, dimensions={0} | all-to-all | bytes 32768 | tf_op jit(solution)/shard_map/all_to_all | solution.py:308
  150.5 0.6 chain.13
  151.2 10.6 %all_to_all.69.refs_1_ = f32[16,1,256]{2,1,0:T(1,128)S(1)} all-to-all(f32[16,1,256]{2,1,0:T(1,128)S(1)} %get-tuple-element.65), channel_id=1, replica_groups=mesh['book'=8,'path_0'=4,'path_1'=4] {'path_0','path_1'}, dimensions={0} | all-to-all | bytes 32768 | tf_op jit(solution)/shard_map/all_to_all | solution.py:308
  161.8 0.6 chain.14
  162.4 10.6 %all_to_all.70.refs_1_ = f32[16,1,256]{2,1,0:T(1,128)S(1)} all-to-all(f32[16,1,256]{2,1,0:T(1,128)S(1)} %get-tuple-element.69), channel_id=1, replica_groups=mesh['book'=8,'path_0'=4,'path_1'=4] {'path_0','path_1'}, dimensions={0} | all-to-all | bytes 32768 | tf_op jit(solution)/shard_map/all_to_all | solution.py:308
  173.1 0.6 chain.15
  173.7 10.6 %all_to_all.71.refs_1_ = f32[16,1,256]{2,1,0:T(1,128)S(1)} all-to-all(f32[16,1,256]{2,1,0:T(1,128)S(1)} %get-tuple-element.73), channel_id=1, replica_groups=mesh['book'=8,'path_0'=4,'path_1'=4] {'path_0','path_1'}, dimensions={0} | all-to-all | bytes 32768 | tf_op jit(solution)/shard_map/all_to_all | solution.py:308
  184.3 0.6 chain.16
  184.9 10.6 %all_to_all.72.refs_1_ = f32[16,1,256]{2,1,0:T(1,128)S(1)} all-to-all(f32[16,1,256]{2,1,0:T(1,128)S(1)} %get-tuple-element.77), channel_id=1, replica_groups=mesh['book'=8,'path_0'=4,'path_1'=4] {'path_0','path_1'}, dimensions={0} | all-to-all | bytes 32768 | tf_op jit(solution)/shard_map/all_to_all | solution.py:308
  195.6 0.6 chain.17
  196.2 10.6 %all_to_all.73.refs_1_ = f32[16,1,256]{2,1,0:T(1,128)S(1)} all-to-all(f32[16,1,256]{2,1,0:T(1,128)S(1)} %get-tuple-element.81), channel_id=1, replica_groups=mesh['book'=8,'path_0'=4,'path_1'=4] {'path_0','path_1'}, dimensions={0} | all-to-all | bytes 32768 | tf_op jit(solution)/shard_map/all_to_all | solution.py:308
  206.8 0.6 chain.18
  207.5 10.6 %all_to_all.74.refs_1_ = f32[16,1,256]{2,1,0:T(1,128)S(1)} all-to-all(f32[16,1,256]{2,1,0:T(1,128)S(1)} %get-tuple-element.85), channel_id=1, replica_groups=mesh['book'=8,'path_0'=4,'path_1'=4] {'path_0','path_1'}, dimensions={0} | all-to-all | bytes 32768 | tf_op jit(solution)/shard_map/all_to_all | solution.py:308
  218.1 0.9 chain.19
  219.0 3.5 %all-to-all-start.12 = ((f32[16,1,128]{2,1,0:T(1,128)}), f32[16,1,128]{2,1,0:T(1,128)S(1)}, u32[]{:S(2)}, u32[]{:S(2)}) async-start(f32[16,1,128]{2,1,0:T(1,128)} %get-tuple-element.89), calls=%async_computation.12 | async-start | bytes 16384 | tf_op jit(solution)/shard_map/all_to_all | solution.py:308
  223.1 6.8 %all-to-all-done.12 = f32[16,1,128]{2,1,0:T(1,128)S(1)} async-done(((f32[16,1,128]{2,1,0:T(1,128)}), f32[16,1,128]{2,1,0:T(1,128)S(1)}, u32[]{:S(2)}, u32[]{:S(2)}) %all-to-all-start.12) | async-done | bytes 8224 | tf_op jit(solution)/shard_map/all_to_all | solution.py:308
  (34 shorter events, 2.6 us)
Async XLA Ops:
  0.6 0.9 copy-start
  1.5 1.5 copy-start.2
  3.1 9.8 %copy-start.3 = (f32[10,20,2048]{2,1,0:T(8,128)S(1)}, f32[10,20,2048]{2,1,0:T(8,128)}, u32[]{:S(2)}) copy-start(f32[10,20,2048]{2,1,0:T(8,128)} %z_all_ref.1) | copy-start | bytes 4915204
  3.1 17.5 %copy-start.1 = (s32[10,2048]{1,0:T(8,128)S(1)}, s32[10,2048]{1,0:T(8,128)}, u32[]{:S(2)}) copy-start(s32[10,2048]{1,0:T(8,128)} %refs_4_.19) | copy-start | bytes 245764
  3.1 17.5 %copy-start.15 = (f32[2048]{0:T(1024)S(1)}, f32[2048]{0:T(1024)}, u32[]{:S(2)}) copy-start(f32[2048]{0:T(1024)} %param.7) | copy-start | bytes 24580
  4.3 16.3 %all-to-all-start = ((f32[16,20,128]{2,1,0:T(8,128)}), f32[16,20,128]{2,1,0:T(8,128)S(1)}, u32[]{:S(2)}, u32[]{:S(2)}) async-start(f32[16,20,128]{2,1,0:T(8,128)} %stats.1), calls=%async_computation | async-start | bytes 393216 | tf_op jit(solution)/shard_map/all_to_all | solution.py:308
  82.0 32.7 %all-to-all-start.2 = ((f32[16,128,256]{2,1,0:T(8,128)}), f32[16,128,256]{2,1,0:T(8,128)}, u32[]{:S(2)}, u32[]{:S(2)}) async-start(f32[16,128,256]{2,1,0:T(8,128)} %inverse.1), calls=%async_computation.2 | async-start | bytes 4194304 | tf_op jit(solution)/shard_map/all_to_all | solution.py:308
  86.4 30.1 %copy-start.14 = (s32[2048]{0:T(1024)S(1)}, s32[2048]{0:T(1024)}, u32[]{:S(2)}) copy-start(s32[2048]{0:T(1024)} %param.9) | copy-start | bytes 24580
  114.7 1.9 copy-start.12
  114.7 2.5 %copy-start.13 = (f32[240,2048]{1,0:T(8,128)S(1)}, f32[240,2048]{1,0:T(8,128)}, u32[]{:S(2)}) copy-start(f32[240,2048]{1,0:T(8,128)} %get-tuple-element.49.refs_2_) | copy-start | bytes 5898244
  117.2 10.8 %copy-start.11 = (f32[240,2048]{1,0:T(8,128)S(1)}, f32[240,2048]{1,0:T(8,128)}, u32[]{:S(2)}) copy-start(f32[240,2048]{1,0:T(8,128)} %get-tuple-element.55.refs_8_.refs_2_) | copy-start | bytes 5898244
  128.0 11.3 %copy-start.10 = (f32[240,2048]{1,0:T(8,128)S(1)}, f32[240,2048]{1,0:T(8,128)}, u32[]{:S(2)}) copy-start(f32[240,2048]{1,0:T(8,128)} %get-tuple-element.59.refs_8_.refs_2_) | copy-start | bytes 5898244
  139.3 11.3 %copy-start.9 = (f32[240,2048]{1,0:T(8,128)S(1)}, f32[240,2048]{1,0:T(8,128)}, u32[]{:S(2)}) copy-start(f32[240,2048]{1,0:T(8,128)} %get-tuple-element.63.refs_8_.refs_2_) | copy-start | bytes 5898244
  150.5 11.3 %copy-start.8 = (f32[240,2048]{1,0:T(8,128)S(1)}, f32[240,2048]{1,0:T(8,128)}, u32[]{:S(2)}) copy-start(f32[240,2048]{1,0:T(8,128)} %get-tuple-element.67.refs_8_.refs_2_) | copy-start | bytes 5898244
  161.8 11.3 %copy-start.7 = (f32[240,2048]{1,0:T(8,128)S(1)}, f32[240,2048]{1,0:T(8,128)}, u32[]{:S(2)}) copy-start(f32[240,2048]{1,0:T(8,128)} %get-tuple-element.71.refs_8_.refs_2_) | copy-start | bytes 5898244
  173.1 11.3 %copy-start.6 = (f32[240,2048]{1,0:T(8,128)S(1)}, f32[240,2048]{1,0:T(8,128)}, u32[]{:S(2)}) copy-start(f32[240,2048]{1,0:T(8,128)} %get-tuple-element.75.refs_8_.refs_2_) | copy-start | bytes 5898244
  184.3 11.3 %copy-start.5 = (f32[240,2048]{1,0:T(8,128)S(1)}, f32[240,2048]{1,0:T(8,128)}, u32[]{:S(2)}) copy-start(f32[240,2048]{1,0:T(8,128)} %get-tuple-element.79.refs_8_.refs_2_) | copy-start | bytes 5898244
  195.6 11.3 %copy-start.4 = (f32[240,2048]{1,0:T(8,128)S(1)}, f32[240,2048]{1,0:T(8,128)}, u32[]{:S(2)}) copy-start(f32[240,2048]{1,0:T(8,128)} %get-tuple-element.83.refs_8_.refs_2_) | copy-start | bytes 5898244
  219.0 10.9 %all-to-all-start.12 = ((f32[16,1,128]{2,1,0:T(1,128)}), f32[16,1,128]{2,1,0:T(1,128)S(1)}, u32[]{:S(2)}, u32[]{:S(2)}) async-start(f32[16,1,128]{2,1,0:T(1,128)} %get-tuple-element.89), calls=%async_computation.12 | async-start | bytes 16384 | tf_op jit(solution)/shard_map/all_to_all | solution.py:308

commit v3 on v2

--- a/solution.py
+++ b/solution.py
@@ -17,6 +17,8 @@
 TN = (((0,), (0,)), ((), ()))
 ROWS = 240
 HALF = 128
+REST = 104
+SLOT = 112
 BLOCK = 16
 CHUNK = 1024
 
@@ -74,119 +76,189 @@
 def rhs_row(phi_ref, weights):
     acc = jnp.zeros((ROWS, 128), f32)
     for c in range(0, weights.shape[1], 128):
-        acc = acc + phi_ref[:, c : c + 128] * weights[:, c : c + 128]
+        acc = acc + phi_ref[c // 128] * weights[:, c : c + 128]
     row = lax.dot_general(
         jnp.ones((8, 128), f32), acc, NT, precision=highest, preferred_element_type=f32
     )
     return jnp.concatenate([row, jnp.zeros((8, 256 - ROWS), f32)], axis=1)
 
 
-def gram_kernel(stats_ref, z_all_ref, m_ref, disc_ref, term_ref, *refs):
-    *phi_refs, slot_ref, v_ref, phi_two_ref, x_ref, gram_ref, rhs_ref, sems = refs
+def column(stats, i):
+    return jnp.sum(jnp.where(lanes_of(stats.shape) == i, stats, 0.0), axis=1, keepdims=True)
+
+
+def moments(stats_ref, d):
+    stats = stats_ref[0]
+    for i in range(1, stats_ref.shape[0]):
+        stats = stats + stats_ref[i]
+    count = column(stats, 3 * d + 2)
+    mean = column(stats, 3 * d) / count
+    return mean, 1.0 / jnp.sqrt(column(stats, 3 * d + 1) / count - mean * mean + 1e-05)
+
+
+def fill_basis(phi_ref, x_ref, z, m, mean, inverse):
+    factors = z.shape[0]
+    x_ref[0:factors, :] = (z - mean) * inverse * m
+    phi_ref[0:1, :] = m
+    phi_ref[1 : 1 + factors, :] = x_ref[0:factors, :]
+    offset = 1 + factors
+    for j in range(factors):
+        left = jnp.broadcast_to(x_ref[j : j + 1, :], (8, 128))
+        for k in range(0, factors - j, 8):
+            phi_ref[offset + k : offset + k + 8, :] = left * x_ref[j + k : j + k + 8, :]
+        offset += factors - j
+    phi_ref[offset : offset + 8, :] = jnp.zeros((8, 128), f32)
+    phi_ref[ROWS - 8 : ROWS, :] = jnp.zeros((8, 128), f32)
+
+
+def basis_kernel(stats_ref, z_ref, m_ref, *refs):
+    *phi_refs, phi_two_ref, x_ref, sems = refs
+    step = pl.program_id(0)
+    dates, paths = m_ref.shape
+    d = dates - 1 - step
+    side = step % 2
+
+    def copy_of(half, date):
+        return pltpu.make_async_copy(phi_two_ref.at[half], phi_refs[date], sems.at[half])
+
+    @pl.when(step >= 2)
+    def _():
+        copy_of(side, 0).wait()
+
+    mean, inverse = moments(stats_ref, d)
+    m = m_ref[pl.ds(d, 1), :].astype(f32)
+    for t in range(paths // 128):
+        at = slice(t * 128, (t + 1) * 128)
+        fill_basis(phi_two_ref.at[side, t], x_ref.at[t], z_ref[:, at], m[:, at], mean, inverse)
+    for date in range(dates):
+
+        @pl.when(d == date)
+        def _(date=date):
+            copy_of(side, date).start()
+
+    @pl.when(step == dates - 1)
+    def _():
+        for half in range(2):
+            copy_of(half, 0).wait()
+
+
+def gram_kernel(stats_ref, z_all_ref, m_ref, disc_ref, term_ref, slots_ref, v_ref, phi_ref, x_ref, gram_ref, rhs_ref):
     step = pl.program_id(0)
     dates, factors, paths = z_all_ref.shape
-    z_ref = z_all_ref.at[jnp.maximum(dates - 1 - step, 0)]
-    side = step % 2
-    phi_ref = phi_two_ref.at[side]
-
-    def copy_of(date):
-        return pltpu.make_async_copy(phi_ref, phi_refs[date], sems.at[side])
-
-    @pl.when((step >= 2) & (step < dates + 2))
+    d = dates - 1 - step
+
+    @pl.when(step == 0)
     def _():
-        copy_of(0).wait()
-
-    @pl.when(step < dates)
+        for t in range(phi_ref.shape[0]):
+            x_ref[t] = jnp.zeros((32, 128), f32)
+        v_ref[...] = term_ref[...] * disc_ref[dates - 1 : dates, :]
+
+    mean, inverse = moments(stats_ref, d)
+    gram_ref[...] = jnp.zeros_like(gram_ref)
+
+    def chunk(c, carry):
+        total = None
+        span = pl.ds(pl.multiple_of(c * CHUNK, CHUNK), CHUNK)
+        flags = m_ref[pl.ds(d, 1), span].astype(f32)
+        values = jnp.where(step == 0, v_ref[:, span], 0.0)
+        for pair in range(0, CHUNK // 128, 2):
+            hi, lo = [], []
+            for t in (pair, pair + 1):
+                at = pl.ds(pl.multiple_of(c * CHUNK + t * 128, 128), 128)
+                own = slice(t * 128, (t + 1) * 128)
+                fill_basis(phi_ref.at[t], x_ref.at[t], z_all_ref[d, :, at], flags[:, own], mean, inverse)
+                phi = phi_ref[t]
+                high = phi.astype(bf16)
+                low = (phi - high.astype(f32)).astype(bf16)
+                value = values[:, own]
+                one = value.astype(bf16).astype(f32)
+                two = (value - one).astype(bf16).astype(f32)
+                three = value - one - two
+                row = rows_of((256 - ROWS, 128))
+                under = jnp.where(row == 0, one, jnp.where(row == 1, two, jnp.where(row == 2, three, 0.0)))
+                hi.append(jnp.concatenate([high, under.astype(bf16)], axis=0))
+                lo.append(jnp.concatenate([low, jnp.zeros((256 - ROWS, 128), bf16)], axis=0))
+            hi = jnp.concatenate(hi, axis=1)
+            lo = jnp.concatenate(lo, axis=1)
+            both = lax.dot_general(
+                jnp.concatenate([hi, lo], axis=0), hi, NT, preferred_element_type=f32
+            )
+            part = both[0:256] + both[256:] + lax.dot_general(hi, lo, NT, preferred_element_type=f32)
+            total = part if total is None else total + part
+        gram_ref[...] += total
+        return carry
+
+    lax.fori_loop(0, paths // CHUNK, chunk, 0)
+    gram = gram_ref[...]
+    row, lane = rows_of((HALF, HALF)), lanes_of((HALF, HALF))
+    beside = jnp.where(lane < REST, gram[0:HALF, HALF:], 0.0)
+    under = jnp.where((row < REST) & (lane < REST), gram[HALF:, HALF:], 0.0)
+    rhs = jnp.where(step == 0, jnp.sum(gram[ROWS : ROWS + 3, :], axis=0, keepdims=True), rhs_ref[...])
+    rhs_ref[...] = rhs
+    packed = folded(gram[0:HALF, 0:HALF], beside, under, rhs)
+    slots_ref[d] = packed
+
+    @pl.when(step == 0)
     def _():
-        d = dates - 1 - step
-        stats = stats_ref[0]
-        for i in range(1, stats_ref.shape[0]):
-            stats = stats + stats_ref[i]
-        lane = lanes_of((factors, 128))
-
-        def column(i):
-            return jnp.sum(jnp.where(lane == i, stats, 0.0), axis=1, keepdims=True)
-
-        count = column(3 * d + 2)
-        mean = column(3 * d) / count
-        inverse = 1.0 / jnp.sqrt(column(3 * d + 1) / count - mean * mean + 1e-05)
-        gram_ref[...] = jnp.zeros_like(gram_ref)
-
-        def chunk(c, carry):
-            at = pl.ds(pl.multiple_of(c * CHUNK, CHUNK), CHUNK)
-            x_ref[...] = (z_ref[:, at] - mean) * inverse
-            phi_ref[0:1, at] = jnp.ones((1, CHUNK), f32)
-            phi_ref[1 : 1 + factors, at] = x_ref[...]
-            offset = 1 + factors
-            for j in range(factors):
-                phi_ref[offset : offset + factors - j, at] = x_ref[j : j + 1, :] * x_ref[j:factors, :]
-                offset += factors - j
-            phi_ref[offset:ROWS, at] = jnp.zeros((ROWS - offset, CHUNK), f32)
-            phi = phi_ref[:, at]
-            m = m_ref[pl.ds(d, 1), at].astype(f32)
-            pad = jnp.zeros((256 - ROWS, CHUNK), bf16)
-            hi = phi.astype(bf16)
-            rest = phi - hi.astype(f32)
-            lo = rest.astype(bf16)
-            him = jnp.concatenate([(phi * m).astype(bf16), pad], axis=0)
-            lom = jnp.concatenate([(rest * m).astype(bf16), pad], axis=0)
-            hi = jnp.concatenate([hi, pad], axis=0)
-            lo = jnp.concatenate([lo, pad], axis=0)
-            gram_ref[...] += (
-                lax.dot_general(him, hi, NT, preferred_element_type=f32)
-                + lax.dot_general(him, lo, NT, preferred_element_type=f32)
-                + lax.dot_general(lom, hi, NT, preferred_element_type=f32)
-            )
-            return carry
-
-        lax.fori_loop(0, paths // CHUNK, chunk, 0)
-        for date in range(dates):
-
-            @pl.when(d == date)
-            def _(date=date):
-                copy_of(date).start()
-
-        @pl.when(step == 0)
-        def _():
-            value = term_ref[...] * disc_ref[dates - 1 : dates, :]
-            v_ref[...] = value
-            rhs_ref[...] = rhs_row(phi_ref, value * m_ref[dates - 1 : dates, :].astype(f32))
-
-        gram = gram_ref[...]
-        slot_ref[0:HALF, :] = folded(gram[0:HALF, 0:HALF], gram[0:HALF, HALF:], gram[HALF:, HALF:])
-        slot_ref[HALF:, :] = rhs_ref[...]
-
-    @pl.when(step >= dates)
-    def _():
-        slot_ref[0:HALF, :] = jnp.zeros((HALF, 256), f32)
-        slot_ref[HALF:, :] = rhs_ref[...]
-
-
-def folded(first, beside, last):
+        for i in range(dates, slots_ref.shape[0]):
+            slots_ref[i] = packed
+
+
+def folded(first, beside, last, rhs=None):
     row, lane = rows_of((HALF, HALF)), lanes_of((HALF, HALF))
-    diagonal = jnp.sum(jnp.where(row == lane, last, 0.0), axis=0, keepdims=True)
     left = jnp.where(row <= lane, first, last)
-    left = jnp.where((row == HALF - 1) & (lane < HALF - 1), diagonal, left)
-    return jnp.concatenate([left, beside], axis=1)
+    low_lane = lanes_of((8, HALF))
+    low = left[REST:SLOT]
+    low = jnp.where(low_lane < 16, pltpu.roll(first[SLOT : SLOT + 8], 16, 1), low)
+    low = jnp.where((low_lane >= 16) & (low_lane < 32), pltpu.roll(first[SLOT + 8 :], 32, 1), low)
+    if rhs is not None:
+        low_row = rows_of((8, HALF))
+        for i in range(4):
+            piece = pltpu.roll(jnp.broadcast_to(rhs, (8, 256)), (32 - 72 * i) % 256, 1)[:, 0:HALF]
+            low = jnp.where((low_row == i) & (low_lane >= 32) & (low_lane < REST), piece, low)
+    left = jnp.concatenate([left[0:REST], low], axis=0)
+    diagonal = jnp.sum(jnp.where(row == lane, last, 0.0), axis=1, keepdims=True)
+    right = jnp.where(lane < REST, beside, pltpu.roll(beside.T, HALF - 8, 1))
+    right = jnp.where(lane == 120, diagonal, right)[0:SLOT]
+    return jnp.concatenate([left, right], axis=1)
 
 
 def unfolded(packed):
     row, lane = rows_of((HALF, HALF)), lanes_of((HALF, HALF))
-    left, beside = packed[:, 0:HALF], packed[:, HALF:]
+    none = jnp.zeros((HALF - SLOT, HALF), f32)
+    left = jnp.concatenate([packed[:, 0:HALF], none], axis=0)
+    right = jnp.concatenate([packed[:, HALF:], none], axis=0)
+    low = left[REST:SLOT]
+    corner = jnp.concatenate(
+        [left[0:SLOT], pltpu.roll(low, HALF - 16, 1), pltpu.roll(low, HALF - 32, 1)], axis=0
+    )
     turned = left.T
     first = jnp.where(row <= lane, left, turned)
-    diagonal = left[HALF - 1 : HALF, :]
+    first = jnp.where((row >= SLOT) & (lane >= SLOT), corner, first)
+    diagonal = jnp.sum(jnp.where(lane == 120, right, 0.0), axis=1, keepdims=True)
     last = jnp.where(row > lane, left, turned)
     last = jnp.where(row == lane, diagonal, last)
-    last = jnp.where((row < HALF - 1) & (lane < HALF - 1), last, 0.0)
+    last = jnp.where((row < REST) & (lane < REST), last, 0.0)
+    beside = jnp.where(row < SLOT, right, pltpu.roll(right, 8, 1).T)
+    beside = jnp.where(lane < REST, beside, 0.0)
     return first, beside, last
+
+
+def unfolded_row(low):
+    lane = lanes_of((1, 256))
+    wide = jnp.concatenate([low, jnp.zeros((8, HALF), f32)], axis=1)
+    total = jnp.zeros((1, 256), f32)
+    for i in range(4):
+        piece = pltpu.roll(wide, (72 * i - 32) % 256, 1)[i : i + 1]
+        total = jnp.where((lane >= 72 * i) & (lane < min(72 * i + 72, 231)), piece, total)
+    return total
 
 
 def inverse_kernel(parts_ref, out_ref, a_ref):
     basis = 231
-    packed = parts_ref[0, 0:HALF, :]
+    packed = parts_ref[0]
     for i in range(1, parts_ref.shape[0]):
-        packed = packed + parts_ref[i, 0:HALF, :]
+        packed = packed + parts_ref[i]
     first, beside, last = unfolded(packed)
     a_ref[0:HALF, 0:HALF] = first
     a_ref[0:HALF, HALF:] = beside
@@ -268,16 +340,18 @@
     else:
         coefs = refs[0][...]
         refs = refs[1:]
-    rhs = parts_ref[0, 0:1, :]
+    rhs = parts_ref[0]
     for i in range(1, parts_ref.shape[0]):
-        rhs = rhs + parts_ref[i, 0:1, :]
+        rhs = rhs + parts_ref[i]
+    if date == dates - 1:
+        rhs = unfolded_row(rhs)
     product = inv_ref[date] * rhs
     coef = jnp.sum(product[:, 0:128] + product[:, 128:], axis=1, keepdims=True)
     coef = jnp.broadcast_to(coef, (ROWS, 128))
     out_ref, coef_ref, send_ref = refs
     continuation = []
     for c in range(0, v_ref.shape[1], 128):
-        continuation.append(jnp.sum(coef * phi_ref[:, c : c + 128], axis=0, keepdims=True))
+        continuation.append(jnp.sum(coef * phi_ref[c // 128], axis=0, keepdims=True))
     continuation = jnp.concatenate(continuation, axis=1)
     exercise = ex_ref[date : date + 1, :]
     opened = jnp.where(index_ref[...] <= date, m_ref[date : date + 1, :].astype(f32), 0.0)
@@ -286,7 +360,7 @@
     value = value + weights * (exercise - value)
     if date:
         value = value * disc_ref[date - 1 : date, :]
-        row = rhs_row(next_ref, value * m_ref[date - 1 : date, :].astype(f32))
+        row = rhs_row(next_ref, value)
         for i in range(send_ref.shape[0]):
             send_ref[i] = row[0:1, :]
     else:
@@ -334,52 +408,62 @@
         name="swap",
     )(strike, states)
 
-    *phi, slots, value = pl.pallas_call(
+    tiles = paths // 128
+    slots, value = pl.pallas_call(
         gram_kernel,
-        grid=(size,),
-        in_specs=[WHOLE, WHOLE, WHOLE, WHOLE, WHOLE],
-        out_specs=[pl.BlockSpec(memory_space=pltpu.HBM)] * dates
-        + [
-            pl.BlockSpec((None, HALF + 8, 256), lambda i: (jnp.where(i < dates, jnp.maximum(dates - 1 - i, 0), i), 0, 0)),
-            WHOLE,
+        grid=(dates,),
+        in_specs=[WHOLE] * 5,
+        out_specs=[WHOLE] * 2,
+        out_shape=[vmem((size, SLOT, 256), f32), vmem((1, paths), f32)],
+        scratch_shapes=[
+            pltpu.VMEM((CHUNK // 128, ROWS, 128), f32),
+            pltpu.VMEM((CHUNK // 128, 32, 128), f32),
+            pltpu.VMEM((256, 256), f32),
+            pltpu.VMEM((1, 256), f32),
         ],
-        out_shape=[pltpu.HBM((ROWS, paths), f32)] * dates
-        + [
-            sds((size, HALF + 8, 256), f32),
-            vmem((1, paths), f32),
+        compiler_params=limit,
+        name="gram",
+    )(near(stats), near(states), near(itm_flags), near(discount), near(terminal))
+    phi = pl.pallas_call(
+        basis_kernel,
+        grid=(dates,),
+        in_specs=[
+            spec((size, factors, 128)),
+            pl.BlockSpec((None, factors, paths), lambda i: (dates - 1 - i, 0, 0)),
+            spec((dates, paths)),
         ],
+        out_specs=[pl.BlockSpec(memory_space=pltpu.HBM)] * dates,
+        out_shape=[pltpu.HBM((tiles, ROWS, 128), f32)] * dates,
         scratch_shapes=[
-            pltpu.VMEM((2, ROWS, paths), f32),
-            pltpu.VMEM((factors, CHUNK), f32),
-            pltpu.VMEM((256, 256), f32),
-            pltpu.VMEM((8, 256), f32),
+            pltpu.VMEM((2, tiles, ROWS, 128), f32),
+            pltpu.VMEM((tiles, 32, 128), f32),
             pltpu.SemaphoreType.DMA((2,)),
         ],
         compiler_params=limit,
-        name="gram",
-    )(near(stats), states, itm_flags, near(discount), terminal)
+        name="basis",
+    )(stats, states, itm_flags)
     slots = exchange(slots)
     inverse = pl.pallas_call(
         inverse_kernel,
         grid=(1,),
-        in_specs=[spec((size, HALF + 8, 256))],
-        out_specs=spec((size, HALF, 256)),
-        out_shape=pltpu.HBM((size, HALF, 256), f32),
+        in_specs=[WHOLE],
+        out_specs=spec((size, SLOT, 256)),
+        out_shape=pltpu.HBM((size, SLOT, 256), f32),
         scratch_shapes=[pltpu.VMEM((256, 256), f32)],
         compiler_params=limit,
         name="inverse",
-    )(slots)
+    )(near(slots))
     inverse = exchange(inverse)
     inverse = pl.pallas_call(
         unfold_kernel,
         grid=(1,),
-        in_specs=[spec((dates, HALF, 256))],
+        in_specs=[spec((dates, SLOT, 256))],
         out_specs=WHOLE,
         out_shape=vmem((dates, ROWS, 256), f32),
         compiler_params=limit,
         name="unfold",
     )(inverse)
-    received = slots[:, HALF : HALF + 1, :]
+    received = slots[:, REST:SLOT, 0:HALF]
     coefs = None
     for date in range(dates - 1, -1, -1):
         args = [inverse, received, phi[date], exercise, itm_flags, date_index, value, discount]

time: 233 us -> 222 us (0.953)
  waiting for transfers between devices: 41.9 us -> 28.7 us
  Pallas kernels: 39.6 us -> 44.6 us
  blocking collectives: 127 us -> 123 us
    all_to_all x3, waiting for transfers between devices: 41.9 us -> 28.7 us  [exchange(): return lax.all_to_all(slots, PATH, 0, 0, tiled=True)]
    pallas_call x3 -> x4, Pallas kernels: 31.1 us -> 36 us  [the longest x1 15.9 us: shards(): pl.pallas_call(gram_kernel, grid=(dates,), in_specs=[WHOLE] * 5, out_spec...]
    all_to_all x10, blocking collectives: 127 us -> 123 us  [exchange(): return lax.all_to_all(slots, PATH, 0, 0, tiled=True)]
  transfers between devices with their start and end apart: 3 -> 3, of which waited for: 3 -> 3; matrix products, arithmetic and copies ran while one was open for 0% -> 1% of each run, Pallas kernels for 0% -> 4%
where the time goes in v3:
time: 222 us; the launch traced here: 221 us
  blocking collectives  123 us (55%)
  Pallas kernels  44.6 us (20%)
  waiting for transfers between devices  28.7 us (13%)
  starting transfers between devices  15.9 us (7%)
  local copies, waits for them, and re-layouts  5.27 us (2%)
  between operations  3.17 us (1%)
    all_to_all x10, blocking collectives, exchange(): return lax.all_to_all(slots, PATH, 0, 0, tiled=True)  123 us
    all_to_all x3, waiting for transfers between devices, exchange(): return lax.all_to_all(slots, PATH, 0, 0, tiled=True)  28.7 us
    pallas_call x1, Pallas kernels, shards(): pl.pallas_call(gram_kernel, grid=(dates,), in_specs=[WHOLE] * 5, out_spec...  15.9 us
    all_to_all x3, starting transfers between devices, exchange(): return lax.all_to_all(slots, PATH, 0, 0, tiled=True)  15.9 us
    pallas_call x1, Pallas kernels, shards(): pl.pallas_call(basis_kernel, grid=(dates,), in_specs=[spec((size, factors...  8.71 us
    pallas_call x1, Pallas kernels, shards(): pl.pallas_call(inverse_kernel, grid=(1,), in_specs=[WHOLE], out_specs=spe...  8.63 us
    pallas_call x10, Pallas kernels, shards(): pl.pallas_call(kernel, in_specs=[WHOLE] * len(args), out_specs=[WHOLE] *...  6.74 us
  transfers between devices with their start and end apart: 3, of which 3 were waited for; matrix products, arithmetic and copies ran while one was open for 1% of the time, Pallas kernels for 4%

profile of v3, /device:TPU:0, one launch (start us, length us, event | category | flops | bytes accessed | tf_op | source)
XLA Modules:
  0.0 221.1 jit_solution(11417390180619109975)
XLA Ops:
  0.6 1.5 copy-done
  2.2 0.9 copy-done.2
  3.1 1.2 stats.1
  4.2 8.0 %all-to-all-start = ((f32[16,20,128]{2,1,0:T(8,128)}), f32[16,20,128]{2,1,0:T(8,128)S(1)}, u32[]{:S(2)}, u32[]{:S(2)}) async-start(f32[16,20,128]{2,1,0:T(8,128)} %stats.1), calls=%async_computation | async-start | bytes 393216 | tf_op jit(solution)/shard_map/all_to_all | solution.py:382
  12.9 0.8 swap.1
  13.7 6.9 %all-to-all-done.stats_ref = f32[16,20,128]{2,1,0:T(8,128)S(1)} async-done(((f32[16,20,128]{2,1,0:T(8,128)}), f32[16,20,128]{2,1,0:T(8,128)S(1)}, u32[]{:S(2)}, u32[]{:S(2)}) %all-to-all-start) | async-done | bytes 163872 | tf_op jit(solution)/shard_map/all_to_all | solution.py:382
  20.6 15.9 %gram.1 = (f32[16,112,256]{2,1,0:T(8,128)S(1)}, f32[1,2048]{1,0:T(1,128)S(1)}) custom-call(f32[16,20,128]{2,1,0:T(8,128)S(1)} %all-to-all-done.stats_ref, f32[10,20,2048]{2,1,0:T(8,128)S(1)} %copy-done.1, s32[10,2048]{1,0:T(8,128)S(1)} %copy-done.3, f32[10,2048]{1,0:T(8,128)S(1)} %get-tuple-element.47.disc_ref.refs_7_, f32[1,2048]{1,0:T(1,128)S(1)} %bitcast.14), custom_call_target="tpu_custom_call" | custom-call | tf_op jit(solution)/shard_map/gram/pallas_call | solution.py:412
  36.5 27.8 %all_to_all.65.parts_ref = f32[16,112,256]{2,1,0:T(8,128)S(1)} all-to-all(f32[16,112,256]{2,1,0:T(8,128)S(1)} %get-tuple-element.48), channel_id=1, replica_groups=mesh['book'=8,'path_0'=4,'path_1'=4] {'path_0','path_1'}, dimensions={0} | all-to-all | bytes 3670016 | tf_op jit(solution)/shard_map/all_to_all | solution.py:382
  64.3 8.6 %inverse.1 = f32[16,112,256]{2,1,0:T(8,128)} custom-call(f32[16,112,256]{2,1,0:T(8,128)S(1)} %all_to_all.65.parts_ref), custom_call_target="tpu_custom_call" | custom-call | tf_op jit(solution)/shard_map/inverse/pallas_call | solution.py:446
  72.9 1.3 copy-done.13
  74.2 4.4 %all-to-all-start.2 = ((f32[16,112,256]{2,1,0:T(8,128)}), f32[16,112,256]{2,1,0:T(8,128)}, u32[]{:S(2)}, u32[]{:S(2)}) async-start(f32[16,112,256]{2,1,0:T(8,128)} %inverse.1), calls=%async_computation.2 | async-start | bytes 3670016 | tf_op jit(solution)/shard_map/all_to_all | solution.py:382
  78.6 8.7 %basis.1 = (f32[16,240,128]{2,1,0:T(8,128)}, f32[16,240,128]{2,1,0:T(8,128)}, f32[16,240,128]{2,1,0:T(8,128)}, f32[16,240,128]{2,1,0:T(8,128)}, f32[16,240,128]{...) custom-call(f32[16,20,128]{2,1,0:T(8,128)S(1)} %all-to-all-done.stat, ...), custom_call_target="tpu_custom_call" | custom-call | tf_op jit(solution)/shard_map/basis/pallas_call | solution.py:427
  87.4 0.8 slice.12.refs_1_
  88.2 15.0 %all-to-all-done.2.packed_ref = f32[16,112,256]{2,1,0:T(8,128)} async-done(((f32[16,112,256]{2,1,0:T(8,128)}), f32[16,112,256]{2,1,0:T(8,128)}, u32[]{:S(2)}, u32[]{:S(2)}) %all-to-all-start.2) | async-done | bytes 1835040 | tf_op jit(solution)/shard_map/all_to_all | solution.py:382
  103.2 2.7 %unfold.1.refs_0_ = f32[10,240,256]{2,1,0:T(8,128)S(1)} custom-call(f32[16,112,256]{2,1,0:T(8,128)} %all-to-all-done.2.packed_ref), custom_call_target="tpu_custom_call" | custom-call | tf_op jit(solution)/shard_map/unfold/pallas_call | solution.py:457
  106.0 0.7 chain.10
  106.7 10.2 %all_to_all.66.refs_1_ = f32[16,1,256]{2,1,0:T(1,128)S(1)} all-to-all(f32[16,1,256]{2,1,0:T(1,128)S(1)} %get-tuple-element.53), channel_id=1, replica_groups=mesh['book'=8,'path_0'=4,'path_1'=4] {'path_0','path_1'}, dimensions={0} | all-to-all | bytes 32768 | tf_op jit(solution)/shard_map/all_to_all | solution.py:382
  117.5 10.6 %all_to_all.67.refs_1_ = f32[16,1,256]{2,1,0:T(1,128)S(1)} all-to-all(f32[16,1,256]{2,1,0:T(1,128)S(1)} %get-tuple-element.57), channel_id=1, replica_groups=mesh['book'=8,'path_0'=4,'path_1'=4] {'path_0','path_1'}, dimensions={0} | all-to-all | bytes 32768 | tf_op jit(solution)/shard_map/all_to_all | solution.py:382
  128.8 10.6 %all_to_all.68.refs_1_ = f32[16,1,256]{2,1,0:T(1,128)S(1)} all-to-all(f32[16,1,256]{2,1,0:T(1,128)S(1)} %get-tuple-element.61), channel_id=1, replica_groups=mesh['book'=8,'path_0'=4,'path_1'=4] {'path_0','path_1'}, dimensions={0} | all-to-all | bytes 32768 | tf_op jit(solution)/shard_map/all_to_all | solution.py:382
  140.0 10.6 %all_to_all.69.refs_1_ = f32[16,1,256]{2,1,0:T(1,128)S(1)} all-to-all(f32[16,1,256]{2,1,0:T(1,128)S(1)} %get-tuple-element.65), channel_id=1, replica_groups=mesh['book'=8,'path_0'=4,'path_1'=4] {'path_0','path_1'}, dimensions={0} | all-to-all | bytes 32768 | tf_op jit(solution)/shard_map/all_to_all | solution.py:382
  150.6 0.6 chain.14
  151.3 10.6 %all_to_all.70.refs_1_ = f32[16,1,256]{2,1,0:T(1,128)S(1)} all-to-all(f32[16,1,256]{2,1,0:T(1,128)S(1)} %get-tuple-element.69), channel_id=1, replica_groups=mesh['book'=8,'path_0'=4,'path_1'=4] {'path_0','path_1'}, dimensions={0} | all-to-all | bytes 32768 | tf_op jit(solution)/shard_map/all_to_all | solution.py:382
  161.9 0.6 chain.15
  162.5 10.6 %all_to_all.71.refs_1_ = f32[16,1,256]{2,1,0:T(1,128)S(1)} all-to-all(f32[16,1,256]{2,1,0:T(1,128)S(1)} %get-tuple-element.73), channel_id=1, replica_groups=mesh['book'=8,'path_0'=4,'path_1'=4] {'path_0','path_1'}, dimensions={0} | all-to-all | bytes 32768 | tf_op jit(solution)/shard_map/all_to_all | solution.py:382
  173.8 10.6 %all_to_all.72.refs_1_ = f32[16,1,256]{2,1,0:T(1,128)S(1)} all-to-all(f32[16,1,256]{2,1,0:T(1,128)S(1)} %get-tuple-element.77), channel_id=1, replica_groups=mesh['book'=8,'path_0'=4,'path_1'=4] {'path_0','path_1'}, dimensions={0} | all-to-all | bytes 32768 | tf_op jit(solution)/shard_map/all_to_all | solution.py:382
  184.4 0.6 chain.17
  185.0 10.6 %all_to_all.73.refs_1_ = f32[16,1,256]{2,1,0:T(1,128)S(1)} all-to-all(f32[16,1,256]{2,1,0:T(1,128)S(1)} %get-tuple-element.81), channel_id=1, replica_groups=mesh['book'=8,'path_0'=4,'path_1'=4] {'path_0','path_1'}, dimensions={0} | all-to-all | bytes 32768 | tf_op jit(solution)/shard_map/all_to_all | solution.py:382
  195.7 0.6 chain.18
  196.3 10.6 %all_to_all.74.refs_1_ = f32[16,1,256]{2,1,0:T(1,128)S(1)} all-to-all(f32[16,1,256]{2,1,0:T(1,128)S(1)} %get-tuple-element.85), channel_id=1, replica_groups=mesh['book'=8,'path_0'=4,'path_1'=4] {'path_0','path_1'}, dimensions={0} | all-to-all | bytes 32768 | tf_op jit(solution)/shard_map/all_to_all | solution.py:382
  206.9 0.9 chain.19
  207.9 3.5 %all-to-all-start.12 = ((f32[16,1,128]{2,1,0:T(1,128)}), f32[16,1,128]{2,1,0:T(1,128)S(1)}, u32[]{:S(2)}, u32[]{:S(2)}) async-start(f32[16,1,128]{2,1,0:T(1,128)} %get-tuple-element.89), calls=%async_computation.12 | async-start | bytes 16384 | tf_op jit(solution)/shard_map/all_to_all | solution.py:382
  212.0 6.8 %all-to-all-done.12 = f32[16,1,128]{2,1,0:T(1,128)S(1)} async-done(((f32[16,1,128]{2,1,0:T(1,128)}), f32[16,1,128]{2,1,0:T(1,128)S(1)}, u32[]{:S(2)}, u32[]{:S(2)}) %all-to-all-start.12) | async-done | bytes 8224 | tf_op jit(solution)/shard_map/all_to_all | solution.py:382
  (37 shorter events, 3.8 us)
Async XLA Ops:
  0.6 1.5 copy-start
  2.2 0.9 copy-start.2
  3.1 9.8 %copy-start.1 = (f32[10,20,2048]{2,1,0:T(8,128)S(1)}, f32[10,20,2048]{2,1,0:T(8,128)}, u32[]{:S(2)}) copy-start(f32[10,20,2048]{2,1,0:T(8,128)} %z_ref.5) | copy-start | bytes 4915204
  3.1 17.5 %copy-start.3 = (s32[10,2048]{1,0:T(8,128)S(1)}, s32[10,2048]{1,0:T(8,128)}, u32[]{:S(2)}) copy-start(s32[10,2048]{1,0:T(8,128)} %refs_4_.19) | copy-start | bytes 245764
  3.1 17.5 %copy-start.16 = (f32[2048]{0:T(1024)S(1)}, f32[2048]{0:T(1024)}, u32[]{:S(2)}) copy-start(f32[2048]{0:T(1024)} %param.7) | copy-start | bytes 24580
  4.2 16.3 %all-to-all-start = ((f32[16,20,128]{2,1,0:T(8,128)}), f32[16,20,128]{2,1,0:T(8,128)S(1)}, u32[]{:S(2)}, u32[]{:S(2)}) async-start(f32[16,20,128]{2,1,0:T(8,128)} %stats.1), calls=%async_computation | async-start | bytes 393216 | tf_op jit(solution)/shard_map/all_to_all | solution.py:382
  72.9 1.3 copy-start.13
  74.2 29.0 %all-to-all-start.2 = ((f32[16,112,256]{2,1,0:T(8,128)}), f32[16,112,256]{2,1,0:T(8,128)}, u32[]{:S(2)}, u32[]{:S(2)}) async-start(f32[16,112,256]{2,1,0:T(8,128)} %inverse.1), calls=%async_computation.2 | async-start | bytes 3670016 | tf_op jit(solution)/shard_map/all_to_all | solution.py:382
  88.2 17.7 %copy-start.12 = (f32[16,240,128]{2,1,0:T(8,128)S(1)}, f32[16,240,128]{2,1,0:T(8,128)}, u32[]{:S(2)}) copy-start(f32[16,240,128]{2,1,0:T(8,128)} %get-tuple-element.52.refs_8_.refs_2_) | copy-start | bytes 5898244
  88.2 17.7 %copy-start.15 = (s32[2048]{0:T(1024)S(1)}, s32[2048]{0:T(1024)}, u32[]{:S(2)}) copy-start(s32[2048]{0:T(1024)} %param.9) | copy-start | bytes 24580
  103.2 2.7 %copy-start.14 = (f32[16,240,128]{2,1,0:T(8,128)S(1)}, f32[16,240,128]{2,1,0:T(8,128)}, u32[]{:S(2)}) copy-start(f32[16,240,128]{2,1,0:T(8,128)} %get-tuple-element.49.refs_2_) | copy-start | bytes 5898244
  106.0 10.9 %copy-start.11 = (f32[16,240,128]{2,1,0:T(8,128)S(1)}, f32[16,240,128]{2,1,0:T(8,128)}, u32[]{:S(2)}) copy-start(f32[16,240,128]{2,1,0:T(8,128)} %get-tuple-element.55.refs_8_.refs_2_) | copy-start | bytes 5898244
  116.8 11.3 %copy-start.10 = (f32[16,240,128]{2,1,0:T(8,128)S(1)}, f32[16,240,128]{2,1,0:T(8,128)}, u32[]{:S(2)}) copy-start(f32[16,240,128]{2,1,0:T(8,128)} %get-tuple-element.59.refs_8_.refs_2_) | copy-start | bytes 5898244
  128.1 11.3 %copy-start.9 = (f32[16,240,128]{2,1,0:T(8,128)S(1)}, f32[16,240,128]{2,1,0:T(8,128)}, u32[]{:S(2)}) copy-start(f32[16,240,128]{2,1,0:T(8,128)} %get-tuple-element.63.refs_8_.refs_2_) | copy-start | bytes 5898244
  139.4 11.3 %copy-start.8 = (f32[16,240,128]{2,1,0:T(8,128)S(1)}, f32[16,240,128]{2,1,0:T(8,128)}, u32[]{:S(2)}) copy-start(f32[16,240,128]{2,1,0:T(8,128)} %get-tuple-element.67.refs_8_.refs_2_) | copy-start | bytes 5898244
  150.6 11.3 %copy-start.7 = (f32[16,240,128]{2,1,0:T(8,128)S(1)}, f32[16,240,128]{2,1,0:T(8,128)}, u32[]{:S(2)}) copy-start(f32[16,240,128]{2,1,0:T(8,128)} %get-tuple-element.71.refs_8_.refs_2_) | copy-start | bytes 5898244
  161.9 11.3 %copy-start.6 = (f32[16,240,128]{2,1,0:T(8,128)S(1)}, f32[16,240,128]{2,1,0:T(8,128)}, u32[]{:S(2)}) copy-start(f32[16,240,128]{2,1,0:T(8,128)} %get-tuple-element.75.refs_8_.refs_2_) | copy-start | bytes 5898244
  173.1 11.3 %copy-start.5 = (f32[16,240,128]{2,1,0:T(8,128)S(1)}, f32[16,240,128]{2,1,0:T(8,128)}, u32[]{:S(2)}) copy-start(f32[16,240,128]{2,1,0:T(8,128)} %get-tuple-element.79.refs_8_.refs_2_) | copy-start | bytes 5898244
  184.4 11.3 %copy-start.4 = (f32[16,240,128]{2,1,0:T(8,128)S(1)}, f32[16,240,128]{2,1,0:T(8,128)}, u32[]{:S(2)}) copy-start(f32[16,240,128]{2,1,0:T(8,128)} %get-tuple-element.83.refs_8_.refs_2_) | copy-start | bytes 5898244
  207.9 10.9 %all-to-all-start.12 = ((f32[16,1,128]{2,1,0:T(1,128)}), f32[16,1,128]{2,1,0:T(1,128)S(1)}, u32[]{:S(2)}, u32[]{:S(2)}) async-start(f32[16,1,128]{2,1,0:T(1,128)} %get-tuple-element.89), calls=%async_computation.12 | async-start | bytes 16384 | tf_op jit(solution)/shard_map/all_to_all | solution.py:382

commit v4 on v3

--- a/solution.py
+++ b/solution.py
@@ -20,7 +20,6 @@
 REST = 104
 SLOT = 112
 BLOCK = 16
-CHUNK = 1024
 
 
 def spec(shape, index=None):
@@ -44,19 +43,28 @@
     return lax.broadcasted_iota(jnp.int32, shape, 0)
 
 
-def stats_kernel(z_ref, m_ref, out_ref):
+def stats_kernel(z_ref, m_ref, out_ref, sum_ref):
+    step = pl.program_id(0)
     dates, factors, _ = z_ref.shape
     lane = lanes_of((factors, 128))
-    packed = jnp.zeros((factors, 128), f32)
-    for d in range(dates):
-        z = z_ref[d]
-        m = m_ref[d : d + 1, :].astype(f32)
+
+    @pl.when(step == 0)
+    def _():
+        sum_ref[...] = jnp.zeros_like(sum_ref)
+
+    packed = sum_ref[0:factors, :]
+    for i in range(dates):
+        d = step * dates + i
+        z = z_ref[i]
+        m = m_ref[pl.ds(d, 1), :].astype(f32)
         mz = z * m
         packed = jnp.where(lane == 3 * d, jnp.sum(mz, axis=1, keepdims=True), packed)
         packed = jnp.where(lane == 3 * d + 1, jnp.sum(mz * z, axis=1, keepdims=True), packed)
         packed = jnp.where(lane == 3 * d + 2, jnp.sum(m, axis=1, keepdims=True), packed)
+    sum_ref[0:factors, :] = packed
+    groups = sum_ref[0:8] + pltpu.roll(sum_ref[8:16], 32, 1) + pltpu.roll(sum_ref[16:24], 64, 1)
     for i in range(out_ref.shape[0]):
-        out_ref[i] = packed
+        out_ref[i] = groups
 
 
 def swap_kernel(strike_ref, z_ref, ex_ref, disc_ref, fac_ref):
@@ -87,10 +95,11 @@
     return jnp.sum(jnp.where(lanes_of(stats.shape) == i, stats, 0.0), axis=1, keepdims=True)
 
 
-def moments(stats_ref, d):
+def moments(stats_ref, d, factors):
     stats = stats_ref[0]
     for i in range(1, stats_ref.shape[0]):
         stats = stats + stats_ref[i]
+    stats = jnp.concatenate([stats, pltpu.roll(stats, 96, 1), pltpu.roll(stats, 64, 1)], axis=0)[0:factors]
     count = column(stats, 3 * d + 2)
     mean = column(stats, 3 * d) / count
     return mean, 1.0 / jnp.sqrt(column(stats, 3 * d + 1) / count - mean * mean + 1e-05)
@@ -125,7 +134,7 @@
     def _():
         copy_of(side, 0).wait()
 
-    mean, inverse = moments(stats_ref, d)
+    mean, inverse = moments(stats_ref, d, z_ref.shape[0])
     m = m_ref[pl.ds(d, 1), :].astype(f32)
     for t in range(paths // 128):
         at = slice(t * 128, (t + 1) * 128)
@@ -142,66 +151,71 @@
             copy_of(half, 0).wait()
 
 
-def gram_kernel(stats_ref, z_all_ref, m_ref, disc_ref, term_ref, slots_ref, v_ref, phi_ref, x_ref, gram_ref, rhs_ref):
+def gram_kernel(stats_ref, z_all_ref, m_ref, disc_ref, term_ref, slots_ref, v_ref, *scratch):
+    phi_ref, x_ref, gram_ref, rhs_ref, mean_ref, inverse_ref = scratch
     step = pl.program_id(0)
     dates, factors, paths = z_all_ref.shape
     d = dates - 1 - step
 
     @pl.when(step == 0)
     def _():
-        for t in range(phi_ref.shape[0]):
-            x_ref[t] = jnp.zeros((32, 128), f32)
+        x_ref[...] = jnp.zeros_like(x_ref)
+        gram_ref[...] = jnp.zeros_like(gram_ref)
         v_ref[...] = term_ref[...] * disc_ref[dates - 1 : dates, :]
-
-    mean, inverse = moments(stats_ref, d)
-    gram_ref[...] = jnp.zeros_like(gram_ref)
-
-    def chunk(c, carry):
-        total = None
-        span = pl.ds(pl.multiple_of(c * CHUNK, CHUNK), CHUNK)
-        flags = m_ref[pl.ds(d, 1), span].astype(f32)
-        values = jnp.where(step == 0, v_ref[:, span], 0.0)
-        for pair in range(0, CHUNK // 128, 2):
-            hi, lo = [], []
-            for t in (pair, pair + 1):
-                at = pl.ds(pl.multiple_of(c * CHUNK + t * 128, 128), 128)
-                own = slice(t * 128, (t + 1) * 128)
-                fill_basis(phi_ref.at[t], x_ref.at[t], z_all_ref[d, :, at], flags[:, own], mean, inverse)
-                phi = phi_ref[t]
-                high = phi.astype(bf16)
-                low = (phi - high.astype(f32)).astype(bf16)
-                value = values[:, own]
-                one = value.astype(bf16).astype(f32)
-                two = (value - one).astype(bf16).astype(f32)
-                three = value - one - two
-                row = rows_of((256 - ROWS, 128))
-                under = jnp.where(row == 0, one, jnp.where(row == 1, two, jnp.where(row == 2, three, 0.0)))
-                hi.append(jnp.concatenate([high, under.astype(bf16)], axis=0))
-                lo.append(jnp.concatenate([low, jnp.zeros((256 - ROWS, 128), bf16)], axis=0))
-            hi = jnp.concatenate(hi, axis=1)
-            lo = jnp.concatenate(lo, axis=1)
-            both = lax.dot_general(
-                jnp.concatenate([hi, lo], axis=0), hi, NT, preferred_element_type=f32
-            )
-            part = both[0:256] + both[256:] + lax.dot_general(hi, lo, NT, preferred_element_type=f32)
-            total = part if total is None else total + part
-        gram_ref[...] += total
-        return carry
-
-    lax.fori_loop(0, paths // CHUNK, chunk, 0)
-    gram = gram_ref[...]
-    row, lane = rows_of((HALF, HALF)), lanes_of((HALF, HALF))
-    beside = jnp.where(lane < REST, gram[0:HALF, HALF:], 0.0)
-    under = jnp.where((row < REST) & (lane < REST), gram[HALF:, HALF:], 0.0)
-    rhs = jnp.where(step == 0, jnp.sum(gram[ROWS : ROWS + 3, :], axis=0, keepdims=True), rhs_ref[...])
-    rhs_ref[...] = rhs
-    packed = folded(gram[0:HALF, 0:HALF], beside, under, rhs)
-    slots_ref[d] = packed
-
-    @pl.when(step == 0)
+        for date in range(dates):
+            mean, inverse = moments(stats_ref, date, factors)
+            mean_ref[date] = jnp.broadcast_to(mean, (factors, 128))
+            inverse_ref[date] = jnp.broadcast_to(inverse, (factors, 128))
+
+    def fold(gram, date, first):
+        row, lane = rows_of((HALF, HALF)), lanes_of((HALF, HALF))
+        beside = jnp.where(lane < REST, gram[0:HALF, HALF:], 0.0)
+        under = jnp.where((row < REST) & (lane < REST), gram[HALF:, HALF:], 0.0)
+        rhs = jnp.sum(gram[ROWS : ROWS + 3, :], axis=0, keepdims=True)
+        rhs = jnp.where(first, rhs, rhs_ref[...])
+        rhs_ref[...] = rhs
+        packed = folded(gram[0:HALF, 0:HALF], beside, under, rhs)
+        slots_ref[date] = packed
+        return packed
+
+    packed = fold(gram_ref[...], d + 1, step == 1)
+    flags = m_ref[pl.ds(d, 1), :].astype(f32)
+    values = jnp.where(step == 0, v_ref[...], 0.0)
+    mean, inverse = mean_ref[d], inverse_ref[d]
+    total = None
+    for pair in range(0, paths // 128, 2):
+        hi, lo = [], []
+        for t in (pair, pair + 1):
+            at = slice(t * 128, (t + 1) * 128)
+            fill_basis(phi_ref.at[t], x_ref.at[t], z_all_ref[d, :, at], flags[:, at], mean, inverse)
+            phi = phi_ref[t]
+            high = phi.astype(bf16)
+            low = (phi - high.astype(f32)).astype(bf16)
+            value = values[:, at]
+            one = value.astype(bf16).astype(f32)
+            two = (value - one).astype(bf16).astype(f32)
+            three = value - one - two
+            row = rows_of((256 - ROWS, 128))
+            under = jnp.where(row == 0, one, jnp.where(row == 1, two, jnp.where(row == 2, three, 0.0)))
+            hi.append(jnp.concatenate([high, under.astype(bf16)], axis=0))
+            lo.append(jnp.concatenate([low, jnp.zeros((256 - ROWS, 128), bf16)], axis=0))
+        hi = jnp.concatenate(hi, axis=1)
+        lo = jnp.concatenate(lo, axis=1)
+        both = lax.dot_general(
+            jnp.concatenate([hi, lo], axis=0), hi, NT, preferred_element_type=f32
+        )
+        part = both[0:256] + both[256:] + lax.dot_general(hi, lo, NT, preferred_element_type=f32)
+        total = part if total is None else total + part
+    gram_ref[...] = total
+
+    @pl.when(step == 1)
     def _():
         for i in range(dates, slots_ref.shape[0]):
             slots_ref[i] = packed
+
+    @pl.when(step == dates - 1)
+    def _():
+        fold(gram_ref[...], 0, False)
 
 
 def folded(first, beside, last, rhs=None):
@@ -254,11 +268,12 @@
     return total
 
 
-def inverse_kernel(parts_ref, out_ref, a_ref):
+def inverse_kernel(parts_ref, out_ref, rhs_ref, a_ref):
     basis = 231
     packed = parts_ref[0]
     for i in range(1, parts_ref.shape[0]):
         packed = packed + parts_ref[i]
+    rhs_ref[0] = unfolded_row(packed[REST:SLOT, 0:HALF])
     first, beside, last = unfolded(packed)
     a_ref[0:HALF, 0:HALF] = first
     a_ref[0:HALF, HALF:] = beside
@@ -343,8 +358,6 @@
     rhs = parts_ref[0]
     for i in range(1, parts_ref.shape[0]):
         rhs = rhs + parts_ref[i]
-    if date == dates - 1:
-        rhs = unfolded_row(rhs)
     product = inv_ref[date] * rhs
     coef = jnp.sum(product[:, 0:128] + product[:, 128:], axis=1, keepdims=True)
     coef = jnp.broadcast_to(coef, (ROWS, 128))
@@ -392,11 +405,17 @@
     limit = pltpu.CompilerParams(vmem_limit_bytes=24 << 20)
     stats = pl.pallas_call(
         stats_kernel,
-        out_shape=vmem((size, factors, 128), f32),
+        grid=(2,),
+        in_specs=[
+            pl.BlockSpec((dates // 2, factors, paths), lambda i: (i, 0, 0)),
+            spec((dates, paths)),
+        ],
+        out_shape=vmem((size, 8, 128), f32),
         out_specs=WHOLE,
+        scratch_shapes=[pltpu.VMEM((24, 128), f32)],
         compiler_params=limit,
         name="stats",
-    )(states, itm_flags)
+    )(pltpu.with_memory_space_constraint(states, pltpu.HBM), pltpu.with_memory_space_constraint(itm_flags, pltpu.HBM))
     stats = exchange(stats)
     exercise, discount = pl.pallas_call(
         swap_kernel,
@@ -416,10 +435,12 @@
         out_specs=[WHOLE] * 2,
         out_shape=[vmem((size, SLOT, 256), f32), vmem((1, paths), f32)],
         scratch_shapes=[
-            pltpu.VMEM((CHUNK // 128, ROWS, 128), f32),
-            pltpu.VMEM((CHUNK // 128, 32, 128), f32),
+            pltpu.VMEM((tiles, ROWS, 128), f32),
+            pltpu.VMEM((tiles, 32, 128), f32),
             pltpu.VMEM((256, 256), f32),
             pltpu.VMEM((1, 256), f32),
+            pltpu.VMEM((dates, factors, 128), f32),
+            pltpu.VMEM((dates, factors, 128), f32),
         ],
         compiler_params=limit,
         name="gram",
@@ -428,7 +449,7 @@
         basis_kernel,
         grid=(dates,),
         in_specs=[
-            spec((size, factors, 128)),
+            spec((size, 8, 128)),
             pl.BlockSpec((None, factors, paths), lambda i: (dates - 1 - i, 0, 0)),
             spec((dates, paths)),
         ],
@@ -443,12 +464,12 @@
         name="basis",
     )(stats, states, itm_flags)
     slots = exchange(slots)
-    inverse = pl.pallas_call(
+    inverse, received = pl.pallas_call(
         inverse_kernel,
         grid=(1,),
         in_specs=[WHOLE],
-        out_specs=spec((size, SLOT, 256)),
-        out_shape=pltpu.HBM((size, SLOT, 256), f32),
+        out_specs=[spec((size, SLOT, 256)), WHOLE],
+        out_shape=[pltpu.HBM((size, SLOT, 256), f32), vmem((1, 1, 256), f32)],
         scratch_shapes=[pltpu.VMEM((256, 256), f32)],
         compiler_params=limit,
         name="inverse",
@@ -463,7 +484,6 @@
         compiler_params=limit,
         name="unfold",
     )(inverse)
-    received = slots[:, REST:SLOT, 0:HALF]
     coefs = None
     for date in range(dates - 1, -1, -1):
         args = [inverse, received, phi[date], exercise, itm_flags, date_index, value, discount]

time: 222 us -> 215 us (0.968)
  local copies, waits for them, and re-layouts: 5.27 us -> 0.66 us
  Pallas kernels: 44.6 us -> 42.2 us
    pallas_call x1, Pallas kernels: 15.9 us -> 11.7 us  [shards(): pl.pallas_call(gram_kernel, grid=(dates,), in_specs=[WHOLE] * 5, out_spec...]
    unnamed x34 -> x28, local copies, waits for them, and re-layouts: 3.81 us -> 0.06 us
  transfers between devices with their start and end apart: 3 -> 3, of which waited for: 3 -> 3; matrix products, arithmetic and copies ran while one was open for 1% -> 0% of each run, Pallas kernels for 4% -> 5%
where the time goes in v4:
time: 215 us; the launch traced here: 214 us
  blocking collectives  123 us (57%)
  Pallas kernels  42.2 us (20%)
  waiting for transfers between devices  28.5 us (13%)
  starting transfers between devices  15.9 us (7%)
  between operations  3.2 us (1%)
    all_to_all x10, blocking collectives, exchange(): return lax.all_to_all(slots, PATH, 0, 0, tiled=True)  123 us
    all_to_all x3, waiting for transfers between devices, exchange(): return lax.all_to_all(slots, PATH, 0, 0, tiled=True)  28.5 us
    all_to_all x3, starting transfers between devices, exchange(): return lax.all_to_all(slots, PATH, 0, 0, tiled=True)  15.9 us
    pallas_call x1, Pallas kernels, shards(): pl.pallas_call(gram_kernel, grid=(dates,), in_specs=[WHOLE] * 5, out_spec...  11.7 us
    pallas_call x1, Pallas kernels, shards(): pl.pallas_call(basis_kernel, grid=(dates,), in_specs=[spec((size, 8, 128)...  9.08 us
    pallas_call x1, Pallas kernels, shards(): pl.pallas_call(inverse_kernel, grid=(1,), in_specs=[WHOLE], out_specs=[sp...  8.61 us
    pallas_call x10, Pallas kernels, shards(): pl.pallas_call(kernel, in_specs=[WHOLE] * len(args), out_specs=[WHOLE] *...  6.66 us
  transfers between devices with their start and end apart: 3, of which 3 were waited for; matrix products, arithmetic and copies ran while one was open for 0% of the time, Pallas kernels for 5%

profile of v4, /device:TPU:0, one launch (start us, length us, event | category | flops | bytes accessed | tf_op | source)
XLA Modules:
  0.0 214.0 jit_solution(2277474421201502759)
XLA Ops:
  0.7 2.6 %stats.1 = f32[16,8,128]{2,1,0:T(8,128)} custom-call(f32[10,20,2048]{2,1,0:T(8,128)} %z_ref.5, s32[10,2048]{1,0:T(8,128)} %refs_4_.19), custom_call_target="tpu_custom_call" | custom-call | tf_op jit(solution)/shard_map/stats/pallas_call | solution.py:406
  3.3 8.0 %all-to-all-start = ((f32[16,8,128]{2,1,0:T(8,128)}), f32[16,8,128]{2,1,0:T(8,128)S(1)}, u32[]{:S(2)}, u32[]{:S(2)}) async-start(f32[16,8,128]{2,1,0:T(8,128)} %stats.1), calls=%async_computation | async-start | bytes 131072 | tf_op jit(solution)/shard_map/all_to_all | solution.py:395
  11.9 0.8 swap.1
  12.7 6.2 %all-to-all-done.stats_ref = f32[16,8,128]{2,1,0:T(8,128)S(1)} async-done(((f32[16,8,128]{2,1,0:T(8,128)}), f32[16,8,128]{2,1,0:T(8,128)S(1)}, u32[]{:S(2)}, u32[]{:S(2)}) %all-to-all-start) | async-done | bytes 65568 | tf_op jit(solution)/shard_map/all_to_all | solution.py:395
  19.0 11.7 %gram.1 = (f32[16,112,256]{2,1,0:T(8,128)S(1)}, f32[1,2048]{1,0:T(1,128)S(1)}) custom-call(f32[16,8,128]{2,1,0:T(8,128)S(1)} %all-to-all-done.stats_ref, f32[10,20,2048]{2,1,0:T(8,128)S(1)} %copy-done, s32[10,2048]{1,0:T(8,128)S(1)} %copy-done.1, f32[10,2048]{1,0:T(8,128)S(1)} %get-tuple-element.49.disc_ref.refs_7_, f32[1,2048]{1,0:T(1,128)S(1)} %bitcast.14), custom_call_target="tpu_custom_call" | custom-call | tf_op jit(solution)/shard_map/gram/pallas_call | solution.py:431
  30.7 27.9 %all_to_all.65.parts_ref = f32[16,112,256]{2,1,0:T(8,128)S(1)} all-to-all(f32[16,112,256]{2,1,0:T(8,128)S(1)} %get-tuple-element.50), channel_id=1, replica_groups=mesh['book'=8,'path_0'=4,'path_1'=4] {'path_0','path_1'}, dimensions={0} | all-to-all | bytes 3670016 | tf_op jit(solution)/shard_map/all_to_all | solution.py:395
  58.6 8.6 %inverse.1 = (f32[16,112,256]{2,1,0:T(8,128)}, f32[1,1,256]{2,1,0:T(1,128)S(1)}) custom-call(f32[16,112,256]{2,1,0:T(8,128)S(1)} %all_to_all.65.parts_ref), custom_call_target="tpu_custom_call" | custom-call | tf_op jit(solution)/shard_map/inverse/pallas_call | solution.py:467
  67.2 4.4 %all-to-all-start.2 = ((f32[16,112,256]{2,1,0:T(8,128)}), f32[16,112,256]{2,1,0:T(8,128)}, u32[]{:S(2)}, u32[]{:S(2)}) async-start(f32[16,112,256]{2,1,0:T(8,128)} %get-tuple-element.51), calls=%async_computation.2 | async-start | bytes 3670016 | tf_op jit(solution)/shard_map/all_to_all | solution.py:395
  71.6 9.1 %basis.1 = (f32[16,240,128]{2,1,0:T(8,128)}, f32[16,240,128]{2,1,0:T(8,128)}, f32[16,240,128]{2,1,0:T(8,128)}, f32[16,240,128]{2,1,0:T(8,128)}, f32[16,240,128]{...) custom-call(f32[16,8,128]{2,1,0:T(8,128)S(1)} %all-to-all-done.stats, ...), custom_call_target="tpu_custom_call" | custom-call | tf_op jit(solution)/shard_map/basis/pallas_call | solution.py:448
  80.8 15.5 %all-to-all-done.2.packed_ref = f32[16,112,256]{2,1,0:T(8,128)} async-done(((f32[16,112,256]{2,1,0:T(8,128)}), f32[16,112,256]{2,1,0:T(8,128)}, u32[]{:S(2)}, u32[]{:S(2)}) %all-to-all-start.2) | async-done | bytes 1835040 | tf_op jit(solution)/shard_map/all_to_all | solution.py:395
  96.2 2.7 %unfold.1.refs_0_ = f32[10,240,256]{2,1,0:T(8,128)S(1)} custom-call(f32[16,112,256]{2,1,0:T(8,128)} %all-to-all-done.2.packed_ref), custom_call_target="tpu_custom_call" | custom-call | tf_op jit(solution)/shard_map/unfold/pallas_call | solution.py:478
  99.0 0.6 chain.10
  99.6 10.1 %all_to_all.66.refs_1_ = f32[16,1,256]{2,1,0:T(1,128)S(1)} all-to-all(f32[16,1,256]{2,1,0:T(1,128)S(1)} %get-tuple-element.57), channel_id=1, replica_groups=mesh['book'=8,'path_0'=4,'path_1'=4] {'path_0','path_1'}, dimensions={0} | all-to-all | bytes 32768 | tf_op jit(solution)/shard_map/all_to_all | solution.py:395
  109.8 0.6 chain.11
  110.4 10.6 %all_to_all.67.refs_1_ = f32[16,1,256]{2,1,0:T(1,128)S(1)} all-to-all(f32[16,1,256]{2,1,0:T(1,128)S(1)} %get-tuple-element.61), channel_id=1, replica_groups=mesh['book'=8,'path_0'=4,'path_1'=4] {'path_0','path_1'}, dimensions={0} | all-to-all | bytes 32768 | tf_op jit(solution)/shard_map/all_to_all | solution.py:395
  121.0 0.6 chain.12
  121.7 10.6 %all_to_all.68.refs_1_ = f32[16,1,256]{2,1,0:T(1,128)S(1)} all-to-all(f32[16,1,256]{2,1,0:T(1,128)S(1)} %get-tuple-element.65), channel_id=1, replica_groups=mesh['book'=8,'path_0'=4,'path_1'=4] {'path_0','path_1'}, dimensions={0} | all-to-all | bytes 32768 | tf_op jit(solution)/shard_map/all_to_all | solution.py:395
  132.3 0.6 chain.13
  132.9 10.6 %all_to_all.69.refs_1_ = f32[16,1,256]{2,1,0:T(1,128)S(1)} all-to-all(f32[16,1,256]{2,1,0:T(1,128)S(1)} %get-tuple-element.69), channel_id=1, replica_groups=mesh['book'=8,'path_0'=4,'path_1'=4] {'path_0','path_1'}, dimensions={0} | all-to-all | bytes 32768 | tf_op jit(solution)/shard_map/all_to_all | solution.py:395
  143.6 0.6 chain.14
  144.2 10.6 %all_to_all.70.refs_1_ = f32[16,1,256]{2,1,0:T(1,128)S(1)} all-to-all(f32[16,1,256]{2,1,0:T(1,128)S(1)} %get-tuple-element.73), channel_id=1, replica_groups=mesh['book'=8,'path_0'=4,'path_1'=4] {'path_0','path_1'}, dimensions={0} | all-to-all | bytes 32768 | tf_op jit(solution)/shard_map/all_to_all | solution.py:395
  154.8 0.6 chain.15
  155.5 10.6 %all_to_all.71.refs_1_ = f32[16,1,256]{2,1,0:T(1,128)S(1)} all-to-all(f32[16,1,256]{2,1,0:T(1,128)S(1)} %get-tuple-element.77), channel_id=1, replica_groups=mesh['book'=8,'path_0'=4,'path_1'=4] {'path_0','path_1'}, dimensions={0} | all-to-all | bytes 32768 | tf_op jit(solution)/shard_map/all_to_all | solution.py:395
  166.1 0.6 chain.16
  166.7 10.6 %all_to_all.72.refs_1_ = f32[16,1,256]{2,1,0:T(1,128)S(1)} all-to-all(f32[16,1,256]{2,1,0:T(1,128)S(1)} %get-tuple-element.81), channel_id=1, replica_groups=mesh['book'=8,'path_0'=4,'path_1'=4] {'path_0','path_1'}, dimensions={0} | all-to-all | bytes 32768 | tf_op jit(solution)/shard_map/all_to_all | solution.py:395
  177.3 0.6 chain.17
  178.0 10.6 %all_to_all.73.refs_1_ = f32[16,1,256]{2,1,0:T(1,128)S(1)} all-to-all(f32[16,1,256]{2,1,0:T(1,128)S(1)} %get-tuple-element.85), channel_id=1, replica_groups=mesh['book'=8,'path_0'=4,'path_1'=4] {'path_0','path_1'}, dimensions={0} | all-to-all | bytes 32768 | tf_op jit(solution)/shard_map/all_to_all | solution.py:395
  188.6 0.6 chain.18
  189.2 10.6 %all_to_all.74.refs_1_ = f32[16,1,256]{2,1,0:T(1,128)S(1)} all-to-all(f32[16,1,256]{2,1,0:T(1,128)S(1)} %get-tuple-element.89), channel_id=1, replica_groups=mesh['book'=8,'path_0'=4,'path_1'=4] {'path_0','path_1'}, dimensions={0} | all-to-all | bytes 32768 | tf_op jit(solution)/shard_map/all_to_all | solution.py:395
  199.8 0.9 chain.19
  200.8 3.5 %all-to-all-start.12 = ((f32[16,1,128]{2,1,0:T(1,128)}), f32[16,1,128]{2,1,0:T(1,128)S(1)}, u32[]{:S(2)}, u32[]{:S(2)}) async-start(f32[16,1,128]{2,1,0:T(1,128)} %get-tuple-element.93), calls=%async_computation.12 | async-start | bytes 16384 | tf_op jit(solution)/shard_map/all_to_all | solution.py:395
  204.9 6.8 %all-to-all-done.12 = f32[16,1,128]{2,1,0:T(1,128)S(1)} async-done(((f32[16,1,128]{2,1,0:T(1,128)}), f32[16,1,128]{2,1,0:T(1,128)S(1)}, u32[]{:S(2)}, u32[]{:S(2)}) %all-to-all-start.12) | async-done | bytes 8224 | tf_op jit(solution)/shard_map/all_to_all | solution.py:395
  (30 shorter events, 1.3 us)
Async XLA Ops:
  0.6 18.3 %copy-start.1 = (s32[10,2048]{1,0:T(8,128)S(1)}, s32[10,2048]{1,0:T(8,128)}, u32[]{:S(2)}) copy-start(s32[10,2048]{1,0:T(8,128)} %refs_4_.19) | copy-start | bytes 245764
  0.6 11.3 %copy-start = (f32[10,20,2048]{2,1,0:T(8,128)S(1)}, f32[10,20,2048]{2,1,0:T(8,128)}, u32[]{:S(2)}) copy-start(f32[10,20,2048]{2,1,0:T(8,128)} %z_ref.5) | copy-start | bytes 4915204
  0.7 18.3 %copy-start.13 = (f32[2048]{0:T(1024)S(1)}, f32[2048]{0:T(1024)}, u32[]{:S(2)}) copy-start(f32[2048]{0:T(1024)} %param.7) | copy-start | bytes 24580
  3.3 15.7 %all-to-all-start = ((f32[16,8,128]{2,1,0:T(8,128)}), f32[16,8,128]{2,1,0:T(8,128)S(1)}, u32[]{:S(2)}, u32[]{:S(2)}) async-start(f32[16,8,128]{2,1,0:T(8,128)} %stats.1), calls=%async_computation | async-start | bytes 131072 | tf_op jit(solution)/shard_map/all_to_all | solution.py:395
  67.2 29.0 %all-to-all-start.2 = ((f32[16,112,256]{2,1,0:T(8,128)}), f32[16,112,256]{2,1,0:T(8,128)}, u32[]{:S(2)}, u32[]{:S(2)}) async-start(f32[16,112,256]{2,1,0:T(8,128)} %get-tuple-element.51), calls=%async_computation.2 | async-start | bytes 3670016 | tf_op jit(solution)/shard_map/all_to_all | solution.py:395
  80.7 18.2 %copy-start.3 = (f32[16,240,128]{2,1,0:T(8,128)S(1)}, f32[16,240,128]{2,1,0:T(8,128)}, u32[]{:S(2)}) copy-start(f32[16,240,128]{2,1,0:T(8,128)} %get-tuple-element.56.refs_8_.refs_2_) | copy-start | bytes 5898244
  80.7 18.2 %copy-start.12 = (s32[2048]{0:T(1024)S(1)}, s32[2048]{0:T(1024)}, u32[]{:S(2)}) copy-start(s32[2048]{0:T(1024)} %param.9) | copy-start | bytes 24580
  96.2 2.7 %copy-start.11 = (f32[16,240,128]{2,1,0:T(8,128)S(1)}, f32[16,240,128]{2,1,0:T(8,128)}, u32[]{:S(2)}) copy-start(f32[16,240,128]{2,1,0:T(8,128)} %get-tuple-element.53.refs_2_) | copy-start | bytes 5898244
  99.0 10.8 %copy-start.10 = (f32[16,240,128]{2,1,0:T(8,128)S(1)}, f32[16,240,128]{2,1,0:T(8,128)}, u32[]{:S(2)}) copy-start(f32[16,240,128]{2,1,0:T(8,128)} %get-tuple-element.59.refs_8_.refs_2_) | copy-start | bytes 5898244
  109.8 11.3 %copy-start.9 = (f32[16,240,128]{2,1,0:T(8,128)S(1)}, f32[16,240,128]{2,1,0:T(8,128)}, u32[]{:S(2)}) copy-start(f32[16,240,128]{2,1,0:T(8,128)} %get-tuple-element.63.refs_8_.refs_2_) | copy-start | bytes 5898244
  121.0 11.3 %copy-start.8 = (f32[16,240,128]{2,1,0:T(8,128)S(1)}, f32[16,240,128]{2,1,0:T(8,128)}, u32[]{:S(2)}) copy-start(f32[16,240,128]{2,1,0:T(8,128)} %get-tuple-element.67.refs_8_.refs_2_) | copy-start | bytes 5898244
  132.3 11.3 %copy-start.7 = (f32[16,240,128]{2,1,0:T(8,128)S(1)}, f32[16,240,128]{2,1,0:T(8,128)}, u32[]{:S(2)}) copy-start(f32[16,240,128]{2,1,0:T(8,128)} %get-tuple-element.71.refs_8_.refs_2_) | copy-start | bytes 5898244
  143.6 11.3 %copy-start.6 = (f32[16,240,128]{2,1,0:T(8,128)S(1)}, f32[16,240,128]{2,1,0:T(8,128)}, u32[]{:S(2)}) copy-start(f32[16,240,128]{2,1,0:T(8,128)} %get-tuple-element.75.refs_8_.refs_2_) | copy-start | bytes 5898244
  154.8 11.3 %copy-start.5 = (f32[16,240,128]{2,1,0:T(8,128)S(1)}, f32[16,240,128]{2,1,0:T(8,128)}, u32[]{:S(2)}) copy-start(f32[16,240,128]{2,1,0:T(8,128)} %get-tuple-element.79.refs_8_.refs_2_) | copy-start | bytes 5898244
  166.1 11.3 %copy-start.4 = (f32[16,240,128]{2,1,0:T(8,128)S(1)}, f32[16,240,128]{2,1,0:T(8,128)}, u32[]{:S(2)}) copy-start(f32[16,240,128]{2,1,0:T(8,128)} %get-tuple-element.83.refs_8_.refs_2_) | copy-start | bytes 5898244
  177.3 11.3 %copy-start.2 = (f32[16,240,128]{2,1,0:T(8,128)S(1)}, f32[16,240,128]{2,1,0:T(8,128)}, u32[]{:S(2)}) copy-start(f32[16,240,128]{2,1,0:T(8,128)} %get-tuple-element.87.refs_8_.refs_2_) | copy-start | bytes 5898244
  200.8 10.9 %all-to-all-start.12 = ((f32[16,1,128]{2,1,0:T(1,128)}), f32[16,1,128]{2,1,0:T(1,128)S(1)}, u32[]{:S(2)}, u32[]{:S(2)}) async-start(f32[16,1,128]{2,1,0:T(1,128)} %get-tuple-element.93), calls=%async_computation.12 | async-start | bytes 16384 | tf_op jit(solution)/shard_map/all_to_all | solution.py:395

commit v5 on v4

--- a/solution.py
+++ b/solution.py
@@ -19,6 +19,9 @@
 HALF = 128
 REST = 104
 SLOT = 112
+SENT = 64
+PIECES = 6
+WIDE = 256 * 9
 BLOCK = 16
 
 
@@ -176,9 +179,10 @@
         rhs_ref[...] = rhs
         packed = folded(gram[0:HALF, 0:HALF], beside, under, rhs)
         slots_ref[date] = packed
-        return packed
-
-    packed = fold(gram_ref[...], d + 1, step == 1)
+        again = 2 * dates - 1 - date
+        slots_ref[jnp.where(again < slots_ref.shape[0], again, date)] = packed
+
+    fold(gram_ref[...], d + 1, step == 1)
     flags = m_ref[pl.ds(d, 1), :].astype(f32)
     values = jnp.where(step == 0, v_ref[...], 0.0)
     mean, inverse = mean_ref[d], inverse_ref[d]
@@ -208,11 +212,6 @@
         total = part if total is None else total + part
     gram_ref[...] = total
 
-    @pl.when(step == 1)
-    def _():
-        for i in range(dates, slots_ref.shape[0]):
-            slots_ref[i] = packed
-
     @pl.when(step == dates - 1)
     def _():
         fold(gram_ref[...], 0, False)
@@ -268,7 +267,7 @@
     return total
 
 
-def inverse_kernel(parts_ref, out_ref, rhs_ref, a_ref):
+def inverse_kernel(dates, place_ref, parts_ref, out_ref, rest_ref, rhs_ref, a_ref):
     basis = 231
     packed = parts_ref[0]
     for i in range(1, parts_ref.shape[0]):
@@ -331,20 +330,49 @@
     lax.fori_loop(0, ROWS // BLOCK, sweep, 0)
     result = -a_ref[...]
     packed = folded(result[0:HALF, 0:HALF], result[0:HALF, HALF:], result[HALF:, HALF:])
+    own = jnp.broadcast_to(place_ref[...] < dates, (SENT, 256))
+    sent = jnp.where(own, packed[0:SENT], packed[SLOT - SENT :])
     for i in range(out_ref.shape[0]):
-        out_ref[i] = packed
-
-
-def unfold_kernel(packed_ref, out_ref):
+        out_ref[i] = sent
+    rest_ref[...] = packed[SENT:SLOT]
+
+
+def pieces_kernel(rest_ref, *out_refs):
+    for p, out_ref in enumerate(out_refs):
+        for i in range(out_ref.shape[0]):
+            out_ref[i, :, 0:256] = jnp.zeros((1, 256), f32)
+            for r in range(8):
+                row = 8 * p + r
+                out_ref[i, :, 256 * (1 + r) : 256 * (2 + r)] = rest_ref[row : row + 1, :]
+
+
+def unfold_pairs_kernel(first_date, dates, parts_ref, out_ref):
     for i in range(out_ref.shape[0]):
-        first, beside, last = unfolded(packed_ref[i])
-        out_ref[i, 0:HALF, 0:HALF] = first
-        out_ref[i, 0:HALF, HALF:] = beside
-        out_ref[i, HALF:, 0:HALF] = beside.T[0 : ROWS - HALF, :]
-        out_ref[i, HALF:, HALF:] = last[0 : ROWS - HALF, :]
-
-
-def chain_kernel(date, dates, *refs):
+        date = first_date + i
+        rest = parts_ref[2 * dates - 1 - date]
+        write_unfolded(jnp.concatenate([parts_ref[date], rest[2 * SENT - SLOT :]], axis=0), out_ref.at[i])
+
+
+def unfold_pieces_kernel(parts_ref, *refs):
+    *piece_refs, out_ref, packed_ref = refs
+    for i in range(out_ref.shape[0]):
+        packed_ref[i, 0:SENT, :] = parts_ref[i]
+        for p, piece_ref in enumerate(piece_refs):
+            for r in range(8):
+                row = SENT + 8 * p + r
+                packed_ref[i, row : row + 1, :] = piece_ref[i, :, 256 * (1 + r) : 256 * (2 + r)]
+        write_unfolded(packed_ref[i], out_ref.at[i])
+
+
+def write_unfolded(packed, out_ref):
+    first, beside, last = unfolded(packed)
+    out_ref[0:HALF, 0:HALF] = first
+    out_ref[0:HALF, HALF:] = beside
+    out_ref[HALF:, 0:HALF] = beside.T[0 : ROWS - HALF, :]
+    out_ref[HALF:, HALF:] = last[0 : ROWS - HALF, :]
+
+
+def chain_kernel(date, dates, first_date, *refs):
     inv_ref, parts_ref, phi_ref, ex_ref, m_ref, index_ref, v_ref, disc_ref = refs[:8]
     refs = refs[8:]
     if date:
@@ -355,10 +383,12 @@
     else:
         coefs = refs[0][...]
         refs = refs[1:]
-    rhs = parts_ref[0]
+    if len(refs) == 4:
+        refs = refs[1:]
+    rhs = parts_ref[0, :, 0:256]
     for i in range(1, parts_ref.shape[0]):
-        rhs = rhs + parts_ref[i]
-    product = inv_ref[date] * rhs
+        rhs = rhs + parts_ref[i, :, 0:256]
+    product = inv_ref[date - first_date] * rhs
     coef = jnp.sum(product[:, 0:128] + product[:, 128:], axis=1, keepdims=True)
     coef = jnp.broadcast_to(coef, (ROWS, 128))
     out_ref, coef_ref, send_ref = refs
@@ -375,7 +405,7 @@
         value = value * disc_ref[date - 1 : date, :]
         row = rhs_row(next_ref, value)
         for i in range(send_ref.shape[0]):
-            send_ref[i] = row[0:1, :]
+            send_ref[i, :, 0:256] = row[0:1, :]
     else:
         total = jnp.broadcast_to(jnp.sum(value, axis=1, keepdims=True), (1, 128))
         for i in range(send_ref.shape[0]):
@@ -417,6 +447,7 @@
         name="stats",
     )(pltpu.with_memory_space_constraint(states, pltpu.HBM), pltpu.with_memory_space_constraint(itm_flags, pltpu.HBM))
     stats = exchange(stats)
+    place = jnp.full((1, 256), lax.axis_index(PATH), jnp.int32)
     exercise, discount = pl.pallas_call(
         swap_kernel,
         in_specs=[pl.BlockSpec(memory_space=pltpu.SMEM), WHOLE],
@@ -428,6 +459,7 @@
     )(strike, states)
 
     tiles = paths // 128
+    discount, place = lax.optimization_barrier((discount, place))
     slots, value = pl.pallas_call(
         gram_kernel,
         grid=(dates,),
@@ -464,36 +496,76 @@
         name="basis",
     )(stats, states, itm_flags)
     slots = exchange(slots)
-    inverse, received = pl.pallas_call(
-        inverse_kernel,
+    def invert(*refs):
+        inverse_kernel(dates, *refs)
+
+    inverse, rest, received = pl.pallas_call(
+        invert,
         grid=(1,),
-        in_specs=[WHOLE],
-        out_specs=[spec((size, SLOT, 256)), WHOLE],
-        out_shape=[pltpu.HBM((size, SLOT, 256), f32), vmem((1, 1, 256), f32)],
+        in_specs=[WHOLE, WHOLE],
+        out_specs=[spec((size, SENT, 256)), WHOLE, WHOLE],
+        out_shape=[
+            pltpu.HBM((size, SENT, 256), f32),
+            vmem((SLOT - SENT, 256), f32),
+            vmem((1, 1, 256), f32),
+        ],
         scratch_shapes=[pltpu.VMEM((256, 256), f32)],
         compiler_params=limit,
         name="inverse",
-    )(near(slots))
+    )(near(place), near(slots))
     inverse = exchange(inverse)
-    inverse = pl.pallas_call(
-        unfold_kernel,
+    pieces = pl.pallas_call(
+        pieces_kernel,
         grid=(1,),
-        in_specs=[spec((dates, SLOT, 256))],
+        in_specs=[WHOLE],
+        out_specs=[spec((size, 1, WIDE))] * PIECES,
+        out_shape=[pltpu.HBM((size, 1, WIDE), f32)] * PIECES,
+        compiler_params=limit,
+        name="pieces",
+    )(near(rest))
+    paired = 2 * dates - size
+
+    def unfold_pairs(*refs):
+        unfold_pairs_kernel(paired, dates, *refs)
+
+    first_inverse = pl.pallas_call(
+        unfold_pairs,
+        grid=(1,),
+        in_specs=[spec((size, SENT, 256))],
         out_specs=WHOLE,
-        out_shape=vmem((dates, ROWS, 256), f32),
+        out_shape=vmem((dates - paired, ROWS, 256), f32),
         compiler_params=limit,
-        name="unfold",
+        name="unfold_pairs",
     )(inverse)
+    other_inverse = None
+    carried = []
     coefs = None
     for date in range(dates - 1, -1, -1):
-        args = [inverse, received, phi[date], exercise, itm_flags, date_index, value, discount]
+        if date == paired - 1:
+            other_inverse = pl.pallas_call(
+                unfold_pieces_kernel,
+                grid=(1,),
+                in_specs=[spec((paired, SENT, 256))] + [WHOLE] * PIECES,
+                out_specs=WHOLE,
+                out_shape=vmem((paired, ROWS, 256), f32),
+                scratch_shapes=[pltpu.VMEM((paired, SLOT, 256), f32)],
+                compiler_params=limit,
+                name="unfold_pieces",
+            )(inverse, *(near(x) for x in carried))
+        first_date = paired if date >= paired else 0
+        args = [first_inverse if date >= paired else other_inverse, received, phi[date], exercise, itm_flags, date_index, value, discount]
         if date:
             args.append(phi[date - 1])
         if date < dates - 1:
             args.append(coefs)
-
-        def kernel(*refs, date=date):
-            chain_kernel(date, dates, *refs)
+        carries = len(carried) < PIECES
+        aliases = {}
+        if carries:
+            aliases = {len(args): 2}
+            args.append(pieces[len(carried)])
+
+        def kernel(*refs, date=date, first_date=first_date):
+            chain_kernel(date, dates, first_date, *refs)
 
         value, coefs, send = pl.pallas_call(
             kernel,
@@ -502,14 +574,17 @@
             out_shape=[
                 vmem((1, paths), f32),
                 vmem((ROWS, 128), f32),
-                vmem((size, 1, 256), f32),
+                vmem((size, 1, WIDE if carries else 256), f32),
             ]
             if date
             else [sds((1, paths), f32), sds((128, 256), f32), sds((size, 1, 128), f32)],
+            input_output_aliases=aliases,
             compiler_params=limit,
             name="chain",
         )(*(near(x) for x in args))
         received = exchange(send)
+        if carries:
+            carried.append(received)
     book_price = jnp.sum(received[:, 0, 0:1], axis=0) / (paths * size)
     basis = 1 + factors + factors * (factors + 1) // 2
     coefficients = coefs[0:dates, 0:basis]

time: 215 us -> 209 us (0.972)
  waiting for transfers between devices: 28.5 us -> 18.1 us
  blocking collectives: 123 us -> 127 us
    all_to_all x3, waiting for transfers between devices: 28.5 us -> 18.1 us  [exchange(): return lax.all_to_all(slots, PATH, 0, 0, tiled=True)]
    all_to_all x10, blocking collectives: 123 us -> 127 us  [exchange(): return lax.all_to_all(slots, PATH, 0, 0, tiled=True)]
    pallas_call x2 -> x4, Pallas kernels: 11.3 us -> 11 us  [the longest x1 8.27 us: shards(): pl.pallas_call(invert, grid=(1,), in_specs=[WHOLE, WHOLE], out_specs=[spe...]
where the time goes in v5:
time: 209 us; the launch traced here: 208 us
  blocking collectives  127 us (61%)
  Pallas kernels  41.9 us (20%)
  waiting for transfers between devices  18.1 us (9%)
  starting transfers between devices  15 us (7%)
  between operations  3.25 us (2%)
  local copies, waits for them, and re-layouts  2.24 us (1%)
    all_to_all x10, blocking collectives, exchange(): return lax.all_to_all(slots, PATH, 0, 0, tiled=True)  127 us
    all_to_all x3, waiting for transfers between devices, exchange(): return lax.all_to_all(slots, PATH, 0, 0, tiled=True)  18.1 us
    all_to_all x3, starting transfers between devices, exchange(): return lax.all_to_all(slots, PATH, 0, 0, tiled=True)  15 us
    pallas_call x1, Pallas kernels, shards(): pl.pallas_call(gram_kernel, grid=(dates,), in_specs=[WHOLE] * 5, out_spec...  11.7 us
    pallas_call x1, Pallas kernels, shards(): pl.pallas_call(basis_kernel, grid=(dates,), in_specs=[spec((size, 8, 128)...  9.13 us
    pallas_call x1, Pallas kernels, shards(): pl.pallas_call(invert, grid=(1,), in_specs=[WHOLE, WHOLE], out_specs=[spe...  8.27 us
    pallas_call x10, Pallas kernels, shards(): pl.pallas_call(kernel, in_specs=[WHOLE] * len(args), out_specs=[WHOLE] *...  6.66 us
  transfers between devices with their start and end apart: 3, of which 3 were waited for; matrix products, arithmetic and copies ran while one was open for 0% of the time, Pallas kernels for 5%

profile of v5, /device:TPU:0, one launch (start us, length us, event | category | flops | bytes accessed | tf_op | source)
XLA Modules:
  0.0 208.0 jit_solution(18034394085187850137)
XLA Ops:
  0.7 2.6 %stats.1 = f32[16,8,128]{2,1,0:T(8,128)} custom-call(f32[10,20,2048]{2,1,0:T(8,128)} %z_ref.5, s32[10,2048]{1,0:T(8,128)} %refs_4_.19), custom_call_target="tpu_custom_call" | custom-call | tf_op jit(solution)/shard_map/stats/pallas_call | solution.py:436
  3.3 8.0 %all-to-all-start = ((f32[16,8,128]{2,1,0:T(8,128)}), f32[16,8,128]{2,1,0:T(8,128)S(1)}, u32[]{:S(2)}, u32[]{:S(2)}) async-start(f32[16,8,128]{2,1,0:T(8,128)} %stats.1), calls=%async_computation | async-start | bytes 131072 | tf_op jit(solution)/shard_map/all_to_all | solution.py:425
  12.0 0.8 swap.1
  12.8 6.2 %all-to-all-done.stats_ref = f32[16,8,128]{2,1,0:T(8,128)S(1)} async-done(((f32[16,8,128]{2,1,0:T(8,128)}), f32[16,8,128]{2,1,0:T(8,128)S(1)}, u32[]{:S(2)}, u32[]{:S(2)}) %all-to-all-start) | async-done | bytes 65568 | tf_op jit(solution)/shard_map/all_to_all | solution.py:425
  19.0 11.7 %gram.1 = (f32[16,112,256]{2,1,0:T(8,128)S(1)}, f32[1,2048]{1,0:T(1,128)S(1)}) custom-call(f32[16,8,128]{2,1,0:T(8,128)S(1)} %all-to-all-done.stats_ref, f32[10,20,2048]{2,1,0:T(8,128)S(1)} %copy-done, s32[10,2048]{1,0:T(8,128)S(1)} %copy-done.1, f32[10,2048]{1,0:T(8,128)S(1)} %get-tuple-element.60.disc_ref.refs_7_, f32[1,2048]{1,0:T(1,128)S(1)} %bitcast.14), custom_call_target="tpu_custom_call" | custom-call | tf_op jit(solution)/shard_map/gram/pallas_call | solution.py:463
  30.7 27.9 %all_to_all.65.refs_1_ = f32[16,112,256]{2,1,0:T(8,128)S(1)} all-to-all(f32[16,112,256]{2,1,0:T(8,128)S(1)} %get-tuple-element.61), channel_id=1, replica_groups=mesh['book'=8,'path_0'=4,'path_1'=4] {'path_0','path_1'}, dimensions={0} | all-to-all | bytes 3670016 | tf_op jit(solution)/shard_map/all_to_all | solution.py:425
  58.6 8.3 %inverse.1 = (f32[16,64,256]{2,1,0:T(8,128)}, f32[48,256]{1,0:T(8,128)S(1)}, f32[1,1,256]{2,1,0:T(1,128)S(1)}) custom-call(s32[1,256]{1,0:T(1,128)S(1)} %broadcast_in_dim.3.refs_0_, f32[16,112,256]{2,1,0:T(8,128)S(1)} %all_to_all.65.refs_1_), custom_call_target="tpu_custom_call" | custom-call | tf_op jit(solution)/shard_map/inverse/pallas_call | solution.py:502
  66.9 3.7 %all-to-all-start.2 = ((f32[16,64,256]{2,1,0:T(8,128)}), f32[16,64,256]{2,1,0:T(8,128)S(1)}, u32[]{:S(2)}, u32[]{:S(2)}) async-start(f32[16,64,256]{2,1,0:T(8,128)} %get-tuple-element.62), calls=%async_computation.2 | async-start | bytes 2097152 | tf_op jit(solution)/shard_map/all_to_all | solution.py:425
  70.5 9.1 %basis.1 = (f32[16,240,128]{2,1,0:T(8,128)}, f32[16,240,128]{2,1,0:T(8,128)}, f32[16,240,128]{2,1,0:T(8,128)}, f32[16,240,128]{2,1,0:T(8,128)}, f32[16,240,128]{...) custom-call(f32[16,8,128]{2,1,0:T(8,128)S(1)} %all-to-all-done.stats, ...), custom_call_target="tpu_custom_call" | custom-call | tf_op jit(solution)/shard_map/basis/pallas_call | solution.py:480
  79.7 1.2 pieces.1
  80.9 5.0 %all-to-all-done.2.refs_0_.parts_ref = f32[16,64,256]{2,1,0:T(8,128)S(1)} async-done(((f32[16,64,256]{2,1,0:T(8,128)}), f32[16,64,256]{2,1,0:T(8,128)S(1)}, u32[]{:S(2)}, u32[]{:S(2)}) %all-to-all-start.2) | async-done | bytes 1048608 | tf_op jit(solution)/shard_map/all_to_all | solution.py:425
  85.9 0.9 unfold_pairs.1.refs_0_
  86.8 1.5 copy-done.11
  88.9 11.1 %all_to_all.66.refs_1_.refs_0_ = f32[16,1,2304]{2,1,0:T(1,128)S(1)} all-to-all(f32[16,1,2304]{2,1,0:T(1,128)S(1)} %get-tuple-element.70), channel_id=1, replica_groups=mesh['book'=8,'path_0'=4,'path_1'=4] {'path_0','path_1'}, dimensions={0} | all-to-all | bytes 294912 | tf_op jit(solution)/shard_map/all_to_all | solution.py:425
  100.1 0.6 chain.11
  100.7 11.1 %all_to_all.67.refs_1_ = f32[16,1,2304]{2,1,0:T(1,128)S(1)} all-to-all(f32[16,1,2304]{2,1,0:T(1,128)S(1)} %get-tuple-element.75), channel_id=1, replica_groups=mesh['book'=8,'path_0'=4,'path_1'=4] {'path_0','path_1'}, dimensions={0} | all-to-all | bytes 294912 | tf_op jit(solution)/shard_map/all_to_all | solution.py:425
  111.9 0.6 chain.12
  112.5 11.1 %all_to_all.68.refs_1_.refs_2_ = f32[16,1,2304]{2,1,0:T(1,128)S(1)} all-to-all(f32[16,1,2304]{2,1,0:T(1,128)S(1)} %get-tuple-element.80), channel_id=1, replica_groups=mesh['book'=8,'path_0'=4,'path_1'=4] {'path_0','path_1'}, dimensions={0} | all-to-all | bytes 294912 | tf_op jit(solution)/shard_map/all_to_all | solution.py:425
  123.7 0.6 chain.13
  124.3 11.1 %all_to_all.69.refs_1_.refs_3_ = f32[16,1,2304]{2,1,0:T(1,128)S(1)} all-to-all(f32[16,1,2304]{2,1,0:T(1,128)S(1)} %get-tuple-element.85), channel_id=1, replica_groups=mesh['book'=8,'path_0'=4,'path_1'=4] {'path_0','path_1'}, dimensions={0} | all-to-all | bytes 294912 | tf_op jit(solution)/shard_map/all_to_all | solution.py:425
  135.5 0.6 chain.14
  136.1 11.4 %all_to_all.70.refs_1_.refs_4_ = f32[16,1,2304]{2,1,0:T(1,128)S(1)} all-to-all(f32[16,1,2304]{2,1,0:T(1,128)S(1)} %get-tuple-element.90), channel_id=1, replica_groups=mesh['book'=8,'path_0'=4,'path_1'=4] {'path_0','path_1'}, dimensions={0} | all-to-all | bytes 294912 | tf_op jit(solution)/shard_map/all_to_all | solution.py:425
  147.6 0.6 chain.15
  148.2 11.1 %all_to_all.71.refs_5_.refs_1_ = f32[16,1,2304]{2,1,0:T(1,128)S(1)} all-to-all(f32[16,1,2304]{2,1,0:T(1,128)S(1)} %get-tuple-element.95), channel_id=1, replica_groups=mesh['book'=8,'path_0'=4,'path_1'=4] {'path_0','path_1'}, dimensions={0} | all-to-all | bytes 294912 | tf_op jit(solution)/shard_map/all_to_all | solution.py:425
  159.3 0.6 unfold_pieces.1.refs_0_
  160.0 0.6 chain.16
  160.6 10.7 %all_to_all.72.refs_1_ = f32[16,1,256]{2,1,0:T(1,128)S(1)} all-to-all(f32[16,1,256]{2,1,0:T(1,128)S(1)} %get-tuple-element.99), channel_id=1, replica_groups=mesh['book'=8,'path_0'=4,'path_1'=4] {'path_0','path_1'}, dimensions={0} | all-to-all | bytes 32768 | tf_op jit(solution)/shard_map/all_to_all | solution.py:425
  171.9 10.6 %all_to_all.73.refs_1_ = f32[16,1,256]{2,1,0:T(1,128)S(1)} all-to-all(f32[16,1,256]{2,1,0:T(1,128)S(1)} %get-tuple-element.103), channel_id=1, replica_groups=mesh['book'=8,'path_0'=4,'path_1'=4] {'path_0','path_1'}, dimensions={0} | all-to-all | bytes 32768 | tf_op jit(solution)/shard_map/all_to_all | solution.py:425
  183.2 10.6 %all_to_all.74.refs_1_ = f32[16,1,256]{2,1,0:T(1,128)S(1)} all-to-all(f32[16,1,256]{2,1,0:T(1,128)S(1)} %get-tuple-element.107), channel_id=1, replica_groups=mesh['book'=8,'path_0'=4,'path_1'=4] {'path_0','path_1'}, dimensions={0} | all-to-all | bytes 32768 | tf_op jit(solution)/shard_map/all_to_all | solution.py:425
  193.8 0.9 chain.19
  194.7 3.4 %all-to-all-start.12 = ((f32[16,1,128]{2,1,0:T(1,128)}), f32[16,1,128]{2,1,0:T(1,128)S(1)}, u32[]{:S(2)}, u32[]{:S(2)}) async-start(f32[16,1,128]{2,1,0:T(1,128)} %get-tuple-element.111), calls=%async_computation.12 | async-start | bytes 16384 | tf_op jit(solution)/shard_map/all_to_all | solution.py:425
  198.7 6.9 %all-to-all-done.12 = f32[16,1,128]{2,1,0:T(1,128)S(1)} async-done(((f32[16,1,128]{2,1,0:T(1,128)}), f32[16,1,128]{2,1,0:T(1,128)S(1)}, u32[]{:S(2)}, u32[]{:S(2)}) %all-to-all-start.12) | async-done | bytes 8224 | tf_op jit(solution)/shard_map/all_to_all | solution.py:425
  (45 shorter events, 3.2 us)
Async XLA Ops:
  0.6 18.3 %copy-start.1 = (s32[10,2048]{1,0:T(8,128)S(1)}, s32[10,2048]{1,0:T(8,128)}, u32[]{:S(2)}) copy-start(s32[10,2048]{1,0:T(8,128)} %refs_4_.19) | copy-start | bytes 245764
  0.6 11.3 %copy-start = (f32[10,20,2048]{2,1,0:T(8,128)S(1)}, f32[10,20,2048]{2,1,0:T(8,128)}, u32[]{:S(2)}) copy-start(f32[10,20,2048]{2,1,0:T(8,128)} %z_ref.5) | copy-start | bytes 4915204
  0.7 18.3 %copy-start.19 = (f32[2048]{0:T(1024)S(1)}, f32[2048]{0:T(1024)}, u32[]{:S(2)}) copy-start(f32[2048]{0:T(1024)} %param.7) | copy-start | bytes 24580
  3.3 15.7 %all-to-all-start = ((f32[16,8,128]{2,1,0:T(8,128)}), f32[16,8,128]{2,1,0:T(8,128)S(1)}, u32[]{:S(2)}, u32[]{:S(2)}) async-start(f32[16,8,128]{2,1,0:T(8,128)} %stats.1), calls=%async_computation | async-start | bytes 131072 | tf_op jit(solution)/shard_map/all_to_all | solution.py:425
  66.9 19.0 %all-to-all-start.2 = ((f32[16,64,256]{2,1,0:T(8,128)}), f32[16,64,256]{2,1,0:T(8,128)S(1)}, u32[]{:S(2)}, u32[]{:S(2)}) async-start(f32[16,64,256]{2,1,0:T(8,128)} %get-tuple-element.62), calls=%async_computation.2 | async-start | bytes 2097152 | tf_op jit(solution)/shard_map/all_to_all | solution.py:425
  70.5 16.2 %copy-start.12 = (s32[2048]{0:T(1024)S(1)}, s32[2048]{0:T(1024)}, u32[]{:S(2)}) copy-start(s32[2048]{0:T(1024)} %param.9) | copy-start | bytes 24580
  79.7 7.1 %copy-start.8 = (f32[16,240,128]{2,1,0:T(8,128)S(1)}, f32[16,240,128]{2,1,0:T(8,128)}, u32[]{:S(2)}) copy-start(f32[16,240,128]{2,1,0:T(8,128)} %get-tuple-element.67.refs_8_.refs_2_) | copy-start | bytes 5898244
  85.9 0.9 copy-start.18
  86.8 1.5 copy-start.11
  88.3 11.8 %copy-start.7 = (f32[16,240,128]{2,1,0:T(8,128)S(1)}, f32[16,240,128]{2,1,0:T(8,128)}, u32[]{:S(2)}) copy-start(f32[16,240,128]{2,1,0:T(8,128)} %get-tuple-element.72.refs_8_.refs_2_) | copy-start | bytes 5898244
  88.3 11.8 %copy-start.17 = (f32[16,1,2304]{2,1,0:T(1,128)S(1)}, f32[16,1,2304]{2,1,0:T(1,128)}, u32[]{:S(2)}) copy-start(f32[16,1,2304]{2,1,0:T(1,128)} %get-tuple-element.74.refs_10_) | copy-start | bytes 442372
  100.1 11.8 %copy-start.6 = (f32[16,240,128]{2,1,0:T(8,128)S(1)}, f32[16,240,128]{2,1,0:T(8,128)}, u32[]{:S(2)}) copy-start(f32[16,240,128]{2,1,0:T(8,128)} %get-tuple-element.77.refs_8_.refs_2_) | copy-start | bytes 5898244
  100.1 11.8 %copy-start.16 = (f32[16,1,2304]{2,1,0:T(1,128)S(1)}, f32[16,1,2304]{2,1,0:T(1,128)}, u32[]{:S(2)}) copy-start(f32[16,1,2304]{2,1,0:T(1,128)} %get-tuple-element.79.refs_10_) | copy-start | bytes 442372
  111.9 11.8 %copy-start.5 = (f32[16,240,128]{2,1,0:T(8,128)S(1)}, f32[16,240,128]{2,1,0:T(8,128)}, u32[]{:S(2)}) copy-start(f32[16,240,128]{2,1,0:T(8,128)} %get-tuple-element.82.refs_8_.refs_2_) | copy-start | bytes 5898244
  111.9 11.8 %copy-start.15 = (f32[16,1,2304]{2,1,0:T(1,128)S(1)}, f32[16,1,2304]{2,1,0:T(1,128)}, u32[]{:S(2)}) copy-start(f32[16,1,2304]{2,1,0:T(1,128)} %get-tuple-element.84.refs_10_) | copy-start | bytes 442372
  123.7 11.8 %copy-start.4 = (f32[16,240,128]{2,1,0:T(8,128)S(1)}, f32[16,240,128]{2,1,0:T(8,128)}, u32[]{:S(2)}) copy-start(f32[16,240,128]{2,1,0:T(8,128)} %get-tuple-element.87.refs_8_.refs_2_) | copy-start | bytes 5898244
  123.7 11.8 %copy-start.14 = (f32[16,1,2304]{2,1,0:T(1,128)S(1)}, f32[16,1,2304]{2,1,0:T(1,128)}, u32[]{:S(2)}) copy-start(f32[16,1,2304]{2,1,0:T(1,128)} %get-tuple-element.89.refs_10_) | copy-start | bytes 442372
  135.5 12.1 %copy-start.10 = (f32[16,240,128]{2,1,0:T(8,128)S(1)}, f32[16,240,128]{2,1,0:T(8,128)}, u32[]{:S(2)}) copy-start(f32[16,240,128]{2,1,0:T(8,128)} %get-tuple-element.92.refs_8_.refs_2_) | copy-start | bytes 5898244
  135.5 12.1 %copy-start.13 = (f32[16,1,2304]{2,1,0:T(1,128)S(1)}, f32[16,1,2304]{2,1,0:T(1,128)}, u32[]{:S(2)}) copy-start(f32[16,1,2304]{2,1,0:T(1,128)} %get-tuple-element.94.refs_10_) | copy-start | bytes 442372
  148.2 11.8 %copy-start.9 = (f32[16,240,128]{2,1,0:T(8,128)S(1)}, f32[16,240,128]{2,1,0:T(8,128)}, u32[]{:S(2)}) copy-start(f32[16,240,128]{2,1,0:T(8,128)} %get-tuple-element.97.refs_8_.refs_2_) | copy-start | bytes 5898244
  160.0 11.3 %copy-start.3 = (f32[16,240,128]{2,1,0:T(8,128)S(1)}, f32[16,240,128]{2,1,0:T(8,128)}, u32[]{:S(2)}) copy-start(f32[16,240,128]{2,1,0:T(8,128)} %get-tuple-element.101.refs_8_.refs_2_) | copy-start | bytes 5898244
  171.3 11.3 %copy-start.2 = (f32[16,240,128]{2,1,0:T(8,128)S(1)}, f32[16,240,128]{2,1,0:T(8,128)}, u32[]{:S(2)}) copy-start(f32[16,240,128]{2,1,0:T(8,128)} %get-tuple-element.105.refs_8_.refs_2_) | copy-start | bytes 5898244
  194.7 10.9 %all-to-all-start.12 = ((f32[16,1,128]{2,1,0:T(1,128)}), f32[16,1,128]{2,1,0:T(1,128)S(1)}, u32[]{:S(2)}, u32[]{:S(2)}) async-start(f32[16,1,128]{2,1,0:T(1,128)} %get-tuple-element.111), calls=%async_computation.12 | async-start | bytes 16384 | tf_op jit(solution)/shard_map/all_to_all | solution.py:425

commit v6 on v5

--- a/solution.py
+++ b/solution.py
@@ -155,7 +155,7 @@
 
 
 def gram_kernel(stats_ref, z_all_ref, m_ref, disc_ref, term_ref, slots_ref, v_ref, *scratch):
-    phi_ref, x_ref, gram_ref, rhs_ref, mean_ref, inverse_ref = scratch
+    phi_ref, x_ref, gram_ref, cross_ref, rhs_ref, mean_ref, inverse_ref = scratch
     step = pl.program_id(0)
     dates, factors, paths = z_all_ref.shape
     d = dates - 1 - step
@@ -164,13 +164,16 @@
     def _():
         x_ref[...] = jnp.zeros_like(x_ref)
         gram_ref[...] = jnp.zeros_like(gram_ref)
+        cross_ref[...] = jnp.zeros_like(cross_ref)
         v_ref[...] = term_ref[...] * disc_ref[dates - 1 : dates, :]
         for date in range(dates):
             mean, inverse = moments(stats_ref, date, factors)
             mean_ref[date] = jnp.broadcast_to(mean, (factors, 128))
             inverse_ref[date] = jnp.broadcast_to(inverse, (factors, 128))
 
-    def fold(gram, date, first):
+    def fold(date, first):
+        cross = cross_ref[...]
+        gram = gram_ref[...] + cross + cross.T
         row, lane = rows_of((HALF, HALF)), lanes_of((HALF, HALF))
         beside = jnp.where(lane < REST, gram[0:HALF, HALF:], 0.0)
         under = jnp.where((row < REST) & (lane < REST), gram[HALF:, HALF:], 0.0)
@@ -182,7 +185,7 @@
         again = 2 * dates - 1 - date
         slots_ref[jnp.where(again < slots_ref.shape[0], again, date)] = packed
 
-    fold(gram_ref[...], d + 1, step == 1)
+    fold(d + 1, step == 1)
     flags = m_ref[pl.ds(d, 1), :].astype(f32)
     values = jnp.where(step == 0, v_ref[...], 0.0)
     mean, inverse = mean_ref[d], inverse_ref[d]
@@ -208,13 +211,13 @@
         both = lax.dot_general(
             jnp.concatenate([hi, lo], axis=0), hi, NT, preferred_element_type=f32
         )
-        part = both[0:256] + both[256:] + lax.dot_general(hi, lo, NT, preferred_element_type=f32)
-        total = part if total is None else total + part
-    gram_ref[...] = total
+        total = both if total is None else total + both
+    gram_ref[...] = total[0:256]
+    cross_ref[...] = total[256:]
 
     @pl.when(step == dates - 1)
     def _():
-        fold(gram_ref[...], 0, False)
+        fold(0, False)
 
 
 def folded(first, beside, last, rhs=None):
@@ -346,11 +349,20 @@
                 out_ref[i, :, 256 * (1 + r) : 256 * (2 + r)] = rest_ref[row : row + 1, :]
 
 
-def unfold_pairs_kernel(first_date, dates, parts_ref, out_ref):
+def unfold_pairs_kernel(first_date, dates, parts_ref, *refs):
+    *far_refs, out_ref, near_a_ref, near_b_ref, sems = refs
+    copies = [
+        pltpu.make_async_copy(far, beside, sems.at[i])
+        for i, (far, beside) in enumerate(zip(far_refs, (near_a_ref, near_b_ref)))
+    ]
+    for copy in copies:
+        copy.start()
     for i in range(out_ref.shape[0]):
         date = first_date + i
         rest = parts_ref[2 * dates - 1 - date]
         write_unfolded(jnp.concatenate([parts_ref[date], rest[2 * SENT - SLOT :]], axis=0), out_ref.at[i])
+    for copy in copies:
+        copy.wait()
 
 
 def unfold_pieces_kernel(parts_ref, *refs):
@@ -470,6 +482,7 @@
             pltpu.VMEM((tiles, ROWS, 128), f32),
             pltpu.VMEM((tiles, 32, 128), f32),
             pltpu.VMEM((256, 256), f32),
+            pltpu.VMEM((256, 256), f32),
             pltpu.VMEM((1, 256), f32),
             pltpu.VMEM((dates, factors, 128), f32),
             pltpu.VMEM((dates, factors, 128), f32),
@@ -528,15 +541,17 @@
     def unfold_pairs(*refs):
         unfold_pairs_kernel(paired, dates, *refs)
 
-    first_inverse = pl.pallas_call(
+    first_inverse, *near_phi = pl.pallas_call(
         unfold_pairs,
         grid=(1,),
-        in_specs=[spec((size, SENT, 256))],
-        out_specs=WHOLE,
-        out_shape=vmem((dates - paired, ROWS, 256), f32),
+        in_specs=[spec((size, SENT, 256))] + [pl.BlockSpec(memory_space=pltpu.HBM)] * 2,
+        out_specs=[WHOLE] * 3,
+        out_shape=[vmem((dates - paired, ROWS, 256), f32)] + [vmem((tiles, ROWS, 128), f32)] * 2,
+        scratch_shapes=[pltpu.SemaphoreType.DMA((2,))],
         compiler_params=limit,
         name="unfold_pairs",
-    )(inverse)
+    )(inverse, *(pltpu.with_memory_space_constraint(phi[d], pltpu.HBM) for d in (dates - 1, dates - 2)))
+    phi = [*phi[: dates - 2], *near_phi[::-1]]
     other_inverse = None
     carried = []
     coefs = None

time: 209 us -> 207 us (level)
  no operation moved by 1% of the time
where the time goes in v6:
time: 207 us; the launch traced here: 206 us
  blocking collectives  127 us (61%)
  Pallas kernels  41.7 us (20%)
  waiting for transfers between devices  18.1 us (9%)
  starting transfers between devices  15.1 us (7%)
  between operations  3.25 us (2%)
    all_to_all x10, blocking collectives, exchange(): return lax.all_to_all(slots, PATH, 0, 0, tiled=True)  127 us
    all_to_all x3, waiting for transfers between devices, exchange(): return lax.all_to_all(slots, PATH, 0, 0, tiled=True)  18.1 us
    all_to_all x3, starting transfers between devices, exchange(): return lax.all_to_all(slots, PATH, 0, 0, tiled=True)  15.1 us
    pallas_call x1, Pallas kernels, shards(): pl.pallas_call(gram_kernel, grid=(dates,), in_specs=[WHOLE] * 5, out_spec...  10.3 us
    pallas_call x1, Pallas kernels, shards(): pl.pallas_call(basis_kernel, grid=(dates,), in_specs=[spec((size, 8, 128)...  9.07 us
    pallas_call x1, Pallas kernels, shards(): pl.pallas_call(invert, grid=(1,), in_specs=[WHOLE, WHOLE], out_specs=[spe...  8.28 us
    pallas_call x10, Pallas kernels, shards(): pl.pallas_call(kernel, in_specs=[WHOLE] * len(args), out_specs=[WHOLE] *...  6.66 us
  transfers between devices with their start and end apart: 3, of which 3 were waited for; matrix products, arithmetic and copies ran while one was open for 0% of the time, Pallas kernels for 5%

profile of v6, /device:TPU:0, one launch (start us, length us, event | category | flops | bytes accessed | tf_op | source)
XLA Modules:
  0.0 206.3 jit_solution(4063289578634578795)
XLA Ops:
  0.7 2.6 %stats.1 = f32[16,8,128]{2,1,0:T(8,128)} custom-call(f32[10,20,2048]{2,1,0:T(8,128)} %z_ref.5, s32[10,2048]{1,0:T(8,128)} %refs_4_.19), custom_call_target="tpu_custom_call" | custom-call | tf_op jit(solution)/shard_map/stats/pallas_call | solution.py:448
  3.3 8.0 %all-to-all-start = ((f32[16,8,128]{2,1,0:T(8,128)}), f32[16,8,128]{2,1,0:T(8,128)S(1)}, u32[]{:S(2)}, u32[]{:S(2)}) async-start(f32[16,8,128]{2,1,0:T(8,128)} %stats.1), calls=%async_computation | async-start | bytes 131072 | tf_op jit(solution)/shard_map/all_to_all | solution.py:437
  11.9 0.8 swap.1
  12.7 6.2 %all-to-all-done.stats_ref = f32[16,8,128]{2,1,0:T(8,128)S(1)} async-done(((f32[16,8,128]{2,1,0:T(8,128)}), f32[16,8,128]{2,1,0:T(8,128)S(1)}, u32[]{:S(2)}, u32[]{:S(2)}) %all-to-all-start) | async-done | bytes 65568 | tf_op jit(solution)/shard_map/all_to_all | solution.py:437
  19.0 10.3 %gram.1 = (f32[16,112,256]{2,1,0:T(8,128)S(1)}, f32[1,2048]{1,0:T(1,128)S(1)}) custom-call(f32[16,8,128]{2,1,0:T(8,128)S(1)} %all-to-all-done.stats_ref, f32[10,20,2048]{2,1,0:T(8,128)S(1)} %copy-done, s32[10,2048]{1,0:T(8,128)S(1)} %copy-done.1, f32[10,2048]{1,0:T(8,128)S(1)} %get-tuple-element.63.disc_ref.refs_7_, f32[1,2048]{1,0:T(1,128)S(1)} %bitcast.14), custom_call_target="tpu_custom_call" | custom-call | tf_op jit(solution)/shard_map/gram/pallas_call | solution.py:475
  29.2 27.9 %all_to_all.65.refs_1_ = f32[16,112,256]{2,1,0:T(8,128)S(1)} all-to-all(f32[16,112,256]{2,1,0:T(8,128)S(1)} %get-tuple-element.64), channel_id=1, replica_groups=mesh['book'=8,'path_0'=4,'path_1'=4] {'path_0','path_1'}, dimensions={0} | all-to-all | bytes 3670016 | tf_op jit(solution)/shard_map/all_to_all | solution.py:437
  57.2 8.3 %inverse.1 = (f32[16,64,256]{2,1,0:T(8,128)}, f32[48,256]{1,0:T(8,128)S(1)}, f32[1,1,256]{2,1,0:T(1,128)S(1)}) custom-call(s32[1,256]{1,0:T(1,128)S(1)} %broadcast_in_dim.3.refs_0_, f32[16,112,256]{2,1,0:T(8,128)S(1)} %all_to_all.65.refs_1_), custom_call_target="tpu_custom_call" | custom-call | tf_op jit(solution)/shard_map/inverse/pallas_call | solution.py:515
  65.4 3.7 %all-to-all-start.2 = ((f32[16,64,256]{2,1,0:T(8,128)}), f32[16,64,256]{2,1,0:T(8,128)S(1)}, u32[]{:S(2)}, u32[]{:S(2)}) async-start(f32[16,64,256]{2,1,0:T(8,128)} %get-tuple-element.65), calls=%async_computation.2 | async-start | bytes 2097152 | tf_op jit(solution)/shard_map/all_to_all | solution.py:437
  69.1 9.1 %basis.1 = (f32[16,240,128]{2,1,0:T(8,128)}, f32[16,240,128]{2,1,0:T(8,128)}, f32[16,240,128]{2,1,0:T(8,128)}, f32[16,240,128]{2,1,0:T(8,128)}, f32[16,240,128]{...) custom-call(f32[16,8,128]{2,1,0:T(8,128)S(1)} %all-to-all-done.stats, ...), custom_call_target="tpu_custom_call" | custom-call | tf_op jit(solution)/shard_map/basis/pallas_call | solution.py:493
  78.2 1.2 pieces.1
  79.3 5.1 %all-to-all-done.2.refs_0_.parts_ref = f32[16,64,256]{2,1,0:T(8,128)S(1)} async-done(((f32[16,64,256]{2,1,0:T(8,128)}), f32[16,64,256]{2,1,0:T(8,128)S(1)}, u32[]{:S(2)}, u32[]{:S(2)}) %all-to-all-start.2) | async-done | bytes 1048608 | tf_op jit(solution)/shard_map/all_to_all | solution.py:437
  84.4 2.2 %unfold_pairs.1 = (f32[6,240,256]{2,1,0:T(8,128)S(1)}, f32[16,240,128]{2,1,0:T(8,128)S(1)}, f32[16,240,128]{2,1,0:T(8,128)S(1)}) custom-call(f32[16,64,256]{2,1,0:T(8,128)S(1)} %all-to-all-done.2.refs_0_.parts_ref, f32[16,240,128]{2,1,0:T(8,128)} %get-tuple-element.66.refs_1_, f32[16,240,128]{2,1,0:T(8,128)} %get-tuple-element.67.refs_2_), custom_call_target="tpu_custom_call" | custom-call | tf_op jit(solution)/shard_map/unfold_pairs/pallas_call | solution.py:544
  87.3 11.1 %all_to_all.66.refs_1_.refs_0_ = f32[16,1,2304]{2,1,0:T(1,128)S(1)} all-to-all(f32[16,1,2304]{2,1,0:T(1,128)S(1)} %get-tuple-element.76), channel_id=1, replica_groups=mesh['book'=8,'path_0'=4,'path_1'=4] {'path_0','path_1'}, dimensions={0} | all-to-all | bytes 294912 | tf_op jit(solution)/shard_map/all_to_all | solution.py:437
  98.4 0.6 chain.11
  99.1 11.1 %all_to_all.67.refs_1_ = f32[16,1,2304]{2,1,0:T(1,128)S(1)} all-to-all(f32[16,1,2304]{2,1,0:T(1,128)S(1)} %get-tuple-element.81), channel_id=1, replica_groups=mesh['book'=8,'path_0'=4,'path_1'=4] {'path_0','path_1'}, dimensions={0} | all-to-all | bytes 294912 | tf_op jit(solution)/shard_map/all_to_all | solution.py:437
  110.2 0.6 chain.12
  110.9 11.1 %all_to_all.68.refs_1_.refs_2_ = f32[16,1,2304]{2,1,0:T(1,128)S(1)} all-to-all(f32[16,1,2304]{2,1,0:T(1,128)S(1)} %get-tuple-element.86), channel_id=1, replica_groups=mesh['book'=8,'path_0'=4,'path_1'=4] {'path_0','path_1'}, dimensions={0} | all-to-all | bytes 294912 | tf_op jit(solution)/shard_map/all_to_all | solution.py:437
  122.0 0.6 chain.13
  122.7 11.1 %all_to_all.69.refs_1_.refs_3_ = f32[16,1,2304]{2,1,0:T(1,128)S(1)} all-to-all(f32[16,1,2304]{2,1,0:T(1,128)S(1)} %get-tuple-element.91), channel_id=1, replica_groups=mesh['book'=8,'path_0'=4,'path_1'=4] {'path_0','path_1'}, dimensions={0} | all-to-all | bytes 294912 | tf_op jit(solution)/shard_map/all_to_all | solution.py:437
  133.8 0.6 chain.14
  134.5 11.4 %all_to_all.70.refs_1_.refs_4_ = f32[16,1,2304]{2,1,0:T(1,128)S(1)} all-to-all(f32[16,1,2304]{2,1,0:T(1,128)S(1)} %get-tuple-element.96), channel_id=1, replica_groups=mesh['book'=8,'path_0'=4,'path_1'=4] {'path_0','path_1'}, dimensions={0} | all-to-all | bytes 294912 | tf_op jit(solution)/shard_map/all_to_all | solution.py:437
  145.9 0.6 chain.15
  146.6 11.1 %all_to_all.71.refs_5_.refs_1_ = f32[16,1,2304]{2,1,0:T(1,128)S(1)} all-to-all(f32[16,1,2304]{2,1,0:T(1,128)S(1)} %get-tuple-element.101), channel_id=1, replica_groups=mesh['book'=8,'path_0'=4,'path_1'=4] {'path_0','path_1'}, dimensions={0} | all-to-all | bytes 294912 | tf_op jit(solution)/shard_map/all_to_all | solution.py:437
  157.7 0.6 unfold_pieces.1.refs_0_
  158.3 0.6 chain.16
  159.0 10.7 %all_to_all.72.refs_1_ = f32[16,1,256]{2,1,0:T(1,128)S(1)} all-to-all(f32[16,1,256]{2,1,0:T(1,128)S(1)} %get-tuple-element.105), channel_id=1, replica_groups=mesh['book'=8,'path_0'=4,'path_1'=4] {'path_0','path_1'}, dimensions={0} | all-to-all | bytes 32768 | tf_op jit(solution)/shard_map/all_to_all | solution.py:437
  169.6 0.6 chain.17
  170.3 10.6 %all_to_all.73.refs_1_ = f32[16,1,256]{2,1,0:T(1,128)S(1)} all-to-all(f32[16,1,256]{2,1,0:T(1,128)S(1)} %get-tuple-element.109), channel_id=1, replica_groups=mesh['book'=8,'path_0'=4,'path_1'=4] {'path_0','path_1'}, dimensions={0} | all-to-all | bytes 32768 | tf_op jit(solution)/shard_map/all_to_all | solution.py:437
  181.5 10.6 %all_to_all.74.refs_1_ = f32[16,1,256]{2,1,0:T(1,128)S(1)} all-to-all(f32[16,1,256]{2,1,0:T(1,128)S(1)} %get-tuple-element.113), channel_id=1, replica_groups=mesh['book'=8,'path_0'=4,'path_1'=4] {'path_0','path_1'}, dimensions={0} | all-to-all | bytes 32768 | tf_op jit(solution)/shard_map/all_to_all | solution.py:437
  192.1 0.9 chain.19
  193.1 3.5 %all-to-all-start.12 = ((f32[16,1,128]{2,1,0:T(1,128)}), f32[16,1,128]{2,1,0:T(1,128)S(1)}, u32[]{:S(2)}, u32[]{:S(2)}) async-start(f32[16,1,128]{2,1,0:T(1,128)} %get-tuple-element.117), calls=%async_computation.12 | async-start | bytes 16384 | tf_op jit(solution)/shard_map/all_to_all | solution.py:437
  197.2 6.8 %all-to-all-done.12 = f32[16,1,128]{2,1,0:T(1,128)S(1)} async-done(((f32[16,1,128]{2,1,0:T(1,128)}), f32[16,1,128]{2,1,0:T(1,128)S(1)}, u32[]{:S(2)}, u32[]{:S(2)}) %all-to-all-start.12) | async-done | bytes 8224 | tf_op jit(solution)/shard_map/all_to_all | solution.py:437
  (41 shorter events, 2.6 us)
Async XLA Ops:
  0.6 11.3 %copy-start = (f32[10,20,2048]{2,1,0:T(8,128)S(1)}, f32[10,20,2048]{2,1,0:T(8,128)}, u32[]{:S(2)}) copy-start(f32[10,20,2048]{2,1,0:T(8,128)} %z_ref.5) | copy-start | bytes 4915204
  0.6 18.3 %copy-start.1 = (s32[10,2048]{1,0:T(8,128)S(1)}, s32[10,2048]{1,0:T(8,128)}, u32[]{:S(2)}) copy-start(s32[10,2048]{1,0:T(8,128)} %refs_4_.19) | copy-start | bytes 245764
  0.7 18.3 %copy-start.17 = (f32[2048]{0:T(1024)S(1)}, f32[2048]{0:T(1024)}, u32[]{:S(2)}) copy-start(f32[2048]{0:T(1024)} %param.7) | copy-start | bytes 24580
  3.3 15.7 %all-to-all-start = ((f32[16,8,128]{2,1,0:T(8,128)}), f32[16,8,128]{2,1,0:T(8,128)S(1)}, u32[]{:S(2)}, u32[]{:S(2)}) async-start(f32[16,8,128]{2,1,0:T(8,128)} %stats.1), calls=%async_computation | async-start | bytes 131072 | tf_op jit(solution)/shard_map/all_to_all | solution.py:437
  65.4 19.0 %all-to-all-start.2 = ((f32[16,64,256]{2,1,0:T(8,128)}), f32[16,64,256]{2,1,0:T(8,128)S(1)}, u32[]{:S(2)}, u32[]{:S(2)}) async-start(f32[16,64,256]{2,1,0:T(8,128)} %get-tuple-element.65), calls=%async_computation.2 | async-start | bytes 2097152 | tf_op jit(solution)/shard_map/all_to_all | solution.py:437
  84.4 2.2 %copy-start.10 = (s32[2048]{0:T(1024)S(1)}, s32[2048]{0:T(1024)}, u32[]{:S(2)}) copy-start(s32[2048]{0:T(1024)} %param.9) | copy-start | bytes 24580
  84.4 2.2 %copy-start.16 = (f32[16,1,2304]{2,1,0:T(1,128)S(1)}, f32[16,1,2304]{2,1,0:T(1,128)}, u32[]{:S(2)}) copy-start(f32[16,1,2304]{2,1,0:T(1,128)} %get-tuple-element.75.refs_9_) | copy-start | bytes 442372
  86.6 11.8 %copy-start.7 = (f32[16,240,128]{2,1,0:T(8,128)S(1)}, f32[16,240,128]{2,1,0:T(8,128)}, u32[]{:S(2)}) copy-start(f32[16,240,128]{2,1,0:T(8,128)} %get-tuple-element.78.refs_8_.refs_2_) | copy-start | bytes 5898244
  86.7 11.8 %copy-start.15 = (f32[16,1,2304]{2,1,0:T(1,128)S(1)}, f32[16,1,2304]{2,1,0:T(1,128)}, u32[]{:S(2)}) copy-start(f32[16,1,2304]{2,1,0:T(1,128)} %get-tuple-element.80.refs_10_) | copy-start | bytes 442372
  98.4 11.8 %copy-start.6 = (f32[16,240,128]{2,1,0:T(8,128)S(1)}, f32[16,240,128]{2,1,0:T(8,128)}, u32[]{:S(2)}) copy-start(f32[16,240,128]{2,1,0:T(8,128)} %get-tuple-element.83.refs_8_.refs_2_) | copy-start | bytes 5898244
  98.4 11.8 %copy-start.14 = (f32[16,1,2304]{2,1,0:T(1,128)S(1)}, f32[16,1,2304]{2,1,0:T(1,128)}, u32[]{:S(2)}) copy-start(f32[16,1,2304]{2,1,0:T(1,128)} %get-tuple-element.85.refs_10_) | copy-start | bytes 442372
  110.2 11.8 %copy-start.5 = (f32[16,240,128]{2,1,0:T(8,128)S(1)}, f32[16,240,128]{2,1,0:T(8,128)}, u32[]{:S(2)}) copy-start(f32[16,240,128]{2,1,0:T(8,128)} %get-tuple-element.88.refs_8_.refs_2_) | copy-start | bytes 5898244
  110.2 11.8 %copy-start.13 = (f32[16,1,2304]{2,1,0:T(1,128)S(1)}, f32[16,1,2304]{2,1,0:T(1,128)}, u32[]{:S(2)}) copy-start(f32[16,1,2304]{2,1,0:T(1,128)} %get-tuple-element.90.refs_10_) | copy-start | bytes 442372
  122.0 11.8 %copy-start.4 = (f32[16,240,128]{2,1,0:T(8,128)S(1)}, f32[16,240,128]{2,1,0:T(8,128)}, u32[]{:S(2)}) copy-start(f32[16,240,128]{2,1,0:T(8,128)} %get-tuple-element.93.refs_8_.refs_2_) | copy-start | bytes 5898244
  122.0 11.8 %copy-start.12 = (f32[16,1,2304]{2,1,0:T(1,128)S(1)}, f32[16,1,2304]{2,1,0:T(1,128)}, u32[]{:S(2)}) copy-start(f32[16,1,2304]{2,1,0:T(1,128)} %get-tuple-element.95.refs_10_) | copy-start | bytes 442372
  133.8 12.1 %copy-start.9 = (f32[16,240,128]{2,1,0:T(8,128)S(1)}, f32[16,240,128]{2,1,0:T(8,128)}, u32[]{:S(2)}) copy-start(f32[16,240,128]{2,1,0:T(8,128)} %get-tuple-element.98.refs_8_.refs_2_) | copy-start | bytes 5898244
  133.8 12.1 %copy-start.11 = (f32[16,1,2304]{2,1,0:T(1,128)S(1)}, f32[16,1,2304]{2,1,0:T(1,128)}, u32[]{:S(2)}) copy-start(f32[16,1,2304]{2,1,0:T(1,128)} %get-tuple-element.100.refs_10_) | copy-start | bytes 442372
  146.5 11.8 %copy-start.8 = (f32[16,240,128]{2,1,0:T(8,128)S(1)}, f32[16,240,128]{2,1,0:T(8,128)}, u32[]{:S(2)}) copy-start(f32[16,240,128]{2,1,0:T(8,128)} %get-tuple-element.103.refs_8_.refs_2_) | copy-start | bytes 5898244
  158.3 11.3 %copy-start.3 = (f32[16,240,128]{2,1,0:T(8,128)S(1)}, f32[16,240,128]{2,1,0:T(8,128)}, u32[]{:S(2)}) copy-start(f32[16,240,128]{2,1,0:T(8,128)} %get-tuple-element.107.refs_8_.refs_2_) | copy-start | bytes 5898244
  169.6 11.3 %copy-start.2 = (f32[16,240,128]{2,1,0:T(8,128)S(1)}, f32[16,240,128]{2,1,0:T(8,128)}, u32[]{:S(2)}) copy-start(f32[16,240,128]{2,1,0:T(8,128)} %get-tuple-element.111.refs_8_.refs_2_) | copy-start | bytes 5898244
  193.1 10.9 %all-to-all-start.12 = ((f32[16,1,128]{2,1,0:T(1,128)}), f32[16,1,128]{2,1,0:T(1,128)S(1)}, u32[]{:S(2)}, u32[]{:S(2)}) async-start(f32[16,1,128]{2,1,0:T(1,128)} %get-tuple-element.117), calls=%async_computation.12 | async-start | bytes 16384 | tf_op jit(solution)/shard_map/all_to_all | solution.py:437

commit v7 on v6

--- a/solution.py
+++ b/solution.py
@@ -10,7 +10,6 @@
 BOOK_PATH = ("book", "path_0", "path_1")
 ridge_weight = 0.05
 temper_scale = 0.5
-highest = lax.Precision.HIGHEST
 f32 = jnp.float32
 bf16 = jnp.bfloat16
 NT = (((1,), (1,)), ((), ()))
@@ -84,13 +83,20 @@
         ex_ref[d : d + 1, :] = 100.0 * ((1.0 - disc) - strike_ref[0] * (0.25 * total))
 
 
+def split(x):
+    one = x.astype(bf16)
+    rest = x - one.astype(f32)
+    two = rest.astype(bf16)
+    return one, two, (rest - two.astype(f32)).astype(bf16)
+
+
 def rhs_row(phi_ref, weights):
     acc = jnp.zeros((ROWS, 128), f32)
     for c in range(0, weights.shape[1], 128):
         acc = acc + phi_ref[c // 128] * weights[:, c : c + 128]
-    row = lax.dot_general(
-        jnp.ones((8, 128), f32), acc, NT, precision=highest, preferred_element_type=f32
-    )
+    ones = jnp.ones((16, 128), bf16)
+    one, two, three = (lax.dot_general(ones, x, NT, preferred_element_type=f32) for x in split(acc))
+    row = (one + two + three)[0:8]
     return jnp.concatenate([row, jnp.zeros((8, 256 - ROWS), f32)], axis=1)
 
 
@@ -285,40 +291,45 @@
     row, lane = rows_of((256, 256)), lanes_of((256, 256))
     added = jnp.where(row < basis, ridge_weight * count, 1.0)
     a_ref[...] = a_ref[...] + jnp.where(row == lane, added, 0.0)
-    lane_a = lanes_of((BLOCK, 128))
+    lane_a = lanes_of((8, 128))
     lane_b = lane_a + 128
-    row_a = rows_of((BLOCK, 128))
+    row_a = rows_of((8, 128))
     lane_r = lanes_of((BLOCK, 256))
-
-    def split(x):
-        one = x.astype(bf16)
-        rest = x - one.astype(f32)
-        two = rest.astype(bf16)
-        return one, two, (rest - two.astype(f32)).astype(bf16)
 
     def sweep(i, carry):
         start = pl.multiple_of(i * BLOCK, BLOCK)
         panel = a_ref[pl.ds(start, BLOCK), :]
-        ra, rb = panel[:, 0:128], panel[:, 128:]
+        halves = [[panel[g : g + 8, h : h + 128] for g in range(0, BLOCK, 8)] for h in (0, 128)]
         cols = []
         for c in range(BLOCK):
-            both = jnp.where(lane_a == start + c, ra, 0.0) + jnp.where(lane_b == start + c, rb, 0.0)
-            cols.append(jnp.broadcast_to(jnp.sum(both, axis=1, keepdims=True), (BLOCK, 128)))
+            col = []
+            for g in range(BLOCK // 8):
+                both = jnp.where(lane_a == start + c, halves[0][g], 0.0)
+                both = both + jnp.where(lane_b == start + c, halves[1][g], 0.0)
+                col.append(jnp.broadcast_to(jnp.sum(both, axis=1, keepdims=True), (8, 128)))
+            cols.append(col)
         for k in range(BLOCK):
-            pivot = 1.0 / cols[k][k : k + 1, :]
-            here = row_a == k
+            group, at = divmod(k, 8)
+            here = row_a == at
+            col = cols[k]
+            pivot = 1.0 / col[group][at : at + 1, :]
             unit = jnp.where(here, 1.0, 0.0)
-            ra = jnp.where(lane_a == start + k, unit, ra)
-            rb = jnp.where(lane_b == start + k, unit, rb)
-            row_k = ra[k : k + 1, :] * pivot
-            ra = jnp.where(here, row_k, ra - cols[k] * row_k)
-            row_k = rb[k : k + 1, :] * pivot
-            rb = jnp.where(here, row_k, rb - cols[k] * row_k)
+
+            def reduced(groups):
+                scaled = groups[group][at : at + 1, :] * pivot
+                out = [x - col[g] * scaled for g, x in enumerate(groups)]
+                out[group] = jnp.where(here, scaled, out[group])
+                return out
+
+            for half, lane_h in zip(halves, (lane_a, lane_b)):
+                is_k = lane_h == start + k
+                for g in range(BLOCK // 8):
+                    half[g] = jnp.where(is_k, unit if g == group else 0.0, half[g])
+                half[:] = reduced(half)
             for c in range(k + 1, BLOCK):
-                f = cols[c][k : k + 1, :] * pivot
-                cols[c] = jnp.where(here, f, cols[c] - cols[k] * f)
+                cols[c] = reduced(cols[c])
         inside = (lane_r >= start) & (lane_r < start + BLOCK)
-        w = jnp.concatenate([ra, rb], axis=1)
+        w = jnp.concatenate([jnp.concatenate(half, axis=0) for half in halves], axis=1)
         w = jnp.where(inside, -w, w)
         r1, r2, r3 = split(panel)
         w1, w2, w3 = split(w)
@@ -419,7 +430,8 @@
         for i in range(send_ref.shape[0]):
             send_ref[i, :, 0:256] = row[0:1, :]
     else:
-        total = jnp.broadcast_to(jnp.sum(value, axis=1, keepdims=True), (1, 128))
+        total = jnp.sum(value, axis=1, keepdims=True) / (value.shape[1] * parts_ref.shape[0])
+        total = jnp.broadcast_to(total, (1, 128))
         for i in range(send_ref.shape[0]):
             send_ref[i] = total
     out_ref[...] = value
@@ -600,7 +612,7 @@
         received = exchange(send)
         if carries:
             carried.append(received)
-    book_price = jnp.sum(received[:, 0, 0:1], axis=0) / (paths * size)
+    book_price = jnp.sum(received[:, 0, 0:1], axis=0)
     basis = 1 + factors + factors * (factors + 1) // 2
     coefficients = coefs[0:dates, 0:basis]
     return (value.reshape(paths), book_price, coefficients)

time: 207 us -> 205 us (level)
  no operation moved by 1% of the time
where the time goes in v7:
time: 205 us
  blocking collectives  128 us (62%)
  Pallas kernels  40.7 us (20%)
  waiting for transfers between devices  18 us (9%)
  starting transfers between devices  15.1 us (7%)
    all_to_all x10, blocking collectives, exchange(): return lax.all_to_all(slots, PATH, 0, 0, tiled=True)  128 us
    all_to_all x3, waiting for transfers between devices, exchange(): return lax.all_to_all(slots, PATH, 0, 0, tiled=True)  18 us
    all_to_all x3, starting transfers between devices, exchange(): return lax.all_to_all(slots, PATH, 0, 0, tiled=True)  15.1 us
    pallas_call x1, Pallas kernels, shards(): pl.pallas_call(gram_kernel, grid=(dates,), in_specs=[WHOLE] * 5, out_spec...  10.2 us
    pallas_call x1, Pallas kernels, shards(): pl.pallas_call(basis_kernel, grid=(dates,), in_specs=[spec((size, 8, 128)...  9.08 us
    pallas_call x1, Pallas kernels, shards(): pl.pallas_call(invert, grid=(1,), in_specs=[WHOLE, WHOLE], out_specs=[spe...  8.24 us
    pallas_call x10, Pallas kernels, shards(): pl.pallas_call(kernel, in_specs=[WHOLE] * len(args), out_specs=[WHOLE] *...  5.73 us
  transfers between devices with their start and end apart: 3, of which 3 were waited for; matrix products, arithmetic and copies ran while one was open for 0% of the time, Pallas kernels for 5%

profile of v7, /device:TPU:0, one launch (start us, length us, event | category | flops | bytes accessed | tf_op | source)
XLA Modules:
  0.0 204.7 jit_solution(8911892973733868794)
XLA Ops:
  0.7 2.6 %stats.1 = f32[16,8,128]{2,1,0:T(8,128)} custom-call(f32[10,20,2048]{2,1,0:T(8,128)} %z_ref.5, s32[10,2048]{1,0:T(8,128)} %refs_4_.19), custom_call_target="tpu_custom_call" | custom-call | tf_op jit(solution)/shard_map/stats/pallas_call | solution.py:460
  3.3 8.0 %all-to-all-start = ((f32[16,8,128]{2,1,0:T(8,128)}), f32[16,8,128]{2,1,0:T(8,128)S(1)}, u32[]{:S(2)}, u32[]{:S(2)}) async-start(f32[16,8,128]{2,1,0:T(8,128)} %stats.1), calls=%async_computation | async-start | bytes 131072 | tf_op jit(solution)/shard_map/all_to_all | solution.py:449
  11.9 0.8 swap.1
  12.7 6.2 %all-to-all-done.stats_ref = f32[16,8,128]{2,1,0:T(8,128)S(1)} async-done(((f32[16,8,128]{2,1,0:T(8,128)}), f32[16,8,128]{2,1,0:T(8,128)S(1)}, u32[]{:S(2)}, u32[]{:S(2)}) %all-to-all-start) | async-done | bytes 65568 | tf_op jit(solution)/shard_map/all_to_all | solution.py:449
  19.0 10.2 %gram.1 = (f32[16,112,256]{2,1,0:T(8,128)S(1)}, f32[1,2048]{1,0:T(1,128)S(1)}) custom-call(f32[16,8,128]{2,1,0:T(8,128)S(1)} %all-to-all-done.stats_ref, f32[10,20,2048]{2,1,0:T(8,128)S(1)} %copy-done, s32[10,2048]{1,0:T(8,128)S(1)} %copy-done.1, f32[10,2048]{1,0:T(8,128)S(1)} %get-tuple-element.63.disc_ref.refs_7_, f32[1,2048]{1,0:T(1,128)S(1)} %bitcast.14), custom_call_target="tpu_custom_call" | custom-call | tf_op jit(solution)/shard_map/gram/pallas_call | solution.py:487
  29.2 27.9 %all_to_all.65.refs_1_ = f32[16,112,256]{2,1,0:T(8,128)S(1)} all-to-all(f32[16,112,256]{2,1,0:T(8,128)S(1)} %get-tuple-element.64), channel_id=1, replica_groups=mesh['book'=8,'path_0'=4,'path_1'=4] {'path_0','path_1'}, dimensions={0} | all-to-all | bytes 3670016 | tf_op jit(solution)/shard_map/all_to_all | solution.py:449
  57.1 8.2 %inverse.1 = (f32[16,64,256]{2,1,0:T(8,128)}, f32[48,256]{1,0:T(8,128)S(1)}, f32[1,1,256]{2,1,0:T(1,128)S(1)}) custom-call(s32[1,256]{1,0:T(1,128)S(1)} %broadcast_in_dim.3.refs_0_, f32[16,112,256]{2,1,0:T(8,128)S(1)} %all_to_all.65.refs_1_), custom_call_target="tpu_custom_call" | custom-call | tf_op jit(solution)/shard_map/inverse/pallas_call | solution.py:527
  65.3 3.7 %all-to-all-start.2 = ((f32[16,64,256]{2,1,0:T(8,128)}), f32[16,64,256]{2,1,0:T(8,128)S(1)}, u32[]{:S(2)}, u32[]{:S(2)}) async-start(f32[16,64,256]{2,1,0:T(8,128)} %get-tuple-element.65), calls=%async_computation.2 | async-start | bytes 2097152 | tf_op jit(solution)/shard_map/all_to_all | solution.py:449
  69.0 9.1 %basis.1 = (f32[16,240,128]{2,1,0:T(8,128)}, f32[16,240,128]{2,1,0:T(8,128)}, f32[16,240,128]{2,1,0:T(8,128)}, f32[16,240,128]{2,1,0:T(8,128)}, f32[16,240,128]{...) custom-call(f32[16,8,128]{2,1,0:T(8,128)S(1)} %all-to-all-done.stats, ...), custom_call_target="tpu_custom_call" | custom-call | tf_op jit(solution)/shard_map/basis/pallas_call | solution.py:505
  78.1 1.2 pieces.1
  79.2 5.1 %all-to-all-done.2.refs_0_.parts_ref = f32[16,64,256]{2,1,0:T(8,128)S(1)} async-done(((f32[16,64,256]{2,1,0:T(8,128)}), f32[16,64,256]{2,1,0:T(8,128)S(1)}, u32[]{:S(2)}, u32[]{:S(2)}) %all-to-all-start.2) | async-done | bytes 1048608 | tf_op jit(solution)/shard_map/all_to_all | solution.py:449
  84.3 2.2 %unfold_pairs.1 = (f32[6,240,256]{2,1,0:T(8,128)S(1)}, f32[16,240,128]{2,1,0:T(8,128)S(1)}, f32[16,240,128]{2,1,0:T(8,128)S(1)}) custom-call(f32[16,64,256]{2,1,0:T(8,128)S(1)} %all-to-all-done.2.refs_0_.parts_ref, f32[16,240,128]{2,1,0:T(8,128)} %get-tuple-element.66.refs_1_, f32[16,240,128]{2,1,0:T(8,128)} %get-tuple-element.67.refs_2_), custom_call_target="tpu_custom_call" | custom-call | tf_op jit(solution)/shard_map/unfold_pairs/pallas_call | solution.py:556
  87.1 11.3 %all_to_all.66.refs_1_.refs_0_ = f32[16,1,2304]{2,1,0:T(1,128)S(1)} all-to-all(f32[16,1,2304]{2,1,0:T(1,128)S(1)} %get-tuple-element.76), channel_id=1, replica_groups=mesh['book'=8,'path_0'=4,'path_1'=4] {'path_0','path_1'}, dimensions={0} | all-to-all | bytes 294912 | tf_op jit(solution)/shard_map/all_to_all | solution.py:449
  98.4 0.5 chain.11
  99.0 11.3 %all_to_all.67.refs_1_ = f32[16,1,2304]{2,1,0:T(1,128)S(1)} all-to-all(f32[16,1,2304]{2,1,0:T(1,128)S(1)} %get-tuple-element.81), channel_id=1, replica_groups=mesh['book'=8,'path_0'=4,'path_1'=4] {'path_0','path_1'}, dimensions={0} | all-to-all | bytes 294912 | tf_op jit(solution)/shard_map/all_to_all | solution.py:449
  110.3 0.5 chain.12
  110.8 11.3 %all_to_all.68.refs_1_.refs_2_ = f32[16,1,2304]{2,1,0:T(1,128)S(1)} all-to-all(f32[16,1,2304]{2,1,0:T(1,128)S(1)} %get-tuple-element.86), channel_id=1, replica_groups=mesh['book'=8,'path_0'=4,'path_1'=4] {'path_0','path_1'}, dimensions={0} | all-to-all | bytes 294912 | tf_op jit(solution)/shard_map/all_to_all | solution.py:449
  122.2 0.5 chain.13
  122.7 11.4 %all_to_all.69.refs_1_.refs_3_ = f32[16,1,2304]{2,1,0:T(1,128)S(1)} all-to-all(f32[16,1,2304]{2,1,0:T(1,128)S(1)} %get-tuple-element.91), channel_id=1, replica_groups=mesh['book'=8,'path_0'=4,'path_1'=4] {'path_0','path_1'}, dimensions={0} | all-to-all | bytes 294912 | tf_op jit(solution)/shard_map/all_to_all | solution.py:449
  134.1 0.5 chain.14
  134.6 11.6 %all_to_all.70.refs_1_.refs_4_ = f32[16,1,2304]{2,1,0:T(1,128)S(1)} all-to-all(f32[16,1,2304]{2,1,0:T(1,128)S(1)} %get-tuple-element.96), channel_id=1, replica_groups=mesh['book'=8,'path_0'=4,'path_1'=4] {'path_0','path_1'}, dimensions={0} | all-to-all | bytes 294912 | tf_op jit(solution)/shard_map/all_to_all | solution.py:449
  146.9 11.1 %all_to_all.71.refs_5_.refs_1_ = f32[16,1,2304]{2,1,0:T(1,128)S(1)} all-to-all(f32[16,1,2304]{2,1,0:T(1,128)S(1)} %get-tuple-element.101), channel_id=1, replica_groups=mesh['book'=8,'path_0'=4,'path_1'=4] {'path_0','path_1'}, dimensions={0} | all-to-all | bytes 294912 | tf_op jit(solution)/shard_map/all_to_all | solution.py:449
  158.0 0.6 unfold_pieces.1.refs_0_
  158.7 0.5 chain.16
  159.2 10.7 %all_to_all.72.refs_1_ = f32[16,1,256]{2,1,0:T(1,128)S(1)} all-to-all(f32[16,1,256]{2,1,0:T(1,128)S(1)} %get-tuple-element.105), channel_id=1, replica_groups=mesh['book'=8,'path_0'=4,'path_1'=4] {'path_0','path_1'}, dimensions={0} | all-to-all | bytes 32768 | tf_op jit(solution)/shard_map/all_to_all | solution.py:449
  170.4 10.7 %all_to_all.73.refs_1_ = f32[16,1,256]{2,1,0:T(1,128)S(1)} all-to-all(f32[16,1,256]{2,1,0:T(1,128)S(1)} %get-tuple-element.109), channel_id=1, replica_groups=mesh['book'=8,'path_0'=4,'path_1'=4] {'path_0','path_1'}, dimensions={0} | all-to-all | bytes 32768 | tf_op jit(solution)/shard_map/all_to_all | solution.py:449
  181.6 10.7 %all_to_all.74.refs_1_ = f32[16,1,256]{2,1,0:T(1,128)S(1)} all-to-all(f32[16,1,256]{2,1,0:T(1,128)S(1)} %get-tuple-element.113), channel_id=1, replica_groups=mesh['book'=8,'path_0'=4,'path_1'=4] {'path_0','path_1'}, dimensions={0} | all-to-all | bytes 32768 | tf_op jit(solution)/shard_map/all_to_all | solution.py:449
  192.3 0.9 chain.19
  193.2 3.5 %all-to-all-start.12 = ((f32[16,1,128]{2,1,0:T(1,128)}), f32[16,1,128]{2,1,0:T(1,128)S(1)}, u32[]{:S(2)}, u32[]{:S(2)}) async-start(f32[16,1,128]{2,1,0:T(1,128)} %get-tuple-element.117), calls=%async_computation.12 | async-start | bytes 16384 | tf_op jit(solution)/shard_map/all_to_all | solution.py:449
  196.7 0.6 slice.7
  197.3 6.8 %all-to-all-done.12 = f32[16,1,128]{2,1,0:T(1,128)S(1)} async-done(((f32[16,1,128]{2,1,0:T(1,128)}), f32[16,1,128]{2,1,0:T(1,128)S(1)}, u32[]{:S(2)}, u32[]{:S(2)}) %all-to-all-start.12) | async-done | bytes 8224 | tf_op jit(solution)/shard_map/all_to_all | solution.py:449
  204.1 0.6 slice_reduce_fusion
  (41 shorter events, 2.2 us)
Async XLA Ops:
  0.6 11.3 %copy-start = (f32[10,20,2048]{2,1,0:T(8,128)S(1)}, f32[10,20,2048]{2,1,0:T(8,128)}, u32[]{:S(2)}) copy-start(f32[10,20,2048]{2,1,0:T(8,128)} %z_ref.5) | copy-start | bytes 4915204
  0.6 18.3 %copy-start.1 = (s32[10,2048]{1,0:T(8,128)S(1)}, s32[10,2048]{1,0:T(8,128)}, u32[]{:S(2)}) copy-start(s32[10,2048]{1,0:T(8,128)} %refs_4_.19) | copy-start | bytes 245764
  0.7 18.3 %copy-start.17 = (f32[2048]{0:T(1024)S(1)}, f32[2048]{0:T(1024)}, u32[]{:S(2)}) copy-start(f32[2048]{0:T(1024)} %param.7) | copy-start | bytes 24580
  3.3 15.7 %all-to-all-start = ((f32[16,8,128]{2,1,0:T(8,128)}), f32[16,8,128]{2,1,0:T(8,128)S(1)}, u32[]{:S(2)}, u32[]{:S(2)}) async-start(f32[16,8,128]{2,1,0:T(8,128)} %stats.1), calls=%async_computation | async-start | bytes 131072 | tf_op jit(solution)/shard_map/all_to_all | solution.py:449
  65.3 19.0 %all-to-all-start.2 = ((f32[16,64,256]{2,1,0:T(8,128)}), f32[16,64,256]{2,1,0:T(8,128)S(1)}, u32[]{:S(2)}, u32[]{:S(2)}) async-start(f32[16,64,256]{2,1,0:T(8,128)} %get-tuple-element.65), calls=%async_computation.2 | async-start | bytes 2097152 | tf_op jit(solution)/shard_map/all_to_all | solution.py:449
  84.3 2.2 %copy-start.10 = (s32[2048]{0:T(1024)S(1)}, s32[2048]{0:T(1024)}, u32[]{:S(2)}) copy-start(s32[2048]{0:T(1024)} %param.9) | copy-start | bytes 24580
  84.3 2.2 %copy-start.16 = (f32[16,1,2304]{2,1,0:T(1,128)S(1)}, f32[16,1,2304]{2,1,0:T(1,128)}, u32[]{:S(2)}) copy-start(f32[16,1,2304]{2,1,0:T(1,128)} %get-tuple-element.75.refs_9_) | copy-start | bytes 442372
  86.5 11.9 %copy-start.7 = (f32[16,240,128]{2,1,0:T(8,128)S(1)}, f32[16,240,128]{2,1,0:T(8,128)}, u32[]{:S(2)}) copy-start(f32[16,240,128]{2,1,0:T(8,128)} %get-tuple-element.78.refs_8_.refs_2_) | copy-start | bytes 5898244
  86.6 11.9 %copy-start.15 = (f32[16,1,2304]{2,1,0:T(1,128)S(1)}, f32[16,1,2304]{2,1,0:T(1,128)}, u32[]{:S(2)}) copy-start(f32[16,1,2304]{2,1,0:T(1,128)} %get-tuple-element.80.refs_10_) | copy-start | bytes 442372
  98.4 11.9 %copy-start.6 = (f32[16,240,128]{2,1,0:T(8,128)S(1)}, f32[16,240,128]{2,1,0:T(8,128)}, u32[]{:S(2)}) copy-start(f32[16,240,128]{2,1,0:T(8,128)} %get-tuple-element.83.refs_8_.refs_2_) | copy-start | bytes 5898244
  98.4 11.9 %copy-start.14 = (f32[16,1,2304]{2,1,0:T(1,128)S(1)}, f32[16,1,2304]{2,1,0:T(1,128)}, u32[]{:S(2)}) copy-start(f32[16,1,2304]{2,1,0:T(1,128)} %get-tuple-element.85.refs_10_) | copy-start | bytes 442372
  110.3 11.9 %copy-start.5 = (f32[16,240,128]{2,1,0:T(8,128)S(1)}, f32[16,240,128]{2,1,0:T(8,128)}, u32[]{:S(2)}) copy-start(f32[16,240,128]{2,1,0:T(8,128)} %get-tuple-element.88.refs_8_.refs_2_) | copy-start | bytes 5898244
  110.3 11.9 %copy-start.13 = (f32[16,1,2304]{2,1,0:T(1,128)S(1)}, f32[16,1,2304]{2,1,0:T(1,128)}, u32[]{:S(2)}) copy-start(f32[16,1,2304]{2,1,0:T(1,128)} %get-tuple-element.90.refs_10_) | copy-start | bytes 442372
  122.2 11.9 %copy-start.4 = (f32[16,240,128]{2,1,0:T(8,128)S(1)}, f32[16,240,128]{2,1,0:T(8,128)}, u32[]{:S(2)}) copy-start(f32[16,240,128]{2,1,0:T(8,128)} %get-tuple-element.93.refs_8_.refs_2_) | copy-start | bytes 5898244
  122.2 11.9 %copy-start.12 = (f32[16,1,2304]{2,1,0:T(1,128)S(1)}, f32[16,1,2304]{2,1,0:T(1,128)}, u32[]{:S(2)}) copy-start(f32[16,1,2304]{2,1,0:T(1,128)} %get-tuple-element.95.refs_10_) | copy-start | bytes 442372
  134.1 12.2 %copy-start.9 = (f32[16,240,128]{2,1,0:T(8,128)S(1)}, f32[16,240,128]{2,1,0:T(8,128)}, u32[]{:S(2)}) copy-start(f32[16,240,128]{2,1,0:T(8,128)} %get-tuple-element.98.refs_8_.refs_2_) | copy-start | bytes 5898244
  134.1 12.2 %copy-start.11 = (f32[16,1,2304]{2,1,0:T(1,128)S(1)}, f32[16,1,2304]{2,1,0:T(1,128)}, u32[]{:S(2)}) copy-start(f32[16,1,2304]{2,1,0:T(1,128)} %get-tuple-element.100.refs_10_) | copy-start | bytes 442372
  146.8 11.8 %copy-start.8 = (f32[16,240,128]{2,1,0:T(8,128)S(1)}, f32[16,240,128]{2,1,0:T(8,128)}, u32[]{:S(2)}) copy-start(f32[16,240,128]{2,1,0:T(8,128)} %get-tuple-element.103.refs_8_.refs_2_) | copy-start | bytes 5898244
  158.7 11.2 %copy-start.3 = (f32[16,240,128]{2,1,0:T(8,128)S(1)}, f32[16,240,128]{2,1,0:T(8,128)}, u32[]{:S(2)}) copy-start(f32[16,240,128]{2,1,0:T(8,128)} %get-tuple-element.107.refs_8_.refs_2_) | copy-start | bytes 5898244
  169.9 11.2 %copy-start.2 = (f32[16,240,128]{2,1,0:T(8,128)S(1)}, f32[16,240,128]{2,1,0:T(8,128)}, u32[]{:S(2)}) copy-start(f32[16,240,128]{2,1,0:T(8,128)} %get-tuple-element.111.refs_8_.refs_2_) | copy-start | bytes 5898244
  193.2 10.9 %all-to-all-start.12 = ((f32[16,1,128]{2,1,0:T(1,128)}), f32[16,1,128]{2,1,0:T(1,128)S(1)}, u32[]{:S(2)}, u32[]{:S(2)}) async-start(f32[16,1,128]{2,1,0:T(1,128)} %get-tuple-element.117), calls=%async_computation.12 | async-start | bytes 16384 | tf_op jit(solution)/shard_map/all_to_all | solution.py:449

commit v8 on v7

--- a/solution.py
+++ b/solution.py
@@ -360,14 +360,17 @@
                 out_ref[i, :, 256 * (1 + r) : 256 * (2 + r)] = rest_ref[row : row + 1, :]
 
 
-def unfold_pairs_kernel(first_date, dates, parts_ref, *refs):
-    *far_refs, out_ref, near_a_ref, near_b_ref, sems = refs
+def unfold_pairs_kernel(first_date, dates, far_parts_ref, *refs):
+    *far_refs, out_ref, near_a_ref, near_b_ref, parts_ref, sems = refs
+    own = pltpu.make_async_copy(far_parts_ref, parts_ref, sems.at[2])
+    own.start()
     copies = [
         pltpu.make_async_copy(far, beside, sems.at[i])
         for i, (far, beside) in enumerate(zip(far_refs, (near_a_ref, near_b_ref)))
     ]
     for copy in copies:
         copy.start()
+    own.wait()
     for i in range(out_ref.shape[0]):
         date = first_date + i
         rest = parts_ref[2 * dates - 1 - date]
@@ -555,14 +558,13 @@
 
     first_inverse, *near_phi = pl.pallas_call(
         unfold_pairs,
-        grid=(1,),
-        in_specs=[spec((size, SENT, 256))] + [pl.BlockSpec(memory_space=pltpu.HBM)] * 2,
+        in_specs=[pl.BlockSpec(memory_space=pltpu.HBM)] * 3,
         out_specs=[WHOLE] * 3,
         out_shape=[vmem((dates - paired, ROWS, 256), f32)] + [vmem((tiles, ROWS, 128), f32)] * 2,
-        scratch_shapes=[pltpu.SemaphoreType.DMA((2,))],
+        scratch_shapes=[pltpu.VMEM((size, SENT, 256), f32), pltpu.SemaphoreType.DMA((3,))],
         compiler_params=limit,
         name="unfold_pairs",
-    )(inverse, *(pltpu.with_memory_space_constraint(phi[d], pltpu.HBM) for d in (dates - 1, dates - 2)))
+    )(*(pltpu.with_memory_space_constraint(x, pltpu.HBM) for x in (inverse, phi[dates - 1], phi[dates - 2])))
     phi = [*phi[: dates - 2], *near_phi[::-1]]
     other_inverse = None
     carried = []

time: 205 us -> 207 us (level)
  no operation moved by 1% of the time
where the time goes in v8:
time: 207 us; the launch traced here: 206 us
  blocking collectives  128 us (62%)
  Pallas kernels  41 us (20%)
  waiting for transfers between devices  18.2 us (9%)
  starting transfers between devices  15.1 us (7%)
    all_to_all x10, blocking collectives, exchange(): return lax.all_to_all(slots, PATH, 0, 0, tiled=True)  128 us
    all_to_all x3, waiting for transfers between devices, exchange(): return lax.all_to_all(slots, PATH, 0, 0, tiled=True)  18.2 us
    all_to_all x3, starting transfers between devices, exchange(): return lax.all_to_all(slots, PATH, 0, 0, tiled=True)  15.1 us
    pallas_call x1, Pallas kernels, shards(): pl.pallas_call(gram_kernel, grid=(dates,), in_specs=[WHOLE] * 5, out_spec...  10.3 us
    pallas_call x1, Pallas kernels, shards(): pl.pallas_call(basis_kernel, grid=(dates,), in_specs=[spec((size, 8, 128)...  9.08 us
    pallas_call x1, Pallas kernels, shards(): pl.pallas_call(invert, grid=(1,), in_specs=[WHOLE, WHOLE], out_specs=[spe...  8.21 us
    pallas_call x10, Pallas kernels, shards(): pl.pallas_call(kernel, in_specs=[WHOLE] * len(args), out_specs=[WHOLE] *...  5.73 us
  transfers between devices with their start and end apart: 3, of which 3 were waited for; matrix products, arithmetic and copies ran while one was open for 0% of the time, Pallas kernels for 5%

profile of v8, /device:TPU:0, one launch (start us, length us, event | category | flops | bytes accessed | tf_op | source)
XLA Modules:
  0.0 206.1 jit_solution(7609834980347100931)
XLA Ops:
  0.7 2.6 %stats.1 = f32[16,8,128]{2,1,0:T(8,128)} custom-call(f32[10,20,2048]{2,1,0:T(8,128)} %z_ref.5, s32[10,2048]{1,0:T(8,128)} %refs_4_.19), custom_call_target="tpu_custom_call" | custom-call | tf_op jit(solution)/shard_map/stats/pallas_call | solution.py:463
  3.3 8.0 %all-to-all-start = ((f32[16,8,128]{2,1,0:T(8,128)}), f32[16,8,128]{2,1,0:T(8,128)S(1)}, u32[]{:S(2)}, u32[]{:S(2)}) async-start(f32[16,8,128]{2,1,0:T(8,128)} %stats.1), calls=%async_computation | async-start | bytes 131072 | tf_op jit(solution)/shard_map/all_to_all | solution.py:452
  11.9 0.8 swap.1
  12.7 6.2 %all-to-all-done.stats_ref = f32[16,8,128]{2,1,0:T(8,128)S(1)} async-done(((f32[16,8,128]{2,1,0:T(8,128)}), f32[16,8,128]{2,1,0:T(8,128)S(1)}, u32[]{:S(2)}, u32[]{:S(2)}) %all-to-all-start) | async-done | bytes 65568 | tf_op jit(solution)/shard_map/all_to_all | solution.py:452
  19.0 10.3 %gram.1 = (f32[16,112,256]{2,1,0:T(8,128)S(1)}, f32[1,2048]{1,0:T(1,128)S(1)}) custom-call(f32[16,8,128]{2,1,0:T(8,128)S(1)} %all-to-all-done.stats_ref, f32[10,20,2048]{2,1,0:T(8,128)S(1)} %copy-done, s32[10,2048]{1,0:T(8,128)S(1)} %copy-done.1, f32[10,2048]{1,0:T(8,128)S(1)} %get-tuple-element.63.disc_ref.refs_7_, f32[1,2048]{1,0:T(1,128)S(1)} %bitcast.14), custom_call_target="tpu_custom_call" | custom-call | tf_op jit(solution)/shard_map/gram/pallas_call | solution.py:490
  29.2 27.9 %all_to_all.65.refs_1_ = f32[16,112,256]{2,1,0:T(8,128)S(1)} all-to-all(f32[16,112,256]{2,1,0:T(8,128)S(1)} %get-tuple-element.64), channel_id=1, replica_groups=mesh['book'=8,'path_0'=4,'path_1'=4] {'path_0','path_1'}, dimensions={0} | all-to-all | bytes 3670016 | tf_op jit(solution)/shard_map/all_to_all | solution.py:452
  57.2 8.2 %inverse.1 = (f32[16,64,256]{2,1,0:T(8,128)}, f32[48,256]{1,0:T(8,128)S(1)}, f32[1,1,256]{2,1,0:T(1,128)S(1)}) custom-call(s32[1,256]{1,0:T(1,128)S(1)} %broadcast_in_dim.3.refs_0_, f32[16,112,256]{2,1,0:T(8,128)S(1)} %all_to_all.65.refs_1_), custom_call_target="tpu_custom_call" | custom-call | tf_op jit(solution)/shard_map/inverse/pallas_call | solution.py:530
  65.4 3.7 %all-to-all-start.2 = ((f32[16,64,256]{2,1,0:T(8,128)}), f32[16,64,256]{2,1,0:T(8,128)S(1)}, u32[]{:S(2)}, u32[]{:S(2)}) async-start(f32[16,64,256]{2,1,0:T(8,128)} %get-tuple-element.65), calls=%async_computation.2 | async-start | bytes 2097152 | tf_op jit(solution)/shard_map/all_to_all | solution.py:452
  69.0 9.1 %basis.1 = (f32[16,240,128]{2,1,0:T(8,128)}, f32[16,240,128]{2,1,0:T(8,128)}, f32[16,240,128]{2,1,0:T(8,128)}, f32[16,240,128]{2,1,0:T(8,128)}, f32[16,240,128]{...) custom-call(f32[16,8,128]{2,1,0:T(8,128)S(1)} %all-to-all-done.stats, ...), custom_call_target="tpu_custom_call" | custom-call | tf_op jit(solution)/shard_map/basis/pallas_call | solution.py:508
  78.1 1.2 pieces.1
  79.3 5.1 %all-to-all-done.2.refs_0_.parts_ref = f32[16,64,256]{2,1,0:T(8,128)S(1)} async-done(((f32[16,64,256]{2,1,0:T(8,128)}), f32[16,64,256]{2,1,0:T(8,128)S(1)}, u32[]{:S(2)}, u32[]{:S(2)}) %all-to-all-start.2) | async-done | bytes 1048608 | tf_op jit(solution)/shard_map/all_to_all | solution.py:452
  84.3 1.0 copy-done.2
  85.3 2.5 %unfold_pairs.1 = (f32[6,240,256]{2,1,0:T(8,128)S(1)}, f32[16,240,128]{2,1,0:T(8,128)S(1)}, f32[16,240,128]{2,1,0:T(8,128)S(1)}) custom-call(f32[16,64,256]{2,1,0:T(8,128)} %copy-done.2, f32[16,240,128]{2,1,0:T(8,128)} %get-tuple-element.66.refs_1_, f32[16,240,128]{2,1,0:T(8,128)} %get-tuple-element.67.refs_2_), custom_call_target="tpu_custom_call" | custom-call | tf_op jit(solution)/shard_map/unfold_pairs/pallas_call | solution.py:559
  88.4 11.3 %all_to_all.66.refs_1_.refs_0_ = f32[16,1,2304]{2,1,0:T(1,128)S(1)} all-to-all(f32[16,1,2304]{2,1,0:T(1,128)S(1)} %get-tuple-element.76), channel_id=1, replica_groups=mesh['book'=8,'path_0'=4,'path_1'=4] {'path_0','path_1'}, dimensions={0} | all-to-all | bytes 294912 | tf_op jit(solution)/shard_map/all_to_all | solution.py:452
  99.7 0.5 chain.11
  100.3 11.3 %all_to_all.67.refs_1_ = f32[16,1,2304]{2,1,0:T(1,128)S(1)} all-to-all(f32[16,1,2304]{2,1,0:T(1,128)S(1)} %get-tuple-element.81), channel_id=1, replica_groups=mesh['book'=8,'path_0'=4,'path_1'=4] {'path_0','path_1'}, dimensions={0} | all-to-all | bytes 294912 | tf_op jit(solution)/shard_map/all_to_all | solution.py:452
  112.2 11.3 %all_to_all.68.refs_1_.refs_2_ = f32[16,1,2304]{2,1,0:T(1,128)S(1)} all-to-all(f32[16,1,2304]{2,1,0:T(1,128)S(1)} %get-tuple-element.86), channel_id=1, replica_groups=mesh['book'=8,'path_0'=4,'path_1'=4] {'path_0','path_1'}, dimensions={0} | all-to-all | bytes 294912 | tf_op jit(solution)/shard_map/all_to_all | solution.py:452
  123.5 0.5 chain.13
  124.0 11.4 %all_to_all.69.refs_1_.refs_3_ = f32[16,1,2304]{2,1,0:T(1,128)S(1)} all-to-all(f32[16,1,2304]{2,1,0:T(1,128)S(1)} %get-tuple-element.91), channel_id=1, replica_groups=mesh['book'=8,'path_0'=4,'path_1'=4] {'path_0','path_1'}, dimensions={0} | all-to-all | bytes 294912 | tf_op jit(solution)/shard_map/all_to_all | solution.py:452
  135.4 0.5 chain.14
  135.9 11.6 %all_to_all.70.refs_1_.refs_4_ = f32[16,1,2304]{2,1,0:T(1,128)S(1)} all-to-all(f32[16,1,2304]{2,1,0:T(1,128)S(1)} %get-tuple-element.96), channel_id=1, replica_groups=mesh['book'=8,'path_0'=4,'path_1'=4] {'path_0','path_1'}, dimensions={0} | all-to-all | bytes 294912 | tf_op jit(solution)/shard_map/all_to_all | solution.py:452
  148.2 11.1 %all_to_all.71.refs_5_.refs_1_ = f32[16,1,2304]{2,1,0:T(1,128)S(1)} all-to-all(f32[16,1,2304]{2,1,0:T(1,128)S(1)} %get-tuple-element.101), channel_id=1, replica_groups=mesh['book'=8,'path_0'=4,'path_1'=4] {'path_0','path_1'}, dimensions={0} | all-to-all | bytes 294912 | tf_op jit(solution)/shard_map/all_to_all | solution.py:452
  159.3 0.6 unfold_pieces.1.refs_0_
  160.5 10.7 %all_to_all.72.refs_1_ = f32[16,1,256]{2,1,0:T(1,128)S(1)} all-to-all(f32[16,1,256]{2,1,0:T(1,128)S(1)} %get-tuple-element.105), channel_id=1, replica_groups=mesh['book'=8,'path_0'=4,'path_1'=4] {'path_0','path_1'}, dimensions={0} | all-to-all | bytes 32768 | tf_op jit(solution)/shard_map/all_to_all | solution.py:452
  171.8 10.7 %all_to_all.73.refs_1_ = f32[16,1,256]{2,1,0:T(1,128)S(1)} all-to-all(f32[16,1,256]{2,1,0:T(1,128)S(1)} %get-tuple-element.109), channel_id=1, replica_groups=mesh['book'=8,'path_0'=4,'path_1'=4] {'path_0','path_1'}, dimensions={0} | all-to-all | bytes 32768 | tf_op jit(solution)/shard_map/all_to_all | solution.py:452
  182.4 0.5 chain.18
  183.0 10.7 %all_to_all.74.refs_1_ = f32[16,1,256]{2,1,0:T(1,128)S(1)} all-to-all(f32[16,1,256]{2,1,0:T(1,128)S(1)} %get-tuple-element.113), channel_id=1, replica_groups=mesh['book'=8,'path_0'=4,'path_1'=4] {'path_0','path_1'}, dimensions={0} | all-to-all | bytes 32768 | tf_op jit(solution)/shard_map/all_to_all | solution.py:452
  193.6 0.9 chain.19
  194.5 3.4 %all-to-all-start.12 = ((f32[16,1,128]{2,1,0:T(1,128)}), f32[16,1,128]{2,1,0:T(1,128)S(1)}, u32[]{:S(2)}, u32[]{:S(2)}) async-start(f32[16,1,128]{2,1,0:T(1,128)} %get-tuple-element.117), calls=%async_computation.12 | async-start | bytes 16384 | tf_op jit(solution)/shard_map/all_to_all | solution.py:452
  198.0 0.6 slice.7
  198.6 6.9 %all-to-all-done.12 = f32[16,1,128]{2,1,0:T(1,128)S(1)} async-done(((f32[16,1,128]{2,1,0:T(1,128)}), f32[16,1,128]{2,1,0:T(1,128)S(1)}, u32[]{:S(2)}, u32[]{:S(2)}) %all-to-all-start.12) | async-done | bytes 8224 | tf_op jit(solution)/shard_map/all_to_all | solution.py:452
  205.5 0.6 slice_reduce_fusion
  (45 shorter events, 2.8 us)
Async XLA Ops:
  0.6 11.3 %copy-start = (f32[10,20,2048]{2,1,0:T(8,128)S(1)}, f32[10,20,2048]{2,1,0:T(8,128)}, u32[]{:S(2)}) copy-start(f32[10,20,2048]{2,1,0:T(8,128)} %z_ref.5) | copy-start | bytes 4915204
  0.6 18.3 %copy-start.1 = (s32[10,2048]{1,0:T(8,128)S(1)}, s32[10,2048]{1,0:T(8,128)}, u32[]{:S(2)}) copy-start(s32[10,2048]{1,0:T(8,128)} %refs_4_.19) | copy-start | bytes 245764
  0.7 18.3 %copy-start.19 = (f32[2048]{0:T(1024)S(1)}, f32[2048]{0:T(1024)}, u32[]{:S(2)}) copy-start(f32[2048]{0:T(1024)} %param.7) | copy-start | bytes 24580
  3.3 15.7 %all-to-all-start = ((f32[16,8,128]{2,1,0:T(8,128)}), f32[16,8,128]{2,1,0:T(8,128)S(1)}, u32[]{:S(2)}, u32[]{:S(2)}) async-start(f32[16,8,128]{2,1,0:T(8,128)} %stats.1), calls=%async_computation | async-start | bytes 131072 | tf_op jit(solution)/shard_map/all_to_all | solution.py:452
  65.4 19.0 %all-to-all-start.2 = ((f32[16,64,256]{2,1,0:T(8,128)}), f32[16,64,256]{2,1,0:T(8,128)S(1)}, u32[]{:S(2)}, u32[]{:S(2)}) async-start(f32[16,64,256]{2,1,0:T(8,128)} %get-tuple-element.65), calls=%async_computation.2 | async-start | bytes 2097152 | tf_op jit(solution)/shard_map/all_to_all | solution.py:452
  84.3 1.0 copy-start.2
  85.3 2.5 %copy-start.12 = (s32[2048]{0:T(1024)S(1)}, s32[2048]{0:T(1024)}, u32[]{:S(2)}) copy-start(s32[2048]{0:T(1024)} %param.9) | copy-start | bytes 24580
  85.3 2.5 %copy-start.18 = (f32[16,1,2304]{2,1,0:T(1,128)S(1)}, f32[16,1,2304]{2,1,0:T(1,128)}, u32[]{:S(2)}) copy-start(f32[16,1,2304]{2,1,0:T(1,128)} %get-tuple-element.75.refs_9_) | copy-start | bytes 442372
  87.9 11.9 %copy-start.9 = (f32[16,240,128]{2,1,0:T(8,128)S(1)}, f32[16,240,128]{2,1,0:T(8,128)}, u32[]{:S(2)}) copy-start(f32[16,240,128]{2,1,0:T(8,128)} %get-tuple-element.78.refs_8_.refs_2_) | copy-start | bytes 5898244
  87.9 11.9 %copy-start.17 = (f32[16,1,2304]{2,1,0:T(1,128)S(1)}, f32[16,1,2304]{2,1,0:T(1,128)}, u32[]{:S(2)}) copy-start(f32[16,1,2304]{2,1,0:T(1,128)} %get-tuple-element.80.refs_10_) | copy-start | bytes 442372
  99.7 11.9 %copy-start.8 = (f32[16,240,128]{2,1,0:T(8,128)S(1)}, f32[16,240,128]{2,1,0:T(8,128)}, u32[]{:S(2)}) copy-start(f32[16,240,128]{2,1,0:T(8,128)} %get-tuple-element.83.refs_8_.refs_2_) | copy-start | bytes 5898244
  99.7 11.9 %copy-start.16 = (f32[16,1,2304]{2,1,0:T(1,128)S(1)}, f32[16,1,2304]{2,1,0:T(1,128)}, u32[]{:S(2)}) copy-start(f32[16,1,2304]{2,1,0:T(1,128)} %get-tuple-element.85.refs_10_) | copy-start | bytes 442372
  111.6 11.9 %copy-start.7 = (f32[16,240,128]{2,1,0:T(8,128)S(1)}, f32[16,240,128]{2,1,0:T(8,128)}, u32[]{:S(2)}) copy-start(f32[16,240,128]{2,1,0:T(8,128)} %get-tuple-element.88.refs_8_.refs_2_) | copy-start | bytes 5898244
  111.6 11.9 %copy-start.15 = (f32[16,1,2304]{2,1,0:T(1,128)S(1)}, f32[16,1,2304]{2,1,0:T(1,128)}, u32[]{:S(2)}) copy-start(f32[16,1,2304]{2,1,0:T(1,128)} %get-tuple-element.90.refs_10_) | copy-start | bytes 442372
  123.5 11.9 %copy-start.6 = (f32[16,240,128]{2,1,0:T(8,128)S(1)}, f32[16,240,128]{2,1,0:T(8,128)}, u32[]{:S(2)}) copy-start(f32[16,240,128]{2,1,0:T(8,128)} %get-tuple-element.93.refs_8_.refs_2_) | copy-start | bytes 5898244
  123.5 11.9 %copy-start.14 = (f32[16,1,2304]{2,1,0:T(1,128)S(1)}, f32[16,1,2304]{2,1,0:T(1,128)}, u32[]{:S(2)}) copy-start(f32[16,1,2304]{2,1,0:T(1,128)} %get-tuple-element.95.refs_10_) | copy-start | bytes 442372
  135.4 12.2 %copy-start.11 = (f32[16,240,128]{2,1,0:T(8,128)S(1)}, f32[16,240,128]{2,1,0:T(8,128)}, u32[]{:S(2)}) copy-start(f32[16,240,128]{2,1,0:T(8,128)} %get-tuple-element.98.refs_8_.refs_2_) | copy-start | bytes 5898244
  135.4 12.2 %copy-start.13 = (f32[16,1,2304]{2,1,0:T(1,128)S(1)}, f32[16,1,2304]{2,1,0:T(1,128)}, u32[]{:S(2)}) copy-start(f32[16,1,2304]{2,1,0:T(1,128)} %get-tuple-element.100.refs_10_) | copy-start | bytes 442372
  147.6 11.7 %copy-start.3 = (f32[16,64,256]{2,1,0:T(8,128)S(1)}, f32[16,64,256]{2,1,0:T(8,128)}, u32[]{:S(2)}) copy-start(f32[16,64,256]{2,1,0:T(8,128)} %copy-done.2) | copy-start | bytes 3145732
  148.1 11.8 %copy-start.10 = (f32[16,240,128]{2,1,0:T(8,128)S(1)}, f32[16,240,128]{2,1,0:T(8,128)}, u32[]{:S(2)}) copy-start(f32[16,240,128]{2,1,0:T(8,128)} %get-tuple-element.103.refs_8_.refs_2_) | copy-start | bytes 5898244
  160.0 11.2 %copy-start.5 = (f32[16,240,128]{2,1,0:T(8,128)S(1)}, f32[16,240,128]{2,1,0:T(8,128)}, u32[]{:S(2)}) copy-start(f32[16,240,128]{2,1,0:T(8,128)} %get-tuple-element.107.refs_8_.refs_2_) | copy-start | bytes 5898244
  171.2 11.2 %copy-start.4 = (f32[16,240,128]{2,1,0:T(8,128)S(1)}, f32[16,240,128]{2,1,0:T(8,128)}, u32[]{:S(2)}) copy-start(f32[16,240,128]{2,1,0:T(8,128)} %get-tuple-element.111.refs_8_.refs_2_) | copy-start | bytes 5898244
  194.5 11.0 %all-to-all-start.12 = ((f32[16,1,128]{2,1,0:T(1,128)}), f32[16,1,128]{2,1,0:T(1,128)S(1)}, u32[]{:S(2)}, u32[]{:S(2)}) async-start(f32[16,1,128]{2,1,0:T(1,128)} %get-tuple-element.117), calls=%async_computation.12 | async-start | bytes 16384 | tf_op jit(solution)/shard_map/all_to_all | solution.py:452
